TPU v7x, 128 devices: a 2x2x16 block of a 8x8x16 slice. The times are simulated.
128 devices in a mesh: groups: 4 (over y, x), slab: 32 (over z, core).
Axes of the slice: x: 2, y: 2, z: 16, core: 2. Of those that a mesh axis runs over, the one named last changes fastest.
The devices are a block of a 8x8x16 slice.
Arguments:
- wavefields: float32 [2, 4, 8, 4096, 512], P(None, None, 'groups', 'slab'), parts along dimension 2, may hold values from -6 to 6
- courant: float32 [4096, 512], P('slab'), may hold values from 0.04 to 0.16
- epsilon: float32 [4096, 512], P('slab'), may hold values from 0.1 to 0.3
- anisotropy_delta: float32 [4096, 512], P('slab'), may hold values from 0 to 0.1
- tilt_angle: float32 [4096, 512], P('slab'), may hold values from -3.140625 to 3.140625
- loc_patch: int32 [1024], replicated, may hold values from 0 to 127, as said below
- slab_counts: int32 [32], replicated, may hold values from 3 to 4
- angle_table: int32 [64], replicated, may hold values from -48 to 47
Outputs:
- gathers: float32 [4096, 4096], P(('groups', 'slab')), parts along dimension 0
There are 4 independent parts, one for each index of `groups`. A program takes and returns all parts, laid end to end along the dimension named above; an argument that names none is the same for every part. Nothing has to cross between parts.
Inputs may be any that keep to these rules, and one draw needn't show every extreme that they name: `loc_patch`: location g names a patch id slab * 4 + column block; locations g of one owner are the 32 rows of an aligned block. Within one block no slab is named by more than 2 locations, and some slab is named by exactly 2 in every block.
All inputs are finite; a program needn't handle non-finite values.
Results may differ from a plain program's by a relative error of at most 0.0055.
Values may be sent and summed in bfloat16 or wider, within the bound.
No kernel may reach another device: no remote copies, remote signals or barrier semaphores. Data moves between devices by JAX's collectives and lax.ppermute only.
A program may use at most 128 MiB of HBM per device.

v0:
```python
import math

import jax
import jax.numpy as jnp
from jax import lax
from jax.sharding import Mesh
from jax.sharding import PartitionSpec as P

STEPS = 2
CAP = 2
SLAB = ("slab_0", "slab_1")
GROUPS_SLAB = ("groups", "slab_0", "slab_1")


SECOND_TERMS = (-205.0 / 72.0, 8.0 / 5.0, -1.0 / 5.0, 8.0 / 315.0, -1.0 / 560.0)
FIRST_TERMS = (4.0 / 5.0, -1.0 / 5.0, 4.0 / 105.0, -1.0 / 280.0)


def padded(array, sides, width):
    for axis, dim in sides:
        size, length = (lax.axis_size(axis), array.shape[dim])
        up = [(i, (i + 1) % size) for i in range(size - 1)]
        down = [(j, i) for i, j in up]
        last = lax.slice_in_dim(array, length - width, length, axis=dim)
        leading = lax.slice_in_dim(array, 0, width, axis=dim)
        before = lax.ppermute(last, axis, up)
        after = lax.ppermute(leading, axis, down)
        array = jnp.concatenate([before, array, after], axis=dim)
    return array


def in_blocks(array, dim, size):
    before, after = (array.shape[:dim], array.shape[dim + 1 :])
    return jnp.moveaxis(array.reshape(*before, size, -1, *after), dim, 0)


def laid_out(blocks, dim):
    shape = list(blocks.shape[1:])
    shape[dim] *= blocks.shape[0]
    return jnp.moveaxis(blocks, 0, dim).reshape(shape)


def turned_blocks(blocks, axes, turns):
    shape = [lax.axis_size(a) for a in axes]
    blocks = blocks.reshape(*shape, *blocks.shape[1:])
    for k in turns:
        blocks = lax.all_to_all(blocks, axes[k], split_axis=k, concat_axis=k, tiled=True)
    return blocks.reshape(-1, *blocks.shape[len(axes) :])


def core_and_chips(array, groups, turns, split_dim, concat_dim):
    size = lax.axis_size(groups[0]) * lax.axis_size(groups[1])
    blocks = in_blocks(array, split_dim, size)
    return laid_out(turned_blocks(blocks, groups, turns), concat_dim)


def pad_columns(field):
    widths = [(0, 0)] * (field.ndim - 1) + [(4, 4)]
    return jnp.pad(field, widths)


def derivatives(field):
    row_count = field.shape[-2] - 8
    column_count = field.shape[-1]
    middle = field[..., 4 : 4 + row_count, :]
    beside = pad_columns(middle)
    second_z = SECOND_TERMS[0] * middle
    second_x = SECOND_TERMS[0] * middle
    first_z = jnp.zeros_like(middle)
    for offset in range(1, 5):
        upper_rows = field[..., 4 + offset : 4 + offset + row_count, :]
        lower_rows = field[..., 4 - offset : 4 - offset + row_count, :]
        second_z = second_z + SECOND_TERMS[offset] * (upper_rows + lower_rows)
        first_z = first_z + FIRST_TERMS[offset - 1] * (upper_rows - lower_rows)
        second_x = second_x + SECOND_TERMS[offset] * (
            beside[..., 4 + offset : 4 + offset + column_count]
            + beside[..., 4 - offset : 4 - offset + column_count]
        )
    spread = pad_columns(first_z)
    mixed_term = jnp.zeros_like(middle)
    for offset in range(1, 5):
        mixed_term = mixed_term + FIRST_TERMS[offset - 1] * (
            spread[..., 4 + offset : 4 + offset + column_count]
            - spread[..., 4 - offset : 4 - offset + column_count]
        )
    return (second_x, second_z, mixed_term)


def advance(current, previous, courant, epsilon, anisotropy_delta, tilt_angle):
    second_x, second_z, mixed_term = derivatives(current)
    sine_tilt = jnp.sin(tilt_angle)
    cosine = jnp.cos(tilt_angle)
    along_axis = (
        sine_tilt * sine_tilt * second_x
        + cosine * cosine * second_z
        + 2.0 * sine_tilt * cosine * mixed_term
    )
    across = second_x + second_z - along_axis
    root_delta = jnp.sqrt(1.0 + 2.0 * anisotropy_delta)
    push_pressure = (1.0 + 2.0 * epsilon) * across[:, 0] + root_delta * along_axis[:, 1]
    push_other = root_delta * across[:, 0] + along_axis[:, 1]
    middle = current[..., 4:-4, :]
    return 2.0 * middle - previous + courant * jnp.stack([push_pressure, push_other], axis=1)


def depth_table(patch, bins):
    wavenumber = jnp.arange(bins, dtype=jnp.int32)[:, None]
    depth_index = jnp.arange(patch, dtype=jnp.int32)[None, :]
    phase = 2.0 * math.pi / patch * jnp.mod(wavenumber * depth_index, patch).astype(jnp.float32)
    scale = 1.0 / math.sqrt(patch)
    return jnp.concatenate([jnp.cos(phase), -jnp.sin(phase)], axis=0) * scale


def slant_table(angle_table, patch, bins):
    wavenumber = jnp.arange(bins, dtype=jnp.int32)[:, None, None]
    lateral = jnp.arange(patch, dtype=jnp.int32)[None, None, :]
    slopes = angle_table[None, :, None]
    modulus = 16 * patch
    phase = (
        2.0
        * math.pi
        / modulus
        * jnp.mod(wavenumber * slopes * lateral, modulus).astype(jnp.float32)
    )
    scale = 1.0 / math.sqrt(patch)
    real_part = jnp.cos(phase) * scale
    imag_part = -jnp.sin(phase) * scale
    upper_half = jnp.stack([real_part, -imag_part], axis=2)
    lower_half = jnp.stack([imag_part, real_part], axis=2)
    return jnp.concatenate([upper_half, lower_half], axis=1).astype(jnp.bfloat16)


def correlate(stacked, angles):
    shaped = stacked.reshape(stacked.shape[:-1] + (2, angles))
    product = shaped[..., 0, :, :, :, :] * shaped[..., 1, :, :, :, :]
    summed = jnp.sum(product, axis=(-4, -2))
    return summed.reshape(summed.shape[:-2] + (summed.shape[-2] * angles,))


def per_device(
    wavefields, courant, epsilon, anisotropy_delta, tilt_angle, loc_patch, slab_counts, angle_table
):
    slab_total = lax.axis_size(SLAB)
    slab_index = lax.axis_index(SLAB)
    slab_rows = wavefields.shape[3]
    lateral_cells = wavefields.shape[4]
    shot_count = wavefields.shape[2]
    bins = slab_rows // 2
    angles = angle_table.shape[0]
    per_slab = lateral_cells // slab_rows
    current = wavefields[:, 0:2]
    previous = wavefields[:, 2:4]
    for iteration in range(STEPS):
        extended = padded(current, ((SLAB, 3),), 4)
        current, previous = (
            advance(extended, previous, courant, epsilon, anisotropy_delta, tilt_angle),
            current,
        )
    pressure = current[:, 0]
    table = depth_table(slab_rows, bins)
    spectra = jnp.einsum("qz,fszx->fsqx", table, pressure, precision=lax.Precision.HIGHEST).astype(
        jnp.bfloat16
    )
    spectra = spectra.reshape(2, shot_count, 2, bins, per_slab, slab_rows)
    slant = slant_table(angle_table, slab_rows, bins)
    blocks = loc_patch.reshape(slab_total, -1)
    block_size = blocks.shape[1]
    owner_slab = blocks // per_slab
    column = blocks % per_slab
    order_ids = jnp.arange(block_size, dtype=jnp.int32)
    earlier = (owner_slab[:, :, None] == owner_slab[:, None, :]) & (
        order_ids[None, None, :] < order_ids[None, :, None]
    )
    ranks = jnp.sum(earlier.astype(jnp.int32), axis=2)
    slab_ids = jnp.arange(slab_total, dtype=jnp.int32)
    counts_of = jnp.sum(jnp.where(owner_slab[..., None] == slab_ids, slab_counts, 0), axis=-1)
    alive = column < counts_of
    mine = ((owner_slab == slab_index) & alive).astype(jnp.float32)
    slot_ids = jnp.arange(CAP, dtype=jnp.int32)
    rank_hot = (ranks[..., None] == slot_ids).astype(jnp.float32)
    column_hot = (column[..., None] == jnp.arange(per_slab, dtype=jnp.int32)).astype(jnp.float32)
    chooser = jnp.einsum("dj,djc,djp->dcp", mine, rank_hot, column_hot)
    stacked = jnp.einsum("kirx,fsrkpx->pfski", slant, spectra, preferred_element_type=jnp.float32)
    own_images = correlate(stacked, angles)
    payload = jnp.einsum("dcp,po->dco", chooser, own_images, precision=lax.Precision.HIGHEST)
    images = core_and_chips(payload, ("slab_0", "slab_1"), (1, 0), 0, 0)
    my_slabs = lax.dynamic_index_in_dim(owner_slab, slab_index, 0, keepdims=False)
    my_ranks = lax.dynamic_index_in_dim(ranks, slab_index, 0, keepdims=False)
    picker = (
        (my_slabs[:, None, None] == slab_ids[None, :, None])
        & (my_ranks[:, None, None] == slot_ids[None, None, :])
    ).astype(jnp.float32)
    return jnp.einsum("jnc,nco->jo", picker, images, precision=lax.Precision.HIGHEST)


def solution(mesh):
    finer = Mesh(mesh.devices.reshape(mesh.shape["groups"], 16, 2), ("groups", "slab_0", "slab_1"))
    in_specs = (
        P(None, None, "groups", SLAB, None),
        P(SLAB, None),
        P(SLAB, None),
        P(SLAB, None),
        P(SLAB, None),
        P(),
        P(),
        P(),
    )
    out_specs = P(GROUPS_SLAB, None)
    return jax.shard_map(
        per_device, mesh=finer, in_specs=in_specs, out_specs=out_specs, check_vma=False
    )
```

profile of v0, /device:TPU:70, one launch (start us, length us, event | category | flops | bytes accessed | tf_op | source)
XLA Modules:
  0.0 197.3 jit_solution(17053475228676591177)
XLA Ops:
  0.0 1.6 fusion.63
  1.6 1.3 collective-permute-start
  3.0 3.2 %collective-permute-start.1 = (f32[2,2,2,4,512]{4,3,2,1,0:T(4,128)}, f32[2,2,2,4,512]{4,3,2,1,0:T(4,128)S(1)}, u32[]{:S(2)}, u32[]{:S(2)}) collective-permute-start(f32[2,2,2,4,512]{4,3,2,1,0:T(4,128)} %get-tuple-element.19), channel_id=1, source_target_pairs={{0,1},{1,2},{2,3},{3,4},{4,5},{5,6},{6,7},{7,8},{8,9},{9,10},{10,1... | collective-permute-start | bytes 196616 | tf_op jit(solution)/shard_map/ppermute | solution.py:26
  6.2 4.8 %fusion.62 = (f32[2,2,2,128,512]{4,3,2,1,0:T(8,128)}, f32[2,2,2,128,512]{4,3,2,1,0:T(8,128)}) fusion(f32[2,4,2,128,512]{4,3,2,1,0:T(8,128)} %param.8), kind=kLoop, calls=%fused_computation.144 | loop fusion | bytes 8388608 | tf_op jit(solution)/shard_map/slice | solution.py:152
  13.6 11.0 %negate_convert_fusion = (bf16[64,64,1,128]{3,1,2,0:T(8,128)(2,1)}, bf16[64,64,1,128]{3,1,2,0:T(8,128)(2,1)}, bf16[64,64,1,128]{3,1,2,0:T(8,128)(2,1)}) fusion(s32[64,64]{1,0:T(8,128)S(1)} %iota_multiply_fusion), kind=kLoop, calls=%fused_computation.52 | loop fusion | flops 11010048 | bytes 3162112 | tf_op jit(solution)/shard_map/convert.7
  24.8 1.3 convert_reduce_fusion
  27.0 1.9 copy.104
  29.3 1.3 copy.80
  30.6 1.8 copy.86
  32.4 2.9 %copy.105 = f32[2,2,2,128,512]{3,4,2,0,1:T(8,128)} copy(f32[2,2,2,128,512]{4,3,2,1,0:T(8,128)} %get-tuple-element.17) | data formatting | bytes 4194304
  36.4 2.0 copy.81
  38.4 2.1 %copy.82 = f32[2,2,2,4,512]{3,4,2,0,1:T(8,128)} copy(f32[2,2,2,4,512]{4,3,2,1,0:T(4,128)S(1)} %collective-permute-done.1) | data formatting | bytes 131072 | tf_op jit(solution)/shard_map/ppermute | solution.py:26
  40.4 14.4 %multiply_add_fusion.5 = f32[2,2,2,128,512]{3,4,2,0,1:T(8,128)S(1)} fusion(f32[2,2,2,4,512]{3,4,2,0,1:T(8,128)} %copy.81, f32[2,2,2,128,512]{3,4,2,0,1:T(8,128)S(1)} %copy.104, f32[2,2,2,4,512]{3,4,2,0,1:T(8,128)} %copy.82), kind=kLoop, calls=%fused_computation.62 | loop fusion | flops 9961472 | bytes 4325376 | tf_op jit(solution)/shard_map/add | solution.py:74
  54.8 8.7 %multiply_add_fusion.4 = (f32[2,2,2,128,512]{3,4,2,0,1:T(8,128)S(1)}, f32[2,2,2,128,512]{3,4,2,0,1:T(8,128)S(1)}, f32[2,2,2,128,512]{3,4,2,0,1:T(8,128)S(1)}) fusion(f32[2,2,2,128,512]{3,4,2,0,1:T(8,128)S(1)} %multiply_add_fusion.5, f32[128,512]{0,1:T(8,128)S(1)} %copy.85, f32[128,512]{0,1:T(8,128)S(1)} %copy.84, f32[128,512]{0,1:T(8,128)S(1)} %copy.83, ...), kind=kLoop, calls=%fused_computation.61 | loop fusion | flops 25690112 | bytes 11403264 | tf_op jit(solution)/shard_map/add | solution.py:94
  63.6 1.4 multiply_add_fusion.11
  66.3 2.7 %fusion.64 = (f32[2,2,2,4,512]{3,4,2,0,1:T(8,128)}, f32[2,2,2,4,512]{3,4,2,0,1:T(8,128)}) fusion(f32[2,2,2,128,512]{3,4,2,0,1:T(8,128)S(1)} %fusion.16), kind=kLoop, calls=%fused_computation.146 | loop fusion | bytes 262144 | tf_op jit(solution)/shard_map/slice | solution.py:24
  69.0 2.2 %copy.87 = f32[2,2,2,4,512]{4,3,2,1,0:T(4,128)S(1)} copy(f32[2,2,2,4,512]{3,4,2,0,1:T(8,128)} %get-tuple-element.22) | data formatting | bytes 131072 | tf_op jit(solution)/shard_map/slice | solution.py:25
  71.2 1.5 collective-permute-start.2
  72.7 2.8 %copy.89 = f32[2,2,2,4,512]{4,3,2,1,0:T(4,128)} copy(f32[2,2,2,4,512]{3,4,2,0,1:T(8,128)} %get-tuple-element.21) | data formatting | bytes 131072 | tf_op jit(solution)/shard_map/slice | solution.py:24
  75.5 4.9 %collective-permute-start.3 = (f32[2,2,2,4,512]{4,3,2,1,0:T(4,128)}, f32[2,2,2,4,512]{4,3,2,1,0:T(4,128)}, u32[]{:S(2)}, u32[]{:S(2)}) collective-permute-start(f32[2,2,2,4,512]{4,3,2,1,0:T(4,128)} %copy.89), channel_id=1, source_target_pairs={{0,1},{1,2},{2,3},{3,4},{4,5},{5,6},{6,7},{7,8},{8,9},{9,10},{10,1... | collective-permute-start | bytes 196616 | tf_op jit(solution)/shard_map/ppermute | solution.py:26
  80.6 2.8 %copy.88 = f32[2,2,2,4,512]{3,4,2,0,1:T(8,128)} copy(f32[2,2,2,4,512]{4,3,2,1,0:T(4,128)} %collective-permute-done.2) | data formatting | bytes 131072 | tf_op jit(solution)/shard_map/ppermute | solution.py:27
  83.4 2.8 %copy.90 = f32[2,2,2,4,512]{3,4,2,0,1:T(8,128)} copy(f32[2,2,2,4,512]{4,3,2,1,0:T(4,128)} %collective-permute-done.3) | data formatting | bytes 131072 | tf_op jit(solution)/shard_map/ppermute | solution.py:26
  86.2 14.9 %multiply_add_fusion.1 = f32[2,2,2,128,512]{3,4,2,0,1:T(8,128)S(1)} fusion(f32[2,2,2,4,512]{3,4,2,0,1:T(8,128)} %copy.88, f32[2,2,2,128,512]{3,4,2,0,1:T(8,128)S(1)} %fusion.16, f32[2,2,2,4,512]{3,4,2,0,1:T(8,128)} %copy.90), kind=kLoop, calls=%fused_computation.58 | loop fusion | flops 9961472 | bytes 4325376 | tf_op jit(solution)/shard_map/add | solution.py:74
  101.1 8.7 %multiply_add_fusion = (f32[2,2,2,128,512]{3,4,2,0,1:T(8,128)S(1)}, f32[2,2,2,128,512]{3,4,2,0,1:T(8,128)S(1)}, f32[2,2,2,128,512]{3,4,2,0,1:T(8,128)S(1)}) fusion(f32[2,2,2,128,512]{3,4,2,0,1:T(8,128)S(1)} %multiply_add_fusion.1, f32[128,512]{0,1:T(8,128)S(1)} %copy.85, f32[128,512]{0,1:T(8,128)S(1)} %copy.84, f32[128,512]{0,1:T(8,128)S(1)} %copy.83, ...), kind=kLoop, calls=%fused_computation.57 | loop fusion | flops 25690112 | bytes 11403264 | tf_op jit(solution)/shard_map/add | solution.py:94
  109.9 1.4 multiply_add_fusion.9
  111.5 1.1 fusion.22
  113.9 3.0 %fusion.21 = f32[4,2,2,64,128]{4,0,2,1,3:T(4,128)S(1)} fusion(bf16[2,2,2,64,4,128]{5,4,2,1,0,3:T(4,128)(2,1)S(1)} %copy.92, bf16[64,64,1,128]{3,1,2,0:T(8,128)(2,1)} %get-tuple-element.30, bf16[64,64,1,128]{3,1,2,0:T(8,128)(2,1)} %get-tuple-element.29, bf16[64,64,1,128]{3,1,2,0:T(8,128)(2,1)S(1)} %copy-done.8), kind=kOutput, calls=%fused_computation.68 | convolution fusion | flops 83886080 | bytes 4194304 | tf_op jit(solution)/shard_map/kirx,fsrkpx->pfski/dot_general | solution.py:183
  119.5 5.4 %all_to_all.10 = f32[16,2,1,2,4096]{4,0,3,2,1:T(8,128)S(1)} all-to-all(f32[16,2,1,2,4096]{4,0,3,2,1:T(8,128)S(1)} %convolution_bitcast_fusion), channel_id=1, replica_groups=mesh['groups'=4,'slab_0'=16,'slab_1'=2] {'slab_1'}, dimensions={1} | all-to-all | bytes 2097152 | tf_op jit(solution)/shard_map/all_to_all | solution.py:47
  124.9 1.8 copy.96
  126.8 18.5 %all-to-all-start.1 = ((f32[16,2,1,2,4096]{4,3,1,2,0:T(2,128)}), f32[16,2,1,2,4096]{4,3,1,2,0:T(2,128)S(1)}, u32[]{:S(2)}, u32[]{:S(2)}) async-start(f32[16,2,1,2,4096]{4,3,1,2,0:T(2,128)} %copy.96), calls=%async_computation.1 | async-start | bytes 2097152 | tf_op jit(solution)/shard_map/all_to_all | solution.py:47
  146.0 49.4 %all-to-all-done.1 = f32[16,2,1,2,4096]{4,3,1,2,0:T(2,128)S(1)} async-done(((f32[16,2,1,2,4096]{4,3,1,2,0:T(2,128)}), f32[16,2,1,2,4096]{4,3,1,2,0:T(2,128)S(1)}, u32[]{:S(2)}, u32[]{:S(2)}) %all-to-all-start.1) | async-done | bytes 1048608 | tf_op jit(solution)/shard_map/all_to_all | solution.py:47
  195.4 1.9 convolution_bitcast_fusion.1
  (64 shorter events, 11.2 us)
Async XLA Ops:
  1.6 34.7 %collective-permute-start = (f32[2,2,2,4,512]{4,3,2,1,0:T(4,128)}, f32[2,2,2,4,512]{4,3,2,1,0:T(4,128)S(1)}, u32[]{:S(2)}, u32[]{:S(2)}) collective-permute-start(f32[2,2,2,4,512]{4,3,2,1,0:T(4,128)} %get-tuple-element.20), channel_id=1, source_target_pairs={{1,0},{2,1},{3,2},{4,3},{5,4},{6,5},{7,6},{8,7},{9,8},{10,9},{11,1... | collective-permute-start | bytes 196616 | tf_op jit(solution)/shard_map/ppermute | solution.py:27
  3.0 8.1 %copy-start.9 = (f32[128,512]{1,0:T(8,128)S(1)}, f32[128,512]{1,0:T(8,128)}, u32[]{:S(2)}) copy-start(f32[128,512]{1,0:T(8,128)} %param.12) | copy-start | bytes 786436
  3.0 9.1 %copy-start.10 = (f32[128,512]{1,0:T(8,128)S(1)}, f32[128,512]{1,0:T(8,128)}, u32[]{:S(2)}) copy-start(f32[128,512]{1,0:T(8,128)} %param.10) | copy-start | bytes 786436
  3.0 9.8 %copy-start.11 = (f32[128,512]{1,0:T(8,128)S(1)}, f32[128,512]{1,0:T(8,128)}, u32[]{:S(2)}) copy-start(f32[128,512]{1,0:T(8,128)} %param.11) | copy-start | bytes 786436
  3.0 10.6 %copy-start.15 = (s32[64]{0:T(128)S(1)}, s32[64]{0:T(128)}, u32[]{:S(2)}) copy-start(s32[64]{0:T(128)} %param.15) | copy-start | bytes 772
  3.0 35.4 %collective-permute-start.1 = (f32[2,2,2,4,512]{4,3,2,1,0:T(4,128)}, f32[2,2,2,4,512]{4,3,2,1,0:T(4,128)S(1)}, u32[]{:S(2)}, u32[]{:S(2)}) collective-permute-start(f32[2,2,2,4,512]{4,3,2,1,0:T(4,128)} %get-tuple-element.19), channel_id=1, source_target_pairs={{0,1},{1,2},{2,3},{3,4},{4,5},{5,6},{6,7},{7,8},{8,9},{9,10},{10,1... | collective-permute-start | bytes 196616 | tf_op jit(solution)/shard_map/ppermute | solution.py:26
  12.0 12.6 %copy-start.14 = (s32[1024]{0:T(1024)S(1)}, s32[1024]{0:T(1024)}, u32[]{:S(2)}) copy-start(s32[1024]{0:T(1024)} %param.13) | copy-start | bytes 12292
  13.6 11.2 %copy-start.16 = (s32[32]{0:T(128)S(1)}, s32[32]{0:T(128)}, u32[]{:S(2)}) copy-start(s32[32]{0:T(128)} %param.14) | copy-start | bytes 388
  26.2 2.7 %copy-start.13 = (s32[32,32]{1,0:T(8,128)}, s32[32,32]{1,0:T(8,128)S(1)}, u32[]{:S(2)}) copy-start(s32[32,32]{1,0:T(8,128)S(1)} %get-tuple-element.5) | copy-start | bytes 12292
  28.9 25.9 %copy-start = (f32[2,2,2,128,512]{3,4,2,0,1:T(8,128)}, f32[2,2,2,128,512]{3,4,2,0,1:T(8,128)S(1)}, u32[]{:S(2)}) copy-start(f32[2,2,2,128,512]{3,4,2,0,1:T(8,128)S(1)} %copy.104) | copy-start | bytes 6291460
  40.4 14.4 %copy-start.4 = (f32[2,2,2,4,512]{3,4,2,0,1:T(8,128)S(1)}, f32[2,2,2,4,512]{3,4,2,0,1:T(8,128)}, u32[]{:S(2)}) copy-start(f32[2,2,2,4,512]{3,4,2,0,1:T(8,128)} %copy.81) | copy-start | bytes 196612
  40.4 14.4 %copy-start.6 = (f32[2,2,2,4,512]{3,4,2,0,1:T(8,128)S(1)}, f32[2,2,2,4,512]{3,4,2,0,1:T(8,128)}, u32[]{:S(2)}) copy-start(f32[2,2,2,4,512]{3,4,2,0,1:T(8,128)} %copy.82) | copy-start | bytes 196612
  63.5 1.7 copy-start.1
  63.6 2.3 %copy-start.7 = (f32[2,2,2,128,512]{3,4,2,0,1:T(8,128)S(1)}, f32[2,2,2,128,512]{3,4,2,0,1:T(8,128)}, u32[]{:S(2)}) copy-start(f32[2,2,2,128,512]{3,4,2,0,1:T(8,128)} %copy.105) | copy-start | bytes 6291460
  71.2 9.4 %collective-permute-start.2 = (f32[2,2,2,4,512]{4,3,2,1,0:T(4,128)S(1)}, f32[2,2,2,4,512]{4,3,2,1,0:T(4,128)}, u32[]{:S(2)}, u32[]{:S(2)}) collective-permute-start(f32[2,2,2,4,512]{4,3,2,1,0:T(4,128)S(1)} %copy.87), channel_id=1, source_target_pairs={{1,0},{2,1},{3,2},{4,3},{5,4},{6,5},{7,6},{8,7},{9,8},{10,9},{11,1... | collective-permute-start | bytes 196616 | tf_op jit(solution)/shard_map/ppermute | solution.py:27
  75.5 7.9 %collective-permute-start.3 = (f32[2,2,2,4,512]{4,3,2,1,0:T(4,128)}, f32[2,2,2,4,512]{4,3,2,1,0:T(4,128)}, u32[]{:S(2)}, u32[]{:S(2)}) collective-permute-start(f32[2,2,2,4,512]{4,3,2,1,0:T(4,128)} %copy.89), channel_id=1, source_target_pairs={{0,1},{1,2},{2,3},{3,4},{4,5},{5,6},{6,7},{7,8},{8,9},{9,10},{10,1... | collective-permute-start | bytes 196616 | tf_op jit(solution)/shard_map/ppermute | solution.py:26
  86.2 14.9 %copy-start.3 = (f32[2,2,2,4,512]{3,4,2,0,1:T(8,128)S(1)}, f32[2,2,2,4,512]{3,4,2,0,1:T(8,128)}, u32[]{:S(2)}) copy-start(f32[2,2,2,4,512]{3,4,2,0,1:T(8,128)} %copy.88) | copy-start | bytes 196612
  86.2 14.9 %copy-start.5 = (f32[2,2,2,4,512]{3,4,2,0,1:T(8,128)S(1)}, f32[2,2,2,4,512]{3,4,2,0,1:T(8,128)}, u32[]{:S(2)}) copy-start(f32[2,2,2,4,512]{3,4,2,0,1:T(8,128)} %copy.90) | copy-start | bytes 196612
  109.8 1.7 copy-start.2
  112.6 1.3 copy-start.8
  117.0 1.5 copy-start.12
  126.8 68.7 %all-to-all-start.1 = ((f32[16,2,1,2,4096]{4,3,1,2,0:T(2,128)}), f32[16,2,1,2,4096]{4,3,1,2,0:T(2,128)S(1)}, u32[]{:S(2)}, u32[]{:S(2)}) async-start(f32[16,2,1,2,4096]{4,3,1,2,0:T(2,128)} %copy.96), calls=%async_computation.1 | async-start | bytes 2097152 | tf_op jit(solution)/shard_map/all_to_all | solution.py:47
where the time goes:
time: 198 us; the launch traced here: 197 us
  other arithmetic  64.9 us (33%)
  waiting for transfers between devices  49.4 us (25%)
  local copies, waits for them, and re-layouts  40 us (20%)
  starting transfers between devices  29.4 us (15%)
  matrix products  7.78 us (4%)
  blocking collectives  5.44 us (3%)
    all_to_all x1, waiting for transfers between devices, turned_blocks(): lax.all_to_all(blocks, axes[k], split_axis=k, concat_axis=k, tiled=True)  49.4 us
    add x2, other arithmetic, derivatives(): first_z = first_z + FIRST_TERMS[offset - 1] * (upper_rows - lower_rows)  29.3 us
    all_to_all x1, starting transfers between devices, turned_blocks(): lax.all_to_all(blocks, axes[k], split_axis=k, concat_axis=k, tiled=True)  18.5 us
    add x2, other arithmetic, advance(): sine_tilt * sine_tilt * second_x + cosine * cosine * second_z  17.4 us
    another operation x2, other arithmetic  11 us
    ppermute x2, starting transfers between devices, padded(): before = lax.ppermute(last, axis, up)  8.15 us
    slice x3, local copies, waits for them, and re-layouts, padded(): last = lax.slice_in_dim(array, length - width, length, axis=dim)  7.17 us
    unnamed x37, local copies, waits for them, and re-layouts  7.06 us
  transfers between devices with their start and end apart: 5, of which 1 were waited for; matrix products, arithmetic and copies ran while one was open for 20% of the time, Pallas kernels for 0%

commit v1 on v0

v1 whole, which is shorter than its diff:
```python
import math

import jax
import jax.numpy as jnp
import numpy as np
from jax import lax
from jax.experimental import pallas as pl
from jax.experimental.pallas import tpu as pltpu
from jax.sharding import Mesh
from jax.sharding import PartitionSpec as P

SLAB = ("chip", "core")
GROUPS_SLAB = ("groups", "chip", "core")
LANES = 128
HALF = 4
SECOND = (-14336.0, 8064.0, -1008.0, 128.0, -9.0)
SECOND_REST = 14.0
SECOND_UNIT = 5040.0
FIRST = (672.0, -168.0, 32.0, -3.0)
FIRST_UNIT = 840.0
BF16 = jnp.bfloat16
F32 = jnp.float32


def weight(kind, offset):
    if abs(offset) > HALF:
        return 0.0
    if kind == 2:
        return SECOND[abs(offset)]
    if offset == 0:
        return 0.0
    return FIRST[abs(offset) - 1] * (1.0 if offset > 0 else -1.0)


def band(kind, outputs, inputs):
    table = np.zeros((len(outputs), len(inputs)), np.float32)
    for i, o in enumerate(outputs):
        for j, n in enumerate(inputs):
            if o is not None and n is not None:
                table[i, j] = weight(kind, n - o)
    return table


def row_tables(rows):
    own = list(range(rows))
    inner = list(range(-HALF, 0)) + list(range(rows, rows + HALF))
    outer = list(range(-2 * HALF, -HALF)) + list(range(rows + HALF, rows + 2 * HALF))
    pad = [None] * 8
    first_in = own + inner + outer
    first_out = own + inner + pad
    second_in = own + inner + pad
    one = np.concatenate([band(2, first_out, first_in), band(1, first_out, first_in)])
    two = np.concatenate([band(2, own, second_in), band(1, own, second_in)])
    return one, two


def column_tables(kind):
    block = list(range(2 * LANES))
    inside = band(kind, block, block).T
    across = np.zeros((2 * LANES, 2 * LANES), np.float32)
    for i in range(2 * LANES):
        for o in range(2 * LANES):
            if (i < LANES) != (o < LANES):
                across[i, o] = weight(kind, i - o)
    return inside, across


def depth_table(patch, bins):
    k = np.arange(bins)[:, None]
    z = np.arange(patch)[None, :]
    phase = (2.0 * math.pi / patch * np.mod(k * z, patch)).astype(np.float32)
    table = np.concatenate([np.cos(phase), -np.sin(phase)]).astype(np.float32) * np.float32(1.0 / math.sqrt(patch))
    return table.astype(np.float32)


def quarter_turns(quarter, cosine, sine):
    odd = (quarter & 1) == 1
    c = jnp.where(odd, sine, cosine)
    s = jnp.where(odd, cosine, sine)
    c = jnp.where(((quarter + 1) & 2) == 2, -c, c)
    s = jnp.where((quarter & 2) == 2, -s, s)
    return c, s


def small_cos_sin(y):
    y2 = y * y
    s = y * (1.0 + y2 * (-1.6666654611e-1 + y2 * (8.3321608736e-3 + y2 * -1.9515295891e-4)))
    c = 1.0 - 0.5 * y2 + y2 * y2 * (4.166664568298827e-2 + y2 * (-1.388731625493765e-3 + y2 * 2.443315711809948e-5))
    return c, s


def double_angle(theta):
    n = jnp.floor(theta * (4.0 / math.pi) + 0.5)
    y = 2.0 * theta - n * 1.5703125
    y = y - n * 4.837512969970703e-4
    y = y - n * 7.54978995489188216e-8
    c, s = small_cos_sin(y)
    return quarter_turns(n.astype(jnp.int32), c, s)


def pack_kernel(w_top, w_bot, c_top, c_bot, e_top, e_bot, d_top, d_bot, t_top, t_bot, up_ref, down_ref):
    low = lax.broadcasted_iota(jnp.int32, (8, w_top.shape[-1]), 0) < HALF

    def half_turn(x):
        return pltpu.roll(x, HALF, 0)

    def emit(out, wave, params, upward):
        def join(a, b):
            return jnp.where(low, half_turn(a), b) if upward else jnp.where(low, a, half_turn(b))

        groups = []
        for w in range(wave.shape[0]):
            for s in range(wave.shape[2]):
                groups.append(wave[w, 0, s])
                groups.append(wave[w, 1, s])
                groups.append(join(wave[w, 2, s], wave[w, 3, s]))
        courant, eps, delta, tilt = (p[...] for p in params)
        high = tilt.astype(BF16).astype(F32)
        groups += [join(courant, eps), join(delta, high), tilt - high]
        groups.append(groups[-1])
        for g in range(0, len(groups), 2):
            out[8 * g : 8 * g + 16, :] = jnp.concatenate(groups[g : g + 2], axis=0).astype(BF16)

    emit(up_ref, w_bot, (c_bot, e_bot, d_bot, t_bot), True)
    emit(down_ref, w_top, (c_top, e_top, d_top, t_top), False)


def pack(wavefields, params):
    two, four, shots, rows, cols = wavefields.shape
    last = rows // 8 - 1
    groups = 2 * shots * 3 + 4
    wave_block = (two, four, shots, 8, cols)
    specs = [
        pl.BlockSpec(wave_block, lambda i: (0, 0, 0, 0, 0)),
        pl.BlockSpec(wave_block, lambda i: (0, 0, 0, last, 0)),
    ]
    args = [wavefields, wavefields]
    for p in params:
        specs += [pl.BlockSpec((8, cols), lambda i: (0, 0)), pl.BlockSpec((8, cols), lambda i: (last, 0))]
        args += [p, p]
    out = jax.ShapeDtypeStruct((8 * groups, cols), BF16)
    return pl.pallas_call(
        pack_kernel,
        grid=(1,),
        in_specs=specs,
        out_specs=[pl.BlockSpec((8 * groups, cols), lambda i: (0, 0))] * 2,
        out_shape=[out, out],
        name="pack",
    )(*args)


def main_kernel(
    counts_ref, wave_ref, courant_ref, eps_ref, delta_ref, tilt_ref, up_ref, down_ref,
    one_ref, two_ref, xx_ref, xx_across_ref, x_ref, x_across_ref, depth_ref, angle_ref,
    out_ref,
    mix_ref, twist_ref, a_ref, b_ref, c_ref, field_ref, slope_ref, row_ref, xx_out, xz_out, next_ref,
    split_ref, spectra_ref, low_c, low_s, high_c, high_s, image_ref,
):
    step = pl.program_id(0)
    rows, cols = courant_ref.shape
    ext = rows + 2 * HALF
    tall = rows + 4 * HALF
    low = lax.broadcasted_iota(jnp.int32, (8, cols), 0) < HALF

    def half_turn(x):
        return pltpu.roll(x, HALF, 0)

    def group(g):
        return (up_ref[8 * g : 8 * g + 8, :].astype(F32), down_ref[8 * g : 8 * g + 8, :].astype(F32))

    def first_halves(g):
        u, d = group(g)
        return jnp.where(low, u, half_turn(d))

    def second_halves(g):
        u, d = group(g)
        return jnp.where(low, half_turn(u), d)

    params = wave_groups = 3 * 4

    @pl.when(step == 0)
    def _():
        def coefficients(at, courant, eps, delta, tilt):
            cosine, sine = double_angle(tilt)
            scaled = courant * (1.0 / SECOND_UNIT)
            mix_ref[at, :] = 0.5 + 0.5 * cosine
            twist_ref[at, :] = sine * (SECOND_UNIT / (FIRST_UNIT * FIRST_UNIT))
            a_ref[at, :] = scaled * (1.0 + 2.0 * eps)
            b_ref[at, :] = scaled * jnp.sqrt(1.0 + 2.0 * delta)
            c_ref[at, :] = scaled

        for r in range(0, rows, 8):
            at = slice(r, r + 8)
            coefficients(at, courant_ref[at, :], eps_ref[at, :], delta_ref[at, :], tilt_ref[at, :])
        high = second_halves(params + 1)
        tilt = high + first_halves(params + 2)
        coefficients(
            slice(rows, ext), first_halves(params), second_halves(params), first_halves(params + 1), tilt
        )

    base = 3 * step

    def dyn_group(ref, g):
        return ref[pl.ds(pl.multiple_of(8 * (base + g), 8), 8), :].astype(F32)

    halo = []
    for f in range(2):
        u, d = (dyn_group(up_ref, f), dyn_group(down_ref, f))
        inner = jnp.where(low, half_turn(u), half_turn(d))
        outer = jnp.where(low, u, d)
        halo.append(inner)
        field_ref[f * tall : f * tall + rows, :] = wave_ref[0, f, 0].astype(BF16)
        field_ref[f * tall + rows : (f + 1) * tall, :] = jnp.concatenate([inner, outer], axis=0).astype(BF16)
    u, d = (dyn_group(up_ref, 2), dyn_group(down_ref, 2))
    halo.append(jnp.where(low, u, half_turn(d)))
    halo.append(jnp.where(low, half_turn(u), d))

    def along_columns(out, source, inside, across):
        left = jnp.dot(source[:, : 2 * LANES], inside[...], preferred_element_type=F32)
        right = jnp.dot(source[:, 2 * LANES :], inside[...], preferred_element_type=F32)
        mid = jnp.dot(source[:, LANES : 3 * LANES], across[...], preferred_element_type=F32)
        n = source.shape[0]
        out[:n, :LANES] = left[:, :LANES]
        out[:n, LANES : 2 * LANES] = left[:, LANES:] + mid[:, :LANES]
        out[:n, 2 * LANES : 3 * LANES] = right[:, :LANES] + mid[:, LANES:]
        out[:n, 3 * LANES :] = right[:, LANES:]

    def derive(table, count):
        for f in range(2):
            source = field_ref[f * tall : (f + 1) * tall, :]
            product = jnp.dot(table[...], source, preferred_element_type=F32)
            row_ref[f * tall : f * tall + count, :] = product[:count]
            slope_ref[f * count : (f + 1) * count, :] = product[count:].astype(BF16)
        along_columns(xx_out, field_ref[...], xx_ref, xx_across_ref)
        along_columns(xz_out, slope_ref[: 2 * count, :], x_ref, x_across_ref)

    def pieces(f, r, count, value):
        at = slice(f * tall + r, f * tall + r + 8)
        zz = row_ref[at, :]
        xx = xx_out[at, :]
        xz = xz_out[f * count + r : f * count + r + 8, :]
        turn = mix_ref[r : r + 8, :] * (xx - zz) - twist_ref[r : r + 8, :] * xz
        rest = SECOND_REST * value
        return (zz + turn) - rest if f == 0 else (xx - turn) - rest

    derive(one_ref, tall)
    for r in range(0, ext, 8):
        at = slice(r, r + 8)
        if r < rows:
            p, q, p0, q0 = (wave_ref[0, f, 0, at, :] for f in range(4))
        else:
            p, q, p0, q0 = halo
        across = pieces(0, r, tall, p)
        along = pieces(1, r, tall, q)
        a, b, c = (a_ref[at, :], b_ref[at, :], c_ref[at, :])
        next_ref[0, at, :] = (2.0 * p - p0) + (a * across + b * along)
        next_ref[1, at, :] = (2.0 * q - q0) + (b * across + c * along)

    for f in range(2):
        field_ref[f * tall : f * tall + rows, :] = next_ref[f, :rows, :].astype(BF16)
        edge = next_ref[f, rows:ext, :]
        field_ref[f * tall + rows : (f + 1) * tall, :] = jnp.concatenate([edge, jnp.zeros_like(edge)], axis=0).astype(BF16)
    derive(two_ref, rows)
    for r in range(0, rows, 16):
        parts = []
        for h in (r, r + 8):
            at = slice(h, h + 8)
            p, q = (next_ref[0, at, :], next_ref[1, at, :])
            across = pieces(0, h, rows, p)
            along = pieces(1, h, rows, q)
            parts.append((2.0 * p - wave_ref[0, 0, 0, at, :]) + (a_ref[at, :] * across + b_ref[at, :] * along))
        value = jnp.concatenate(parts, axis=0)
        top = value.astype(BF16)
        split_ref[r : r + 16, :] = top
        split_ref[rows + r : rows + r + 16, :] = (value - top.astype(F32)).astype(BF16)
        split_ref[2 * rows + r : 2 * rows + r + 16, :] = top
    spectra = jnp.dot(depth_ref[...], split_ref[...], preferred_element_type=F32)
    bins = rows // 2
    per_slab = cols // LANES
    for part in range(2):
        for m in range(per_slab):
            start = 16 * part + per_slab * step + m
            spectra_ref[pl.ds(start, bins, stride=32), :] = spectra[
                part * bins : (part + 1) * bins, m * LANES : (m + 1) * LANES
            ]

    @pl.when(step == pl.num_programs(0) - 1)
    def _():
        right_half = lax.broadcasted_iota(jnp.int32, (LANES, LANES), 1) >= LANES // 2
        angles = jnp.concatenate([angle_ref[...], angle_ref[...]], axis=1)
        lateral = lax.broadcasted_iota(jnp.int32, (LANES, LANES), 0)
        modulus = 16 * LANES
        turn = (lateral * angles) & (modulus - 1)
        quarter = (turn + modulus // 8) >> int(math.log2(modulus // 4))
        rest = turn - quarter * (modulus // 4)
        c1, s1 = small_cos_sin(rest.astype(F32) * (2.0 * math.pi / modulus))
        c1, s1 = quarter_turns(quarter, c1, s1)

        def times(x, y):
            return (x[0] * y[0] - x[1] * y[1], x[0] * y[1] + x[1] * y[0])

        unit = (jnp.ones_like(c1), jnp.zeros_like(c1))
        value = unit
        for j in range(8):
            low_c[j], low_s[j] = value
            value = (c1, s1) if j == 0 else times(value, (c1, s1))
        eighth = value
        scale = 1.0 / math.sqrt(LANES)
        value = (jnp.where(right_half, 0.0, scale), jnp.where(right_half, scale, 0.0))
        for j in range(8):
            high_c[j], high_s[j] = value
            value = times(value, eighth)

        left_lane = lax.broadcasted_iota(jnp.int32, (8, LANES), 1) < LANES // 2
        alive = lax.broadcasted_iota(jnp.int32, (8, LANES), 0) < counts_ref[lax.axis_index(SLAB)]

        def some(j, carry):
            hc, hs = (high_c[j], high_s[j])
            pair = []
            for i in range(8):
                lc, ls = (low_c[i], low_s[i])
                real = (hc * lc - hs * ls).astype(BF16)
                imag = (hc * ls + hs * lc).astype(BF16)
                at = pl.multiple_of((8 * j + i) * 32, 32)
                left = jnp.concatenate(
                    [spectra_ref[pl.ds(at, 16), :], spectra_ref[pl.ds(at + 16, 16), :]], axis=1
                ).astype(BF16)
                stack = jnp.dot(left, jnp.concatenate([real, imag], axis=0), preferred_element_type=F32)
                product = stack[:8] * stack[8:]
                pair.append(product + half_turn_small(product))
                if i % 2 == 1:
                    even, odd = pair
                    even = even + pltpu.roll(even, LANES // 2, 1)
                    odd = odd + pltpu.roll(odd, LANES // 2, 1)
                    pair = []
                    where_to = pl.multiple_of((4 * j + i // 2) * LANES, LANES)
                    image_ref[:, pl.ds(where_to, LANES)] = jnp.where(
                        alive, jnp.where(left_lane, even, odd), 0.0
                    )
            return carry

        def half_turn_small(x):
            return pltpu.roll(x, 4, 0)

        lax.fori_loop(0, bins // 8, some, 0)
        out_ref[...] = image_ref[:per_slab, :].astype(BF16)


def images_of(wavefields, params, up, down, slab_counts, angle_table):
    two, four, shots, rows, cols = wavefields.shape
    bins = rows // 2
    per_slab = cols // rows
    angles = angle_table.shape[0]
    ext = rows + 2 * HALF
    tall = rows + 4 * HALF
    one, both = row_tables(rows)
    xx, xx_across = column_tables(2)
    x, x_across = column_tables(1)
    depth = depth_table(rows, bins)
    depth_top = depth.astype(jnp.bfloat16)
    depth_low = (depth - depth_top.astype(np.float32)).astype(jnp.bfloat16)
    depth = np.concatenate([depth_top, depth_top, depth_low], axis=1)
    tables = [jnp.asarray(t, dtype=BF16) for t in (one, both, xx, xx_across, x, x_across, depth)]

    def whole(a):
        return pl.BlockSpec(a.shape, lambda i: (0,) * a.ndim)

    angle_row = angle_table.reshape(1, angles)
    args = [slab_counts, wavefields, *params, up, down, *tables, angle_row]
    specs = [
        pl.BlockSpec(memory_space=pltpu.SMEM),
        pl.BlockSpec((1, four, 1, rows, cols), lambda i: (i // shots, 0, i % shots, 0, 0)),
    ] + [whole(a) for a in args[2:]]
    out_shape = (per_slab, bins * angles)
    scratch = [pltpu.VMEM((ext, cols), F32)] * 5 + [
        pltpu.VMEM((2 * tall, cols), BF16),
        pltpu.VMEM((2 * tall, cols), BF16),
        pltpu.VMEM((2 * tall, cols), F32),
        pltpu.VMEM((2 * tall, cols), F32),
        pltpu.VMEM((2 * tall, cols), F32),
        pltpu.VMEM((2, ext, cols), F32),
        pltpu.VMEM((3 * rows, cols), BF16),
        pltpu.VMEM((32 * bins, LANES), F32),
    ] + [pltpu.VMEM((8, LANES, LANES), F32)] * 4 + [pltpu.VMEM((8, bins * angles), F32)]
    return pl.pallas_call(
        main_kernel,
        grid=(2 * shots,),
        in_specs=specs,
        out_specs=pl.BlockSpec(out_shape, lambda i: (0, 0)),
        out_shape=jax.ShapeDtypeStruct(out_shape, BF16),
        scratch_shapes=scratch,
        name="images",
    )(*args)


def pick_kernel(loc_ref, own_ref, other_ref, out_ref):
    slab = lax.axis_index(SLAB)
    core = lax.axis_index("core")
    count = out_ref.shape[0]
    per_row = LANES // count
    loc = loc_ref[pl.ds(slab // per_row, 1), :]
    loc = pltpu.roll(loc, (LANES - (slab % per_row) * count) % LANES, 1)[:, :count]
    held = own_ref.shape[0]
    per_slab = 4
    owner = loc // per_slab
    index = (owner // 2) * per_slab + loc % per_slab
    mine = owner % 2 == core
    row = lax.broadcasted_iota(jnp.int32, (held, count), 0)
    hit = row == index
    own_hot = jnp.where(hit & mine, 1.0, 0.0).astype(BF16)
    other_hot = jnp.where(hit & jnp.logical_not(mine), 1.0, 0.0).astype(BF16)

    def choose(hot, ref):
        return lax.dot_general(hot, ref[...], (((0,), (0,)), ((), ())), preferred_element_type=F32)

    out_ref[...] = choose(own_hot, own_ref) + choose(other_hot, other_ref)


def pick(loc_patch, own, other, count):
    width = own.shape[1]
    return pl.pallas_call(
        pick_kernel,
        out_shape=jax.ShapeDtypeStruct((count, width), F32),
        name="pick",
    )(loc_patch.reshape(-1, LANES), own, other)


def per_device(
    wavefields, courant, epsilon, anisotropy_delta, tilt_angle, loc_patch, slab_counts, angle_table
):
    slabs = lax.axis_size(SLAB)
    params = (courant, epsilon, anisotropy_delta, tilt_angle)
    up_send, down_send = pack(wavefields, params)
    up = lax.ppermute(up_send, SLAB, [(i, i + 1) for i in range(slabs - 1)])
    down = lax.ppermute(down_send, SLAB, [(i + 1, i) for i in range(slabs - 1)])
    images = images_of(wavefields, params, up, down, slab_counts, angle_table)
    own = lax.all_gather(images, "chip", tiled=True)
    other = lax.ppermute(own, "core", [(0, 1), (1, 0)])
    return pick(loc_patch, own, other, loc_patch.shape[0] // slabs)


def solution(mesh):
    slabs = mesh.shape["slab"]
    finer = Mesh(mesh.devices.reshape(mesh.shape["groups"], slabs // 2, 2), GROUPS_SLAB)
    in_specs = (
        P(None, None, "groups", SLAB, None),
        P(SLAB, None),
        P(SLAB, None),
        P(SLAB, None),
        P(SLAB, None),
        P(),
        P(),
        P(),
    )
    out_specs = P(GROUPS_SLAB, None)
    return jax.shard_map(
        per_device, mesh=finer, in_specs=in_specs, out_specs=out_specs, check_vma=False
    )
```

time: 198 us -> 72 us (0.36)
  the two profiles are of different devices: /device:TPU:70 before, /device:TPU:69 now
where the time goes in v1:
time: 72 us; the launch traced here: 71.9 us
  blocking collectives  30.8 us (43%)
  starting transfers between devices  19.5 us (27%)
  Pallas kernels  17.3 us (24%)
  waiting for transfers between devices  2.69 us (4%)
  local copies, waits for them, and re-layouts  1.57 us (2%)
    all_gather x1, blocking collectives, per_device(): own = lax.all_gather(images, 'chip', tiled=True)  30.8 us
    pallas_call x1, Pallas kernels, images_of(): pl.pallas_call(main_kernel, grid=(2 * shots,), in_specs=specs, out_specs=...  13 us
    ppermute x1, starting transfers between devices, per_device(): down = lax.ppermute(down_send, SLAB, [(i + 1, i) for i in range(slabs - 1)])  8.06 us
    ppermute x1, starting transfers between devices, per_device(): other = lax.ppermute(own, 'core', [(0, 1), (1, 0)])  6.32 us
    ppermute x1, starting transfers between devices, per_device(): up = lax.ppermute(up_send, SLAB, [(i, i + 1) for i in range(slabs - 1)])  5.08 us
    pallas_call x1, Pallas kernels, pick(): pl.pallas_call(pick_kernel, out_shape=jax.ShapeDtypeStruct((count, width)...  2.44 us
    pallas_call x1, Pallas kernels, pack(): pl.pallas_call(pack_kernel, grid=(1,), in_specs=specs, out_specs=[pl.Bloc...  1.81 us
    unnamed x9, local copies, waits for them, and re-layouts  1.57 us
  transfers between devices with their start and end apart: 3, of which 2 were waited for; matrix products, arithmetic and copies ran while one was open for 0% of the time, Pallas kernels for 0%

profile of v1, /device:TPU:69, one launch (start us, length us, event | category | flops | bytes accessed | tf_op | source)
XLA Modules:
  0.0 71.9 jit_solution(17705364096049610173)
XLA Ops:
  0.0 1.8 %pack.1 = (bf16[128,512]{1,0:T(8,128)(2,1)}, bf16[128,512]{1,0:T(8,128)(2,1)}) custom-call(f32[2,4,2,128,512]{4,3,2,1,0:T(8,128)} %wave_ref.1, f32[2,4,2,128,512]{4,3,2,1,0:T(8,128)} %wave_ref.1, f32[128,512]{1,0:T(8,128)} %courant_ref.1, f32[128,512]{1,0:T(8,128)} %courant_ref.1, f32[128,512]{1,0:T(8,128)} %eps_ref.1, f32[128,512]{1,0:T(8,128)} %eps_ref.1, ...), custom_call_target="tpu_custom_call" | custom-call | tf_op jit(solution)/shard_map/pack/pallas_call | solution.py:142
  1.8 5.1 %collective-permute-start = (bf16[128,512]{1,0:T(8,128)(2,1)}, bf16[128,512]{1,0:T(8,128)(2,1)S(1)}, u32[]{:S(2)}, u32[]{:S(2)}) collective-permute-start(bf16[128,512]{1,0:T(8,128)(2,1)} %get-tuple-element.7), channel_id=1, source_target_pairs={{0,1},{1,2},{2,3},{3,4},{4,5},{5,6},{6,7},{7,8},{8,9},{9,10},{10,1... | collective-permute-start | bytes 393224 | tf_op jit(solution)/shard_map/ppermute | solution.py:434
  6.9 8.1 %collective-permute-start.1 = (bf16[128,512]{1,0:T(8,128)(2,1)}, bf16[128,512]{1,0:T(8,128)(2,1)S(1)}, u32[]{:S(2)}, u32[]{:S(2)}) collective-permute-start(bf16[128,512]{1,0:T(8,128)(2,1)} %get-tuple-element.8), channel_id=1, source_target_pairs={{1,0},{2,1},{3,2},{4,3},{5,4},{6,5},{7,6},{8,7},{9,8},{10,9},{11,1... | collective-permute-start | bytes 393224 | tf_op jit(solution)/shard_map/ppermute | solution.py:435
  15.0 0.0 collective-permute-done.up_ref
  15.0 0.0 copy-start.2
  15.0 1.2 %collective-permute-done.1.down_ref = bf16[128,512]{1,0:T(8,128)(2,1)S(1)} collective-permute-done((bf16[128,512]{1,0:T(8,128)(2,1)}, bf16[128,512]{1,0:T(8,128)(2,1)S(1)}, u32[]{:S(2)}, u32[]{:S(2)}) %collective-permute-start.1) | collective-permute-done | bytes 131104 | tf_op jit(solution)/shard_map/ppermute | solution.py:435
  16.1 0.0 copy-start.3
  16.1 0.0 copy-done.2
  16.1 0.6 copy-done.3
  16.8 13.0 %images.1 = bf16[4,4096]{1,0:T(4,128)(2,1)} custom-call(s32[32]{0:T(128)} %counts_ref.1, f32[2,4,2,128,512]{4,3,2,1,0:T(8,128)} %wave_ref.1, f32[128,512]{1,0:T(8,128)} %courant_ref.1, f32[128,512]{1,0:T(8,128)} %eps_ref.1, f32[128,512]{1,0:T(8,128)} %delta_ref.1, f32[128,512]{1,0:T(8,128)} %tilt_ref.1, bf16[128,512]{1,0:T(8,128)(2,1)} %copy-done.2, ...), custom_call_target="tpu_custom_call" | custom-call | tf_op jit(solution)/shard_map/images/pallas_call | solution.py:385
  29.8 30.8 %all-gather = bf16[16,4,4096]{2,1,0:T(4,128)(2,1)S(1)} all-gather(bf16[1,4,4096]{2,1,0:T(4,128)(2,1)} %bitcast.3), channel_id=1, replica_groups=mesh['groups'=4,'chip'=16,'core'=2] {'chip'}, dimensions={0}, use_global_device_ids=true | all-gather | bytes 557056 | tf_op jit(solution)/shard_map/all_gather | solution.py:437
  60.6 0.1 reshape.9.own_ref
  60.8 0.0 copy-start
  60.8 6.3 %collective-permute-start.2 = (bf16[64,4096]{1,0:T(8,128)(2,1)S(1)}, bf16[64,4096]{1,0:T(8,128)(2,1)S(1)}, u32[]{:S(2)}, u32[]{:S(2)}) collective-permute-start(bf16[64,4096]{1,0:T(8,128)(2,1)S(1)} %reshape.9.own_ref), channel_id=1, source_target_pairs={{0,1},{1,0},{2,3},{3,2},{4,5},{5,4},{6,7},{7,6},{8,9},{9,8},{10,11... | collective-permute-start | bytes 1572872 | tf_op jit(solution)/shard_map/ppermute | solution.py:438
  67.1 1.5 %collective-permute-done.2.other_ref = bf16[64,4096]{1,0:T(8,128)(2,1)S(1)} collective-permute-done((bf16[64,4096]{1,0:T(8,128)(2,1)S(1)}, bf16[64,4096]{1,0:T(8,128)(2,1)S(1)}, u32[]{:S(2)}, u32[]{:S(2)}) %collective-permute-start.2) | collective-permute-done | bytes 524320 | tf_op jit(solution)/shard_map/ppermute | solution.py:438
  68.6 0.0 copy-start.1
  68.6 0.0 copy-done
  68.6 0.8 %copy-done.1 = bf16[64,4096]{1,0:T(8,128)(2,1)} copy-done((bf16[64,4096]{1,0:T(8,128)(2,1)}, bf16[64,4096]{1,0:T(8,128)(2,1)S(1)}, u32[]{:S(2)}) %copy-start.1) | copy-done | bytes 524312
  69.4 2.4 %pick.1 = f32[32,4096]{1,0:T(8,128)} custom-call(s32[8,128]{1,0:T(8,128)} %bitcast.4, bf16[64,4096]{1,0:T(8,128)(2,1)} %copy-done, bf16[64,4096]{1,0:T(8,128)(2,1)} %copy-done.1), custom_call_target="tpu_custom_call" | custom-call | tf_op jit(solution)/shard_map/pick/pallas_call | solution.py:421
Async XLA Ops:
  1.8 13.2 %collective-permute-start = (bf16[128,512]{1,0:T(8,128)(2,1)}, bf16[128,512]{1,0:T(8,128)(2,1)S(1)}, u32[]{:S(2)}, u32[]{:S(2)}) collective-permute-start(bf16[128,512]{1,0:T(8,128)(2,1)} %get-tuple-element.7), channel_id=1, source_target_pairs={{0,1},{1,2},{2,3},{3,4},{4,5},{5,6},{6,7},{7,8},{8,9},{9,10},{10,1... | collective-permute-start | bytes 393224 | tf_op jit(solution)/shard_map/ppermute | solution.py:434
  6.9 9.2 %collective-permute-start.1 = (bf16[128,512]{1,0:T(8,128)(2,1)}, bf16[128,512]{1,0:T(8,128)(2,1)S(1)}, u32[]{:S(2)}, u32[]{:S(2)}) collective-permute-start(bf16[128,512]{1,0:T(8,128)(2,1)} %get-tuple-element.8), channel_id=1, source_target_pairs={{1,0},{2,1},{3,2},{4,3},{5,4},{6,5},{7,6},{8,7},{9,8},{10,9},{11,1... | collective-permute-start | bytes 393224 | tf_op jit(solution)/shard_map/ppermute | solution.py:435
  15.0 1.2 %copy-start.2 = (bf16[128,512]{1,0:T(8,128)(2,1)}, bf16[128,512]{1,0:T(8,128)(2,1)S(1)}, u32[]{:S(2)}) copy-start(bf16[128,512]{1,0:T(8,128)(2,1)S(1)} %collective-permute-done.up_ref) | copy-start | bytes 393220
  16.1 0.7 copy-start.3
  60.8 7.9 %copy-start = (bf16[64,4096]{1,0:T(8,128)(2,1)}, bf16[64,4096]{1,0:T(8,128)(2,1)S(1)}, u32[]{:S(2)}) copy-start(bf16[64,4096]{1,0:T(8,128)(2,1)S(1)} %reshape.9.own_ref) | copy-start | bytes 1572868
  60.8 7.9 %collective-permute-start.2 = (bf16[64,4096]{1,0:T(8,128)(2,1)S(1)}, bf16[64,4096]{1,0:T(8,128)(2,1)S(1)}, u32[]{:S(2)}, u32[]{:S(2)}) collective-permute-start(bf16[64,4096]{1,0:T(8,128)(2,1)S(1)} %reshape.9.own_ref), channel_id=1, source_target_pairs={{0,1},{1,0},{2,3},{3,2},{4,5},{5,4},{6,7},{7,6},{8,9},{9,8},{10,11... | collective-permute-start | bytes 1572872 | tf_op jit(solution)/shard_map/ppermute | solution.py:438
  68.6 0.8 %copy-start.1 = (bf16[64,4096]{1,0:T(8,128)(2,1)}, bf16[64,4096]{1,0:T(8,128)(2,1)S(1)}, u32[]{:S(2)}) copy-start(bf16[64,4096]{1,0:T(8,128)(2,1)S(1)} %collective-permute-done.2.other_ref) | copy-start | bytes 1572868

commit v2 on v1

--- a/solution.py
+++ b/solution.py
@@ -9,8 +9,8 @@
 from jax.sharding import Mesh
 from jax.sharding import PartitionSpec as P
 
-SLAB = ("chip", "core")
-GROUPS_SLAB = ("groups", "chip", "core")
+SLAB = ("far", "near", "core")
+GROUPS_SLAB = ("groups", "far", "near", "core")
 LANES = 128
 HALF = 4
 SECOND = (-14336.0, 8064.0, -1008.0, 128.0, -9.0)
@@ -20,6 +20,11 @@
 FIRST_UNIT = 840.0
 BF16 = jnp.bfloat16
 F32 = jnp.float32
+VMEM_WHOLE = pl.BlockSpec(memory_space=pltpu.VMEM)
+
+
+def in_vmem(*arrays):
+    return [pltpu.with_memory_space_constraint(a, pltpu.VMEM) for a in arrays]
 
 
 def weight(kind, offset):
@@ -98,7 +103,9 @@
     return quarter_turns(n.astype(jnp.int32), c, s)
 
 
-def pack_kernel(w_top, w_bot, c_top, c_bot, e_top, e_bot, d_top, d_bot, t_top, t_bot, up_ref, down_ref):
+def pack_kernel(
+    w_top, w_bot, c_top, c_bot, e_top, e_bot, d_top, d_bot, t_top, t_bot, partner_ref, neighbour_ref
+):
     low = lax.broadcasted_iota(jnp.int32, (8, w_top.shape[-1]), 0) < HALF
 
     def half_turn(x):
@@ -121,8 +128,19 @@
         for g in range(0, len(groups), 2):
             out[8 * g : 8 * g + 16, :] = jnp.concatenate(groups[g : g + 2], axis=0).astype(BF16)
 
-    emit(up_ref, w_bot, (c_bot, e_bot, d_bot, t_bot), True)
-    emit(down_ref, w_top, (c_top, e_top, d_top, t_top), False)
+    tops = (w_top, (c_top, e_top, d_top, t_top))
+    bottoms = (w_bot, (c_bot, e_bot, d_bot, t_bot))
+    first = lax.axis_index("core") == 0
+
+    @pl.when(first)
+    def _():
+        emit(partner_ref, *bottoms, True)
+        emit(neighbour_ref, *tops, False)
+
+    @pl.when(jnp.logical_not(first))
+    def _():
+        emit(partner_ref, *tops, False)
+        emit(neighbour_ref, *bottoms, True)
 
 
 def pack(wavefields, params):
@@ -138,80 +156,134 @@
     for p in params:
         specs += [pl.BlockSpec((8, cols), lambda i: (0, 0)), pl.BlockSpec((8, cols), lambda i: (last, 0))]
         args += [p, p]
-    out = jax.ShapeDtypeStruct((8 * groups, cols), BF16)
+    out = pltpu.VMEM((8 * groups, cols), BF16)
     return pl.pallas_call(
         pack_kernel,
         grid=(1,),
         in_specs=specs,
-        out_specs=[pl.BlockSpec((8 * groups, cols), lambda i: (0, 0))] * 2,
+        out_specs=[VMEM_WHOLE] * 2,
         out_shape=[out, out],
+        compiler_params=pltpu.CompilerParams(vmem_limit_bytes=8 << 20),
         name="pack",
-    )(*args)
+    )(*(pltpu.with_memory_space_constraint(a, pltpu.HBM) for a in args))
+
+
+def coefficients(courant, eps, delta, tilt):
+    cosine, sine = double_angle(tilt)
+    scaled = courant * (1.0 / SECOND_UNIT)
+    return (
+        0.5 + 0.5 * cosine,
+        sine * (SECOND_UNIT / (FIRST_UNIT * FIRST_UNIT)),
+        scaled * (1.0 + 2.0 * eps),
+        scaled * jnp.sqrt(1.0 + 2.0 * delta),
+        scaled,
+    )
+
+
+def prepare_kernel(
+    counts_ref, courant_ref, eps_ref, delta_ref, tilt_ref, angle_ref,
+    mix_ref, twist_ref, a_ref, b_ref, c_ref, low_c, low_s, high_c, high_s, alive_ref,
+):
+    for r in range(0, courant_ref.shape[0], 8):
+        at = slice(r, r + 8)
+        values = coefficients(courant_ref[at, :], eps_ref[at, :], delta_ref[at, :], tilt_ref[at, :])
+        for ref, value in zip((mix_ref, twist_ref, a_ref, b_ref, c_ref), values, strict=True):
+            ref[at, :] = value
+
+    right_half = lax.broadcasted_iota(jnp.int32, (LANES, LANES), 1) >= LANES // 2
+    angles = jnp.concatenate([angle_ref[...], angle_ref[...]], axis=1)
+    lateral = lax.broadcasted_iota(jnp.int32, (LANES, LANES), 0)
+    modulus = 16 * LANES
+    turn = (lateral * angles) & (modulus - 1)
+    quarter = (turn + modulus // 8) >> int(math.log2(modulus // 4))
+    rest = turn - quarter * (modulus // 4)
+    c1, s1 = small_cos_sin(rest.astype(F32) * (2.0 * math.pi / modulus))
+    c1, s1 = quarter_turns(quarter, c1, s1)
+
+    def times(x, y):
+        return (x[0] * y[0] - x[1] * y[1], x[0] * y[1] + x[1] * y[0])
+
+    value = (jnp.ones_like(c1), jnp.zeros_like(c1))
+    for j in range(8):
+        low_c[j], low_s[j] = value
+        value = (c1, s1) if j == 0 else times(value, (c1, s1))
+    eighth = value
+    scale = 1.0 / math.sqrt(LANES)
+    value = (jnp.where(right_half, 0.0, scale), jnp.where(right_half, scale, 0.0))
+    for j in range(8):
+        high_c[j], high_s[j] = value
+        value = times(value, eighth)
+    live = lax.broadcasted_iota(jnp.int32, (8, LANES), 0) < counts_ref[lax.axis_index(SLAB)]
+    alive_ref[...] = jnp.where(live, 1.0, 0.0)
+
+
+def prepare(params, slab_counts, angle_table):
+    rows, cols = params[0].shape
+    field = pltpu.VMEM((rows, cols), F32)
+    table = pltpu.VMEM((8, LANES, LANES), F32)
+    return pl.pallas_call(
+        prepare_kernel,
+        in_specs=[pl.BlockSpec(memory_space=pltpu.SMEM)] + [VMEM_WHOLE] * 5,
+        out_specs=[VMEM_WHOLE] * 10,
+        out_shape=[field] * 5 + [table] * 4 + [pltpu.VMEM((8, LANES), F32)],
+        compiler_params=pltpu.CompilerParams(vmem_limit_bytes=8 << 20),
+        name="prepare",
+    )(slab_counts, *in_vmem(*params, angle_table.reshape(1, -1)))
 
 
 def main_kernel(
-    counts_ref, wave_ref, courant_ref, eps_ref, delta_ref, tilt_ref, up_ref, down_ref,
-    one_ref, two_ref, xx_ref, xx_across_ref, x_ref, x_across_ref, depth_ref, angle_ref,
+    wave_ref, partner_ref, neighbour_ref, mix_ref, twist_ref, a_ref, b_ref, c_ref,
+    low_c, low_s, high_c, high_s, alive_ref,
+    one_ref, two_ref, xx_ref, xx_across_ref, x_ref, x_across_ref, depth_ref,
     out_ref,
-    mix_ref, twist_ref, a_ref, b_ref, c_ref, field_ref, slope_ref, row_ref, xx_out, xz_out, next_ref,
-    split_ref, spectra_ref, low_c, low_s, high_c, high_s, image_ref,
+    edge_ref, field_ref, slope_ref, row_ref, xx_out, xz_out, next_ref, split_ref, spectra_ref, image_ref,
 ):
     step = pl.program_id(0)
-    rows, cols = courant_ref.shape
+    shots = wave_ref.shape[2]
+    which = step // shots
+    shot = step % shots
+    rows, cols = mix_ref.shape
     ext = rows + 2 * HALF
     tall = rows + 4 * HALF
     low = lax.broadcasted_iota(jnp.int32, (8, cols), 0) < HALF
+    first = lax.axis_index("core") == 0
 
     def half_turn(x):
         return pltpu.roll(x, HALF, 0)
 
     def group(g):
-        return (up_ref[8 * g : 8 * g + 8, :].astype(F32), down_ref[8 * g : 8 * g + 8, :].astype(F32))
-
-    def first_halves(g):
-        u, d = group(g)
-        return jnp.where(low, u, half_turn(d))
-
-    def second_halves(g):
-        u, d = group(g)
-        return jnp.where(low, half_turn(u), d)
-
-    params = wave_groups = 3 * 4
+        at = pl.ds(g if isinstance(g, int) else pl.multiple_of(g, 8), 8)
+        a, b = (partner_ref[at, :].astype(F32), neighbour_ref[at, :].astype(F32))
+        return jnp.where(first, b, a), jnp.where(first, a, b)
 
     @pl.when(step == 0)
     def _():
-        def coefficients(at, courant, eps, delta, tilt):
-            cosine, sine = double_angle(tilt)
-            scaled = courant * (1.0 / SECOND_UNIT)
-            mix_ref[at, :] = 0.5 + 0.5 * cosine
-            twist_ref[at, :] = sine * (SECOND_UNIT / (FIRST_UNIT * FIRST_UNIT))
-            a_ref[at, :] = scaled * (1.0 + 2.0 * eps)
-            b_ref[at, :] = scaled * jnp.sqrt(1.0 + 2.0 * delta)
-            c_ref[at, :] = scaled
-
-        for r in range(0, rows, 8):
-            at = slice(r, r + 8)
-            coefficients(at, courant_ref[at, :], eps_ref[at, :], delta_ref[at, :], tilt_ref[at, :])
-        high = second_halves(params + 1)
-        tilt = high + first_halves(params + 2)
-        coefficients(
-            slice(rows, ext), first_halves(params), second_halves(params), first_halves(params + 1), tilt
+        start = 8 * 3 * 2 * shots
+
+        def first_halves(g):
+            u, d = group(start + 8 * g)
+            return jnp.where(low, u, half_turn(d))
+
+        def second_halves(g):
+            u, d = group(start + 8 * g)
+            return jnp.where(low, half_turn(u), d)
+
+        values = coefficients(
+            first_halves(0), second_halves(0), first_halves(1), second_halves(1) + first_halves(2)
         )
-
-    base = 3 * step
-
-    def dyn_group(ref, g):
-        return ref[pl.ds(pl.multiple_of(8 * (base + g), 8), 8), :].astype(F32)
-
+        for i, value in enumerate(values):
+            edge_ref[i] = value
+
+    base = 8 * 3 * step
     halo = []
     for f in range(2):
-        u, d = (dyn_group(up_ref, f), dyn_group(down_ref, f))
+        u, d = group(base + 8 * f)
         inner = jnp.where(low, half_turn(u), half_turn(d))
         outer = jnp.where(low, u, d)
         halo.append(inner)
-        field_ref[f * tall : f * tall + rows, :] = wave_ref[0, f, 0].astype(BF16)
+        field_ref[f * tall : f * tall + rows, :] = wave_ref[which, f, shot].astype(BF16)
         field_ref[f * tall + rows : (f + 1) * tall, :] = jnp.concatenate([inner, outer], axis=0).astype(BF16)
-    u, d = (dyn_group(up_ref, 2), dyn_group(down_ref, 2))
+    u, d = group(base + 16)
     halo.append(jnp.where(low, u, half_turn(d)))
     halo.append(jnp.where(low, half_turn(u), d))
 
@@ -234,12 +306,18 @@
         along_columns(xx_out, field_ref[...], xx_ref, xx_across_ref)
         along_columns(xz_out, slope_ref[: 2 * count, :], x_ref, x_across_ref)
 
+    def coefficient(i, r):
+        if r < rows:
+            return (mix_ref, twist_ref, a_ref, b_ref, c_ref)[i][r : r + 8, :]
+        return edge_ref[i]
+
     def pieces(f, r, count, value):
         at = slice(f * tall + r, f * tall + r + 8)
         zz = row_ref[at, :]
         xx = xx_out[at, :]
         xz = xz_out[f * count + r : f * count + r + 8, :]
-        turn = mix_ref[r : r + 8, :] * (xx - zz) - twist_ref[r : r + 8, :] * xz
+        mix, twist = (coefficient(i, r) for i in range(2))
+        turn = mix * (xx - zz) - twist * xz
         rest = SECOND_REST * value
         return (zz + turn) - rest if f == 0 else (xx - turn) - rest
 
@@ -247,12 +325,12 @@
     for r in range(0, ext, 8):
         at = slice(r, r + 8)
         if r < rows:
-            p, q, p0, q0 = (wave_ref[0, f, 0, at, :] for f in range(4))
+            p, q, p0, q0 = (wave_ref[which, f, shot, at, :] for f in range(4))
         else:
             p, q, p0, q0 = halo
         across = pieces(0, r, tall, p)
         along = pieces(1, r, tall, q)
-        a, b, c = (a_ref[at, :], b_ref[at, :], c_ref[at, :])
+        a, b, c = (coefficient(i, r) for i in range(2, 5))
         next_ref[0, at, :] = (2.0 * p - p0) + (a * across + b * along)
         next_ref[1, at, :] = (2.0 * q - q0) + (b * across + c * along)
 
@@ -268,7 +346,7 @@
             p, q = (next_ref[0, at, :], next_ref[1, at, :])
             across = pieces(0, h, rows, p)
             along = pieces(1, h, rows, q)
-            parts.append((2.0 * p - wave_ref[0, 0, 0, at, :]) + (a_ref[at, :] * across + b_ref[at, :] * along))
+            parts.append((2.0 * p - wave_ref[which, 0, shot, at, :]) + (a_ref[at, :] * across + b_ref[at, :] * along))
         value = jnp.concatenate(parts, axis=0)
         top = value.astype(BF16)
         split_ref[r : r + 16, :] = top
@@ -286,33 +364,8 @@
 
     @pl.when(step == pl.num_programs(0) - 1)
     def _():
-        right_half = lax.broadcasted_iota(jnp.int32, (LANES, LANES), 1) >= LANES // 2
-        angles = jnp.concatenate([angle_ref[...], angle_ref[...]], axis=1)
-        lateral = lax.broadcasted_iota(jnp.int32, (LANES, LANES), 0)
-        modulus = 16 * LANES
-        turn = (lateral * angles) & (modulus - 1)
-        quarter = (turn + modulus // 8) >> int(math.log2(modulus // 4))
-        rest = turn - quarter * (modulus // 4)
-        c1, s1 = small_cos_sin(rest.astype(F32) * (2.0 * math.pi / modulus))
-        c1, s1 = quarter_turns(quarter, c1, s1)
-
-        def times(x, y):
-            return (x[0] * y[0] - x[1] * y[1], x[0] * y[1] + x[1] * y[0])
-
-        unit = (jnp.ones_like(c1), jnp.zeros_like(c1))
-        value = unit
-        for j in range(8):
-            low_c[j], low_s[j] = value
-            value = (c1, s1) if j == 0 else times(value, (c1, s1))
-        eighth = value
-        scale = 1.0 / math.sqrt(LANES)
-        value = (jnp.where(right_half, 0.0, scale), jnp.where(right_half, scale, 0.0))
-        for j in range(8):
-            high_c[j], high_s[j] = value
-            value = times(value, eighth)
-
         left_lane = lax.broadcasted_iota(jnp.int32, (8, LANES), 1) < LANES // 2
-        alive = lax.broadcasted_iota(jnp.int32, (8, LANES), 0) < counts_ref[lax.axis_index(SLAB)]
+        alive = alive_ref[...]
 
         def some(j, carry):
             hc, hs = (high_c[j], high_s[j])
@@ -334,9 +387,7 @@
                     odd = odd + pltpu.roll(odd, LANES // 2, 1)
                     pair = []
                     where_to = pl.multiple_of((4 * j + i // 2) * LANES, LANES)
-                    image_ref[:, pl.ds(where_to, LANES)] = jnp.where(
-                        alive, jnp.where(left_lane, even, odd), 0.0
-                    )
+                    image_ref[:, pl.ds(where_to, LANES)] = alive * jnp.where(left_lane, even, odd)
             return carry
 
         def half_turn_small(x):
@@ -346,11 +397,10 @@
         out_ref[...] = image_ref[:per_slab, :].astype(BF16)
 
 
-def images_of(wavefields, params, up, down, slab_counts, angle_table):
+def images_of(wavefields, partner, neighbour, prepared, angles):
     two, four, shots, rows, cols = wavefields.shape
     bins = rows // 2
     per_slab = cols // rows
-    angles = angle_table.shape[0]
     ext = rows + 2 * HALF
     tall = rows + 4 * HALF
     one, both = row_tables(rows)
@@ -361,18 +411,10 @@
     depth_low = (depth - depth_top.astype(np.float32)).astype(jnp.bfloat16)
     depth = np.concatenate([depth_top, depth_top, depth_low], axis=1)
     tables = [jnp.asarray(t, dtype=BF16) for t in (one, both, xx, xx_across, x, x_across, depth)]
-
-    def whole(a):
-        return pl.BlockSpec(a.shape, lambda i: (0,) * a.ndim)
-
-    angle_row = angle_table.reshape(1, angles)
-    args = [slab_counts, wavefields, *params, up, down, *tables, angle_row]
-    specs = [
-        pl.BlockSpec(memory_space=pltpu.SMEM),
-        pl.BlockSpec((1, four, 1, rows, cols), lambda i: (i // shots, 0, i % shots, 0, 0)),
-    ] + [whole(a) for a in args[2:]]
+    args = [wavefields, partner, neighbour, *prepared, *tables]
     out_shape = (per_slab, bins * angles)
-    scratch = [pltpu.VMEM((ext, cols), F32)] * 5 + [
+    scratch = [
+        pltpu.VMEM((5, 2 * HALF, cols), F32),
         pltpu.VMEM((2 * tall, cols), BF16),
         pltpu.VMEM((2 * tall, cols), BF16),
         pltpu.VMEM((2 * tall, cols), F32),
@@ -381,29 +423,32 @@
         pltpu.VMEM((2, ext, cols), F32),
         pltpu.VMEM((3 * rows, cols), BF16),
         pltpu.VMEM((32 * bins, LANES), F32),
-    ] + [pltpu.VMEM((8, LANES, LANES), F32)] * 4 + [pltpu.VMEM((8, bins * angles), F32)]
+        pltpu.VMEM((8, bins * angles), F32),
+    ]
     return pl.pallas_call(
         main_kernel,
-        grid=(2 * shots,),
-        in_specs=specs,
-        out_specs=pl.BlockSpec(out_shape, lambda i: (0, 0)),
-        out_shape=jax.ShapeDtypeStruct(out_shape, BF16),
+        grid=(two * shots,),
+        in_specs=[VMEM_WHOLE] * len(args),
+        out_specs=VMEM_WHOLE,
+        out_shape=pltpu.VMEM(out_shape, BF16),
         scratch_shapes=scratch,
+        compiler_params=pltpu.CompilerParams(vmem_limit_bytes=24 << 20),
         name="images",
-    )(*args)
-
-
-def pick_kernel(loc_ref, own_ref, other_ref, out_ref):
+    )(*in_vmem(*args))
+
+
+def pick_kernel(loc_ref, own_ref, other_ref, out_ref, *, per_slab):
     slab = lax.axis_index(SLAB)
     core = lax.axis_index("core")
+    far, near = (lax.axis_size("far"), lax.axis_size("near"))
     count = out_ref.shape[0]
     per_row = LANES // count
     loc = loc_ref[pl.ds(slab // per_row, 1), :]
     loc = pltpu.roll(loc, (LANES - (slab % per_row) * count) % LANES, 1)[:, :count]
     held = own_ref.shape[0]
-    per_slab = 4
     owner = loc // per_slab
-    index = (owner // 2) * per_slab + loc % per_slab
+    chip = owner // 2
+    index = ((chip % near) * far + chip // near) * per_slab + loc % per_slab
     mine = owner % 2 == core
     row = lax.broadcasted_iota(jnp.int32, (held, count), 0)
     hit = row == index
@@ -416,32 +461,39 @@
     out_ref[...] = choose(own_hot, own_ref) + choose(other_hot, other_ref)
 
 
-def pick(loc_patch, own, other, count):
+def pick(loc_patch, own, other, count, per_slab):
     width = own.shape[1]
     return pl.pallas_call(
-        pick_kernel,
+        lambda *refs: pick_kernel(*refs, per_slab=per_slab),
+        in_specs=[VMEM_WHOLE] * 3,
         out_shape=jax.ShapeDtypeStruct((count, width), F32),
+        compiler_params=pltpu.CompilerParams(vmem_limit_bytes=8 << 20),
         name="pick",
-    )(loc_patch.reshape(-1, LANES), own, other)
+    )(*in_vmem(loc_patch.reshape(-1, LANES), own, other))
 
 
 def per_device(
     wavefields, courant, epsilon, anisotropy_delta, tilt_angle, loc_patch, slab_counts, angle_table
 ):
     slabs = lax.axis_size(SLAB)
+    per_slab = wavefields.shape[4] // wavefields.shape[3]
     params = (courant, epsilon, anisotropy_delta, tilt_angle)
-    up_send, down_send = pack(wavefields, params)
-    up = lax.ppermute(up_send, SLAB, [(i, i + 1) for i in range(slabs - 1)])
-    down = lax.ppermute(down_send, SLAB, [(i + 1, i) for i in range(slabs - 1)])
-    images = images_of(wavefields, params, up, down, slab_counts, angle_table)
-    own = lax.all_gather(images, "chip", tiled=True)
+    to_partner, to_neighbour = pack(wavefields, params)
+    partner = lax.ppermute(to_partner, "core", [(0, 1), (1, 0)])
+    pairs = [(i, i + 1) for i in range(1, slabs - 1, 2)]
+    neighbour = lax.ppermute(to_neighbour, SLAB, pairs + [(j, i) for i, j in pairs])
+    prepared = prepare(params, slab_counts, angle_table)
+    images = images_of(wavefields, partner, neighbour, prepared, angle_table.shape[0])
+    own = lax.all_gather(lax.all_gather(images, "far", tiled=True), "near", tiled=True)
     other = lax.ppermute(own, "core", [(0, 1), (1, 0)])
-    return pick(loc_patch, own, other, loc_patch.shape[0] // slabs)
+    return pick(loc_patch, own, other, loc_patch.shape[0] // slabs, per_slab)
 
 
 def solution(mesh):
-    slabs = mesh.shape["slab"]
-    finer = Mesh(mesh.devices.reshape(mesh.shape["groups"], slabs // 2, 2), GROUPS_SLAB)
+    chips = mesh.shape["slab"] // 2
+    near = 4 if chips % 4 == 0 else 1
+    shape = (mesh.shape["groups"], chips // near, near, 2)
+    finer = Mesh(mesh.devices.reshape(shape), GROUPS_SLAB)
     in_specs = (
         P(None, None, "groups", SLAB, None),
         P(SLAB, None),

time: 72 us -> 66.3 us (0.921)
  Pallas kernels: 17.3 us -> 13.5 us
  starting transfers between devices: 19.5 us -> 15.9 us
  waiting for transfers between devices: 2.69 us -> 4.43 us
  local copies, waits for them, and re-layouts: 1.57 us -> 0.11 us
  blocking collectives: 30.8 us -> 32.1 us
    pallas_call x3 -> x4, Pallas kernels: 17.3 us -> 13.5 us  [the longest x1 9.57 us: images_of(): pl.pallas_call(main_kernel, grid=(two * shots,), in_specs=[VMEM_WHOLE] *...]
    ppermute x1, starting transfers between devices: 6.32 us -> 3.95 us  [per_device(): other = lax.ppermute(own, 'core', [(0, 1), (1, 0)])]
    ppermute x2, waiting for transfers between devices: 1.15 us -> 2.89 us  [the longest x1 2.89 us: per_device(): lax.ppermute(to_neighbour, SLAB, pairs + [(j, i) for i, j in pairs])]
    unnamed x9 -> x31, local copies, waits for them, and re-layouts: 1.57 us -> 0.11 us
    all_gather x1 -> x2, blocking collectives: 30.8 us -> 32.1 us  [the longest x1 16.7 us: per_device(): lax.all_gather(images, 'far', tiled=True)]
    ppermute x2, starting transfers between devices: 13.1 us -> 11.9 us  [the longest x1 10 us: per_device(): partner = lax.ppermute(to_partner, 'core', [(0, 1), (1, 0)])]
  transfers between devices with their start and end apart: 3 -> 3, of which waited for: 2 -> 2; matrix products, arithmetic and copies ran while one was open for 0% -> 0% of each run, Pallas kernels for 0% -> 2%
where the time goes in v2:
time: 66.3 us; the launch traced here: 66.2 us
  blocking collectives  32.1 us (48%)
  starting transfers between devices  15.9 us (24%)
  Pallas kernels  13.5 us (20%)
  waiting for transfers between devices  4.43 us (7%)
    all_gather x1, blocking collectives, per_device(): lax.all_gather(images, 'far', tiled=True)  16.7 us
    all_gather x1, blocking collectives, per_device(): lax.all_gather(lax.all_gather(images, 'far', tiled=True), 'near', tiled=T...  15.3 us
    ppermute x1, starting transfers between devices, per_device(): partner = lax.ppermute(to_partner, 'core', [(0, 1), (1, 0)])  10 us
    pallas_call x1, Pallas kernels, images_of(): pl.pallas_call(main_kernel, grid=(two * shots,), in_specs=[VMEM_WHOLE] *...  9.57 us
    ppermute x1, starting transfers between devices, per_device(): other = lax.ppermute(own, 'core', [(0, 1), (1, 0)])  3.95 us
    ppermute x1, waiting for transfers between devices, per_device(): lax.ppermute(to_neighbour, SLAB, pairs + [(j, i) for i, j in pairs])  2.89 us
    ppermute x1, starting transfers between devices, per_device(): lax.ppermute(to_neighbour, SLAB, pairs + [(j, i) for i, j in pairs])  1.94 us
    ppermute x1, waiting for transfers between devices, per_device(): other = lax.ppermute(own, 'core', [(0, 1), (1, 0)])  1.54 us
  transfers between devices with their start and end apart: 3, of which 2 were waited for; matrix products, arithmetic and copies ran while one was open for 0% of the time, Pallas kernels for 2%

profile of v2, /device:TPU:69, one launch (start us, length us, event | category | flops | bytes accessed | tf_op | source)
XLA Modules:
  0.0 66.2 jit_solution(13525569241605259845)
XLA Ops:
  0.0 0.0 copy-start.8
  0.0 0.0 copy-start.9
  0.0 0.0 copy-start.10
  0.0 0.0 copy-start.11
  0.1 0.0 copy-start.4
  0.1 0.0 copy-start.3
  0.1 0.0 copy-start.2
  0.1 0.0 copy-start.1
  0.1 0.0 copy-start
  0.1 0.0 copy-start.14
  0.1 0.0 copy-start.13
  0.1 1.2 %pack.1 = (bf16[128,512]{1,0:T(8,128)(2,1)S(1)}, bf16[128,512]{1,0:T(8,128)(2,1)S(1)}) custom-call(f32[2,4,2,128,512]{4,3,2,1,0:T(8,128)} %wave_ref.1, f32[2,4,2,128,512]{4,3,2,1,0:T(8,128)} %wave_ref.1, f32[128,512]{1,0:T(8,128)} %courant_ref.1, f32[128,512]{1,0:T(8,128)} %courant_ref.1, f32[128,512]{1,0:T(8,128)} %eps_ref.1, f32[128,512]{1,0:T(8,128)} %eps_ref.1, ...), custom_call_target="tpu_custom_call" | custom-call | tf_op jit(solution)/shard_map/pack/pallas_call | solution.py:160
  1.4 10.0 %collective-permute-start = (bf16[128,512]{1,0:T(8,128)(2,1)S(1)}, bf16[128,512]{1,0:T(8,128)(2,1)S(1)}, u32[]{:S(2)}, u32[]{:S(2)}) collective-permute-start(bf16[128,512]{1,0:T(8,128)(2,1)S(1)} %get-tuple-element.17), channel_id=1, source_target_pairs={{0,1},{1,0},{2,3},{3,2},{4,5},{5,4},{6,7},{7,6},{8,9},{9,8},{10,11... | collective-permute-start | bytes 393224 | tf_op jit(solution)/shard_map/ppermute | solution.py:482
  11.4 1.9 %collective-permute-start.1 = (bf16[128,512]{1,0:T(8,128)(2,1)S(1)}, bf16[128,512]{1,0:T(8,128)(2,1)S(1)}, u32[]{:S(2)}, u32[]{:S(2)}) collective-permute-start(bf16[128,512]{1,0:T(8,128)(2,1)S(1)} %get-tuple-element.18), channel_id=1, source_target_pairs={{1,2},{3,4},{5,6},{7,8},{9,10},{11,12},{13,14},{15,16},{17,18},{19... | collective-permute-start | bytes 393224 | tf_op jit(solution)/shard_map/ppermute | solution.py:484
  13.3 0.0 copy-done.4
  13.3 0.0 copy-done.3
  13.4 0.0 copy-done.2
  13.4 0.0 copy-done.1
  13.4 0.0 copy-done.14
  13.4 0.0 copy-done.13
  13.4 1.4 %prepare.1 = (f32[128,512]{1,0:T(8,128)S(1)}, f32[128,512]{1,0:T(8,128)S(1)}, f32[128,512]{1,0:T(8,128)S(1)}, f32[128,512]{1,0:T(8,128)S(1)}, f32[128,512]{1,0:T...) custom-call(s32[32]{0:T(128)S(1)} %copy-done.13, ...), custom_call_target="tpu_custom_call" | custom-call | tf_op jit(solution)/shard_map/prepare/pallas_call | solution.py:224
  14.8 0.0 collective-permute-done.partner_ref
  14.8 2.9 %collective-permute-done.1.neighbour_ref = bf16[128,512]{1,0:T(8,128)(2,1)S(1)} collective-permute-done((bf16[128,512]{1,0:T(8,128)(2,1)S(1)}, bf16[128,512]{1,0:T(8,128)(2,1)S(1)}, u32[]{:S(2)}, u32[]{:S(2)}) %collective-permute-start.1) | collective-permute-done | bytes 131104 | tf_op jit(solution)/shard_map/ppermute | solution.py:484
  17.7 0.0 copy-done.5
  17.7 0.0 copy-done.6
  17.8 0.0 copy-start.12
  17.8 9.6 %images.1 = bf16[4,4096]{1,0:T(4,128)(2,1)S(1)} custom-call(f32[2,4,2,128,512]{4,3,2,1,0:T(8,128)S(1)} %copy-done, bf16[128,512]{1,0:T(8,128)(2,1)S(1)} %collective-permute-done.partner_ref, bf16[128,512]{1,0:T(8,128)(2,1)S(1)} %collective-permute-done.1.neighbour_ref, f32[128,512]{1,0:T(8,128)S(1)} %get-tuple-element.19.mix_ref, ...), custom_call_target="tpu_custom_call" | custom-call | tf_op jit(solution)/shard_map/images/pallas_call | solution.py:428
  27.3 16.7 %all-gather = bf16[4,4,4096]{2,1,0:T(4,128)(2,1)S(1)} all-gather(bf16[1,4,4096]{2,1,0:T(4,128)(2,1)S(1)} %bitcast.3), channel_id=1, replica_groups=mesh['groups'=4,'far'=4,'near'=4,'core'=2] {'far'}, dimensions={0}, use_global_device_ids=true | all-gather | bytes 163840 | tf_op jit(solution)/shard_map/all_gather | solution.py:487
  44.1 15.3 %all_gather.7.refs_1_ = bf16[64,4096]{1,0:T(8,128)(2,1)S(1)} all-gather(bf16[16,4096]{1,0:T(8,128)(2,1)S(1)} %reshape.9), channel_id=1, replica_groups=mesh['groups'=4,'far'=4,'near'=4,'core'=2] {'near'}, dimensions={0}, use_global_device_ids=true | all-gather | bytes 655360 | tf_op jit(solution)/shard_map/all_gather | solution.py:487
  59.5 4.0 %collective-permute-start.2 = (bf16[64,4096]{1,0:T(8,128)(2,1)S(1)}, bf16[64,4096]{1,0:T(8,128)(2,1)S(1)}, u32[]{:S(2)}, u32[]{:S(2)}) collective-permute-start(bf16[64,4096]{1,0:T(8,128)(2,1)S(1)} %all_gather.7.refs_1_), channel_id=1, source_target_pairs={{0,1},{1,0},{2,3},{3,2},{4,5},{5,4},{6,7},{7,6},{8,9},{9,8},{10,11... | collective-permute-start | bytes 1572872 | tf_op jit(solution)/shard_map/ppermute | solution.py:488
  63.4 1.5 %collective-permute-done.2.refs_2_ = bf16[64,4096]{1,0:T(8,128)(2,1)S(1)} collective-permute-done((bf16[64,4096]{1,0:T(8,128)(2,1)S(1)}, bf16[64,4096]{1,0:T(8,128)(2,1)S(1)}, u32[]{:S(2)}, u32[]{:S(2)}) %collective-permute-start.2) | collective-permute-done | bytes 524320 | tf_op jit(solution)/shard_map/ppermute | solution.py:488
  65.0 1.2 %pick.1 = f32[32,4096]{1,0:T(8,128)} custom-call(s32[8,128]{1,0:T(8,128)S(1)} %bitcast.4, bf16[64,4096]{1,0:T(8,128)(2,1)S(1)} %all_gather.7.refs_1_, bf16[64,4096]{1,0:T(8,128)(2,1)S(1)} %collective-permute-done.2.refs_2_), custom_call_target="tpu_custom_call" | custom-call | tf_op jit(solution)/shard_map/pick/pallas_call | solution.py:466
  (11 shorter events, 0.1 us)
Async XLA Ops:
  0.0 17.7 %copy-start.5 = (bf16[288,144]{1,0:T(8,128)(2,1)S(1)}, bf16[288,144]{1,0:T(8,128)(2,1)}, u32[]{:S(2)}) copy-start(bf16[288,144]{1,0:T(8,128)(2,1)} %constant.14.clone.one_ref) | copy-start | bytes 248836
  0.0 17.7 %copy-start.6 = (bf16[256,256]{1,0:T(8,128)(2,1)S(1)}, bf16[256,256]{1,0:T(8,128)(2,1)}, u32[]{:S(2)}) copy-start(bf16[256,256]{1,0:T(8,128)(2,1)} %constant.19.clone.x_across_ref) | copy-start | bytes 393220
  0.0 17.7 %copy-start.7 = (bf16[256,256]{1,0:T(8,128)(2,1)S(1)}, bf16[256,256]{1,0:T(8,128)(2,1)}, u32[]{:S(2)}) copy-start(bf16[256,256]{1,0:T(8,128)(2,1)} %constant.18.clone.x_ref) | copy-start | bytes 393220
  0.0 17.7 %copy-start.8 = (bf16[256,256]{1,0:T(8,128)(2,1)S(1)}, bf16[256,256]{1,0:T(8,128)(2,1)}, u32[]{:S(2)}) copy-start(bf16[256,256]{1,0:T(8,128)(2,1)} %constant.17.clone.xx_across_ref) | copy-start | bytes 393220
  0.0 17.7 %copy-start.9 = (bf16[256,256]{1,0:T(8,128)(2,1)S(1)}, bf16[256,256]{1,0:T(8,128)(2,1)}, u32[]{:S(2)}) copy-start(bf16[256,256]{1,0:T(8,128)(2,1)} %constant.16.clone.xx_ref) | copy-start | bytes 393220
  0.0 17.7 %copy-start.10 = (bf16[256,144]{1,0:T(8,128)(2,1)S(1)}, bf16[256,144]{1,0:T(8,128)(2,1)}, u32[]{:S(2)}) copy-start(bf16[256,144]{1,0:T(8,128)(2,1)} %constant.15.clone.two_ref) | copy-start | bytes 221188
  0.0 17.7 %copy-start.11 = (bf16[128,384]{1,0:T(8,128)(2,1)S(1)}, bf16[128,384]{1,0:T(8,128)(2,1)}, u32[]{:S(2)}) copy-start(bf16[128,384]{1,0:T(8,128)(2,1)} %constant.20.clone.depth_ref) | copy-start | bytes 294916
  0.1 13.3 %copy-start.4 = (f32[128,512]{1,0:T(8,128)S(1)}, f32[128,512]{1,0:T(8,128)}, u32[]{:S(2)}) copy-start(f32[128,512]{1,0:T(8,128)} %tilt_ref.1) | copy-start | bytes 786436
  0.1 13.3 %copy-start.3 = (f32[128,512]{1,0:T(8,128)S(1)}, f32[128,512]{1,0:T(8,128)}, u32[]{:S(2)}) copy-start(f32[128,512]{1,0:T(8,128)} %delta_ref.1) | copy-start | bytes 786436
  0.1 13.3 %copy-start.2 = (f32[128,512]{1,0:T(8,128)S(1)}, f32[128,512]{1,0:T(8,128)}, u32[]{:S(2)}) copy-start(f32[128,512]{1,0:T(8,128)} %eps_ref.1) | copy-start | bytes 786436
  0.1 13.3 %copy-start.1 = (f32[128,512]{1,0:T(8,128)S(1)}, f32[128,512]{1,0:T(8,128)}, u32[]{:S(2)}) copy-start(f32[128,512]{1,0:T(8,128)} %courant_ref.1) | copy-start | bytes 786436
  0.1 17.6 %copy-start = (f32[2,4,2,128,512]{4,3,2,1,0:T(8,128)S(1)}, f32[2,4,2,128,512]{4,3,2,1,0:T(8,128)}, u32[]{:S(2)}) copy-start(f32[2,4,2,128,512]{4,3,2,1,0:T(8,128)} %wave_ref.1) | copy-start | bytes 12582916
  0.1 13.3 %copy-start.14 = (s32[64]{0:T(128)S(1)}, s32[64]{0:T(128)}, u32[]{:S(2)}) copy-start(s32[64]{0:T(128)} %param.22) | copy-start | bytes 772
  0.1 13.3 %copy-start.13 = (s32[32]{0:T(128)S(1)}, s32[32]{0:T(128)}, u32[]{:S(2)}) copy-start(s32[32]{0:T(128)} %counts_ref.1) | copy-start | bytes 388
  1.4 13.4 %collective-permute-start = (bf16[128,512]{1,0:T(8,128)(2,1)S(1)}, bf16[128,512]{1,0:T(8,128)(2,1)S(1)}, u32[]{:S(2)}, u32[]{:S(2)}) collective-permute-start(bf16[128,512]{1,0:T(8,128)(2,1)S(1)} %get-tuple-element.17), channel_id=1, source_target_pairs={{0,1},{1,0},{2,3},{3,2},{4,5},{5,4},{6,7},{7,6},{8,9},{9,8},{10,11... | collective-permute-start | bytes 393224 | tf_op jit(solution)/shard_map/ppermute | solution.py:482
  11.4 6.3 %collective-permute-start.1 = (bf16[128,512]{1,0:T(8,128)(2,1)S(1)}, bf16[128,512]{1,0:T(8,128)(2,1)S(1)}, u32[]{:S(2)}, u32[]{:S(2)}) collective-permute-start(bf16[128,512]{1,0:T(8,128)(2,1)S(1)} %get-tuple-element.18), channel_id=1, source_target_pairs={{1,2},{3,4},{5,6},{7,8},{9,10},{11,12},{13,14},{15,16},{17,18},{19... | collective-permute-start | bytes 393224 | tf_op jit(solution)/shard_map/ppermute | solution.py:484
  17.8 47.2 %copy-start.12 = (s32[1024]{0:T(1024)S(1)}, s32[1024]{0:T(1024)}, u32[]{:S(2)}) copy-start(s32[1024]{0:T(1024)} %param.20) | copy-start | bytes 12292
  59.5 5.5 %collective-permute-start.2 = (bf16[64,4096]{1,0:T(8,128)(2,1)S(1)}, bf16[64,4096]{1,0:T(8,128)(2,1)S(1)}, u32[]{:S(2)}, u32[]{:S(2)}) collective-permute-start(bf16[64,4096]{1,0:T(8,128)(2,1)S(1)} %all_gather.7.refs_1_), channel_id=1, source_target_pairs={{0,1},{1,0},{2,3},{3,2},{4,5},{5,4},{6,7},{7,6},{8,9},{9,8},{10,11... | collective-permute-start | bytes 1572872 | tf_op jit(solution)/shard_map/ppermute | solution.py:488

commit v3 on v2

--- a/solution.py
+++ b/solution.py
@@ -9,10 +9,12 @@
 from jax.sharding import Mesh
 from jax.sharding import PartitionSpec as P
 
-SLAB = ("far", "near", "core")
-GROUPS_SLAB = ("groups", "far", "near", "core")
+SLAB = ("chip", "core")
+GROUPS_SLAB = ("groups", "chip", "core")
 LANES = 128
 HALF = 4
+PITCH = 40
+FAR, NEAR = ((0, 3, 6), (0, 1, 2))
 SECOND = (-14336.0, 8064.0, -1008.0, 128.0, -9.0)
 SECOND_REST = 14.0
 SECOND_UNIT = 5040.0
@@ -240,8 +242,6 @@
 ):
     step = pl.program_id(0)
     shots = wave_ref.shape[2]
-    which = step // shots
-    shot = step % shots
     rows, cols = mix_ref.shape
     ext = rows + 2 * HALF
     tall = rows + 4 * HALF
@@ -274,93 +274,130 @@
         for i, value in enumerate(values):
             edge_ref[i] = value
 
-    base = 8 * 3 * step
-    halo = []
-    for f in range(2):
-        u, d = group(base + 8 * f)
-        inner = jnp.where(low, half_turn(u), half_turn(d))
-        outer = jnp.where(low, u, d)
-        halo.append(inner)
-        field_ref[f * tall : f * tall + rows, :] = wave_ref[which, f, shot].astype(BF16)
-        field_ref[f * tall + rows : (f + 1) * tall, :] = jnp.concatenate([inner, outer], axis=0).astype(BF16)
-    u, d = group(base + 16)
-    halo.append(jnp.where(low, u, half_turn(d)))
-    halo.append(jnp.where(low, half_turn(u), d))
+    bins = rows // 2
+    per_slab = cols // LANES
 
     def along_columns(out, source, inside, across):
+        n = source.shape[0]
+        out[:n, LANES : 3 * LANES] = jnp.dot(
+            source[:, LANES : 3 * LANES], across[...], preferred_element_type=F32
+        )
         left = jnp.dot(source[:, : 2 * LANES], inside[...], preferred_element_type=F32)
+        out[:n, :LANES] = left[:, :LANES]
+        out[:n, LANES : 2 * LANES] += left[:, LANES:]
         right = jnp.dot(source[:, 2 * LANES :], inside[...], preferred_element_type=F32)
-        mid = jnp.dot(source[:, LANES : 3 * LANES], across[...], preferred_element_type=F32)
-        n = source.shape[0]
-        out[:n, :LANES] = left[:, :LANES]
-        out[:n, LANES : 2 * LANES] = left[:, LANES:] + mid[:, :LANES]
-        out[:n, 2 * LANES : 3 * LANES] = right[:, :LANES] + mid[:, LANES:]
+        out[:n, 2 * LANES : 3 * LANES] += right[:, :LANES]
         out[:n, 3 * LANES :] = right[:, LANES:]
-
-    def derive(table, count):
-        for f in range(2):
-            source = field_ref[f * tall : (f + 1) * tall, :]
-            product = jnp.dot(table[...], source, preferred_element_type=F32)
-            row_ref[f * tall : f * tall + count, :] = product[:count]
-            slope_ref[f * count : (f + 1) * count, :] = product[count:].astype(BF16)
-        along_columns(xx_out, field_ref[...], xx_ref, xx_across_ref)
-        along_columns(xz_out, slope_ref[: 2 * count, :], x_ref, x_across_ref)
 
     def coefficient(i, r):
         if r < rows:
             return (mix_ref, twist_ref, a_ref, b_ref, c_ref)[i][r : r + 8, :]
         return edge_ref[i]
 
-    def pieces(f, r, count, value):
-        at = slice(f * tall + r, f * tall + r + 8)
-        zz = row_ref[at, :]
-        xx = xx_out[at, :]
-        xz = xz_out[f * count + r : f * count + r + 8, :]
-        mix, twist = (coefficient(i, r) for i in range(2))
-        turn = mix * (xx - zz) - twist * xz
-        rest = SECOND_REST * value
-        return (zz + turn) - rest if f == 0 else (xx - turn) - rest
-
-    derive(one_ref, tall)
-    for r in range(0, ext, 8):
-        at = slice(r, r + 8)
-        if r < rows:
-            p, q, p0, q0 = (wave_ref[which, f, shot, at, :] for f in range(4))
-        else:
-            p, q, p0, q0 = halo
-        across = pieces(0, r, tall, p)
-        along = pieces(1, r, tall, q)
-        a, b, c = (coefficient(i, r) for i in range(2, 5))
-        next_ref[0, at, :] = (2.0 * p - p0) + (a * across + b * along)
-        next_ref[1, at, :] = (2.0 * q - q0) + (b * across + c * along)
-
-    for f in range(2):
-        field_ref[f * tall : f * tall + rows, :] = next_ref[f, :rows, :].astype(BF16)
-        edge = next_ref[f, rows:ext, :]
-        field_ref[f * tall + rows : (f + 1) * tall, :] = jnp.concatenate([edge, jnp.zeros_like(edge)], axis=0).astype(BF16)
-    derive(two_ref, rows)
-    for r in range(0, rows, 16):
-        parts = []
-        for h in (r, r + 8):
-            at = slice(h, h + 8)
-            p, q = (next_ref[0, at, :], next_ref[1, at, :])
-            across = pieces(0, h, rows, p)
-            along = pieces(1, h, rows, q)
-            parts.append((2.0 * p - wave_ref[which, 0, shot, at, :]) + (a_ref[at, :] * across + b_ref[at, :] * along))
-        value = jnp.concatenate(parts, axis=0)
-        top = value.astype(BF16)
-        split_ref[r : r + 16, :] = top
-        split_ref[rows + r : rows + r + 16, :] = (value - top.astype(F32)).astype(BF16)
-        split_ref[2 * rows + r : 2 * rows + r + 16, :] = top
-    spectra = jnp.dot(depth_ref[...], split_ref[...], preferred_element_type=F32)
-    bins = rows // 2
-    per_slab = cols // LANES
-    for part in range(2):
-        for m in range(per_slab):
-            start = 16 * part + per_slab * step + m
-            spectra_ref[pl.ds(start, bins, stride=32), :] = spectra[
-                part * bins : (part + 1) * bins, m * LANES : (m + 1) * LANES
-            ]
+    class Item:
+        def __init__(self, shot):
+            self.shot = shot
+            self.field, self.slope, self.zz, self.xx, self.xz, self.next, self.split = (
+                ref.at[shot]
+                for ref in (field_ref, slope_ref, row_ref, xx_out, xz_out, next_ref, split_ref)
+            )
+
+        def load(self):
+            base = 8 * 3 * (step * shots + self.shot)
+            self.halo = []
+            for f in range(2):
+                u, d = group(base + 8 * f)
+                inner = jnp.where(low, half_turn(u), half_turn(d))
+                outer = jnp.where(low, u, d)
+                self.halo.append(inner)
+                self.field[f * tall : f * tall + rows, :] = wave_ref[step, f, self.shot].astype(BF16)
+                self.field[f * tall + rows : (f + 1) * tall, :] = jnp.concatenate(
+                    [inner, outer], axis=0
+                ).astype(BF16)
+            u, d = group(base + 16)
+            self.halo.append(jnp.where(low, u, half_turn(d)))
+            self.halo.append(jnp.where(low, half_turn(u), d))
+
+        def derive(self, table, count):
+            for f in range(2):
+                source = self.field[f * tall : (f + 1) * tall, :]
+                product = jnp.dot(table[count:, :], source, preferred_element_type=F32)
+                self.slope[f * count : (f + 1) * count, :] = product.astype(BF16)
+                self.zz[f * tall : f * tall + count, :] = jnp.dot(
+                    table[:count, :], source, preferred_element_type=F32
+                )
+            along_columns(self.xx, self.field[...], xx_ref, xx_across_ref)
+            along_columns(self.xz, self.slope[: 2 * count, :], x_ref, x_across_ref)
+
+        def pieces(self, f, r, count, value):
+            at = slice(f * tall + r, f * tall + r + 8)
+            zz = self.zz[at, :]
+            xx = self.xx[at, :]
+            xz = self.xz[f * count + r : f * count + r + 8, :]
+            mix, twist = (coefficient(i, r) for i in range(2))
+            turn = mix * (xx - zz) - twist * xz
+            rest = SECOND_REST * value
+            return (zz + turn) - rest if f == 0 else (xx - turn) - rest
+
+        def first(self):
+            for r in range(0, ext, 8):
+                at = slice(r, r + 8)
+                if r < rows:
+                    p, q, p0, q0 = (wave_ref[step, f, self.shot, at, :] for f in range(4))
+                else:
+                    p, q, p0, q0 = self.halo
+                across = self.pieces(0, r, tall, p)
+                along = self.pieces(1, r, tall, q)
+                a, b, c = (coefficient(i, r) for i in range(2, 5))
+                self.next[0, at, :] = (2.0 * p - p0) + (a * across + b * along)
+                self.next[1, at, :] = (2.0 * q - q0) + (b * across + c * along)
+
+        def turn_over(self):
+            for f in range(2):
+                self.field[f * tall : f * tall + rows, :] = self.next[f, :rows, :].astype(BF16)
+                edge = self.next[f, rows:ext, :]
+                self.field[f * tall + rows : (f + 1) * tall, :] = jnp.concatenate(
+                    [edge, jnp.zeros_like(edge)], axis=0
+                ).astype(BF16)
+
+        def second(self):
+            for r in range(0, rows, 16):
+                parts = []
+                for h in (r, r + 8):
+                    at = slice(h, h + 8)
+                    p, q = (self.next[0, at, :], self.next[1, at, :])
+                    across = self.pieces(0, h, rows, p)
+                    along = self.pieces(1, h, rows, q)
+                    parts.append(
+                        (2.0 * p - wave_ref[step, 0, self.shot, at, :])
+                        + (a_ref[at, :] * across + b_ref[at, :] * along)
+                    )
+                value = jnp.concatenate(parts, axis=0)
+                top = value.astype(BF16)
+                self.split[r : r + 16, :] = top
+                self.split[rows + r : rows + r + 16, :] = (value - top.astype(F32)).astype(BF16)
+                self.split[2 * rows + r : 2 * rows + r + 16, :] = top
+
+        def transform(self):
+            spectra = jnp.dot(depth_ref[...], self.split[...], preferred_element_type=F32)
+            for part in range(2):
+                for m in range(per_slab):
+                    start = 16 * part + per_slab * (step * shots + self.shot) + m
+                    spectra_ref[pl.ds(start, bins, stride=PITCH), :] = spectra[
+                        part * bins : (part + 1) * bins, m * LANES : (m + 1) * LANES
+                    ]
+
+    items = [Item(shot) for shot in range(shots)]
+    for item in items:
+        item.load()
+        item.derive(one_ref, tall)
+    for item in items:
+        item.first()
+        item.turn_over()
+        item.derive(two_ref, rows)
+    for item in items:
+        item.second()
+        item.transform()
 
     @pl.when(step == pl.num_programs(0) - 1)
     def _():
@@ -374,7 +411,7 @@
                 lc, ls = (low_c[i], low_s[i])
                 real = (hc * lc - hs * ls).astype(BF16)
                 imag = (hc * ls + hs * lc).astype(BF16)
-                at = pl.multiple_of((8 * j + i) * 32, 32)
+                at = pl.multiple_of((8 * j + i) * PITCH, 8)
                 left = jnp.concatenate(
                     [spectra_ref[pl.ds(at, 16), :], spectra_ref[pl.ds(at + 16, 16), :]], axis=1
                 ).astype(BF16)
@@ -415,41 +452,45 @@
     out_shape = (per_slab, bins * angles)
     scratch = [
         pltpu.VMEM((5, 2 * HALF, cols), F32),
-        pltpu.VMEM((2 * tall, cols), BF16),
-        pltpu.VMEM((2 * tall, cols), BF16),
-        pltpu.VMEM((2 * tall, cols), F32),
-        pltpu.VMEM((2 * tall, cols), F32),
-        pltpu.VMEM((2 * tall, cols), F32),
-        pltpu.VMEM((2, ext, cols), F32),
-        pltpu.VMEM((3 * rows, cols), BF16),
-        pltpu.VMEM((32 * bins, LANES), F32),
+        pltpu.VMEM((shots, 2 * tall, cols), BF16),
+        pltpu.VMEM((shots, 2 * tall, cols), BF16),
+        pltpu.VMEM((shots, 2 * tall, cols), F32),
+        pltpu.VMEM((shots, 2 * tall, cols), F32),
+        pltpu.VMEM((shots, 2 * tall, cols), F32),
+        pltpu.VMEM((shots, 2, ext, cols), F32),
+        pltpu.VMEM((shots, 3 * rows, cols), BF16),
+        pltpu.VMEM((PITCH * bins, LANES), F32),
         pltpu.VMEM((8, bins * angles), F32),
     ]
     return pl.pallas_call(
         main_kernel,
-        grid=(two * shots,),
+        grid=(two,),
         in_specs=[VMEM_WHOLE] * len(args),
         out_specs=VMEM_WHOLE,
         out_shape=pltpu.VMEM(out_shape, BF16),
         scratch_shapes=scratch,
-        compiler_params=pltpu.CompilerParams(vmem_limit_bytes=24 << 20),
+        compiler_params=pltpu.CompilerParams(vmem_limit_bytes=32 << 20),
         name="images",
     )(*in_vmem(*args))
 
 
 def pick_kernel(loc_ref, own_ref, other_ref, out_ref, *, per_slab):
     slab = lax.axis_index(SLAB)
-    core = lax.axis_index("core")
-    far, near = (lax.axis_size("far"), lax.axis_size("near"))
+    chip, core = (lax.axis_index("chip"), lax.axis_index("core"))
+    chips = lax.axis_size("chip")
     count = out_ref.shape[0]
     per_row = LANES // count
     loc = loc_ref[pl.ds(slab // per_row, 1), :]
     loc = pltpu.roll(loc, (LANES - (slab % per_row) * count) % LANES, 1)[:, :count]
     held = own_ref.shape[0]
     owner = loc // per_slab
-    chip = owner // 2
-    index = ((chip % near) * far + chip // near) * per_slab + loc % per_slab
-    mine = owner % 2 == core
+    ahead = lax.rem(owner // 2 - chip + chips, chips)
+    up = ahead <= chips // 2
+    hops = jnp.where(up, ahead, chips - ahead)
+    holder = jnp.where(up, 1, 0)
+    place = (hops % len(NEAR)) * len(FAR) + hops // len(NEAR)
+    index = (2 * place + jnp.where(owner % 2 == holder, 0, 1)) * per_slab + loc % per_slab
+    mine = holder == core
     row = lax.broadcasted_iota(jnp.int32, (held, count), 0)
     hit = row == index
     own_hot = jnp.where(hit & mine, 1.0, 0.0).astype(BF16)
@@ -472,27 +513,43 @@
     )(*in_vmem(loc_patch.reshape(-1, LANES), own, other))
 
 
+def swap_cores(array):
+    return lax.ppermute(array, "core", [(0, 1), (1, 0)])
+
+
+def onward(array, hops):
+    chips = lax.axis_size("chip")
+    pairs = [(2 * i, 2 * ((i + hops) % chips)) for i in range(chips)]
+    pairs += [(2 * i + 1, 2 * ((i - hops) % chips) + 1) for i in range(chips)]
+    return lax.ppermute(array, SLAB, pairs)
+
+
+def spread(images):
+    held = jnp.concatenate([images, swap_cores(images)])
+    for hops in (FAR, NEAR):
+        held = jnp.concatenate([held] + [onward(held, h) for h in hops[1:]])
+    return held
+
+
 def per_device(
     wavefields, courant, epsilon, anisotropy_delta, tilt_angle, loc_patch, slab_counts, angle_table
 ):
     slabs = lax.axis_size(SLAB)
+    assert FAR[-1] + NEAR[-1] >= slabs // 4
     per_slab = wavefields.shape[4] // wavefields.shape[3]
     params = (courant, epsilon, anisotropy_delta, tilt_angle)
     to_partner, to_neighbour = pack(wavefields, params)
-    partner = lax.ppermute(to_partner, "core", [(0, 1), (1, 0)])
+    partner = swap_cores(to_partner)
     pairs = [(i, i + 1) for i in range(1, slabs - 1, 2)]
     neighbour = lax.ppermute(to_neighbour, SLAB, pairs + [(j, i) for i, j in pairs])
     prepared = prepare(params, slab_counts, angle_table)
     images = images_of(wavefields, partner, neighbour, prepared, angle_table.shape[0])
-    own = lax.all_gather(lax.all_gather(images, "far", tiled=True), "near", tiled=True)
-    other = lax.ppermute(own, "core", [(0, 1), (1, 0)])
-    return pick(loc_patch, own, other, loc_patch.shape[0] // slabs, per_slab)
+    own = spread(images)
+    return pick(loc_patch, own, swap_cores(own), loc_patch.shape[0] // slabs, per_slab)
 
 
 def solution(mesh):
-    chips = mesh.shape["slab"] // 2
-    near = 4 if chips % 4 == 0 else 1
-    shape = (mesh.shape["groups"], chips // near, near, 2)
+    shape = (mesh.shape["groups"], mesh.shape["slab"] // 2, 2)
     finer = Mesh(mesh.devices.reshape(shape), GROUPS_SLAB)
     in_specs = (
         P(None, None, "groups", SLAB, None),

time: 66.3 us -> 55.1 us (0.83)
  blocking collectives: 32.1 us -> 0 us
  waiting for transfers between devices: 4.43 us -> 16.9 us
  starting transfers between devices: 15.9 us -> 25.4 us
  Pallas kernels: 13.5 us -> 12.1 us
    all_gather x2 -> x0, blocking collectives: 32.1 us -> none  [the longest x1 16.7 us: per_device(): lax.all_gather(images, 'far', tiled=True)]
    ppermute x2 -> x7, waiting for transfers between devices: 1.54 us -> 14 us  [the longest x4 11.1 us: onward(): return lax.ppermute(array, SLAB, pairs)]
    ppermute x2 -> x7, starting transfers between devices: 14 us -> 23.4 us  [the longest x4 12.4 us: onward(): return lax.ppermute(array, SLAB, pairs)]
    pallas_call x1, Pallas kernels: 9.57 us -> 8.15 us  [images_of(): pl.pallas_call(main_kernel, grid=(two,), in_specs=[VMEM_WHOLE] * len(args...]
  transfers between devices with their start and end apart: 3 -> 8, of which waited for: 2 -> 7; matrix products, arithmetic and copies ran while one was open for 0% -> 0% of each run, Pallas kernels for 2% -> 3%
where the time goes in v3:
time: 55.1 us; the launch traced here: 55 us
  starting transfers between devices  25.4 us (46%)
  waiting for transfers between devices  16.9 us (31%)
  Pallas kernels  12.1 us (22%)
    ppermute x4, starting transfers between devices, onward(): return lax.ppermute(array, SLAB, pairs)  12.4 us
    ppermute x4, waiting for transfers between devices, onward(): return lax.ppermute(array, SLAB, pairs)  11.1 us
    ppermute x3, starting transfers between devices, swap_cores(): return lax.ppermute(array, 'core', [(0, 1), (1, 0)])  11 us
    pallas_call x1, Pallas kernels, images_of(): pl.pallas_call(main_kernel, grid=(two,), in_specs=[VMEM_WHOLE] * len(args...  8.15 us
    ppermute x1, waiting for transfers between devices, per_device(): lax.ppermute(to_neighbour, SLAB, pairs + [(j, i) for i, j in pairs])  2.89 us
    ppermute x3, waiting for transfers between devices, swap_cores(): return lax.ppermute(array, 'core', [(0, 1), (1, 0)])  2.81 us
    ppermute x1, starting transfers between devices, per_device(): lax.ppermute(to_neighbour, SLAB, pairs + [(j, i) for i, j in pairs])  1.94 us
    pallas_call x1, Pallas kernels, prepare(): pl.pallas_call(prepare_kernel, in_specs=[pl.BlockSpec(memory_space=pltpu....  1.39 us
  transfers between devices with their start and end apart: 8, of which 7 were waited for; matrix products, arithmetic and copies ran while one was open for 0% of the time, Pallas kernels for 3%

profile of v3, /device:TPU:69, one launch (start us, length us, event | category | flops | bytes accessed | tf_op | source)
XLA Modules:
  0.0 55.0 jit_solution(6343556541126371688)
XLA Ops:
  0.0 0.0 copy-start.8
  0.0 0.0 copy-start.9
  0.0 0.0 copy-start.10
  0.0 0.0 copy-start.11
  0.1 0.0 copy-start.4
  0.1 0.0 copy-start.3
  0.1 0.0 copy-start.2
  0.1 1.2 %pack.1 = (bf16[128,512]{1,0:T(8,128)(2,1)S(1)}, bf16[128,512]{1,0:T(8,128)(2,1)S(1)}) custom-call(f32[2,4,2,128,512]{4,3,2,1,0:T(8,128)} %wave_ref.1, f32[2,4,2,128,512]{4,3,2,1,0:T(8,128)} %wave_ref.1, f32[128,512]{1,0:T(8,128)} %courant_ref.1, f32[128,512]{1,0:T(8,128)} %courant_ref.1, f32[128,512]{1,0:T(8,128)} %eps_ref.1, f32[128,512]{1,0:T(8,128)} %eps_ref.1, ...), custom_call_target="tpu_custom_call" | custom-call | tf_op jit(solution)/shard_map/pack/pallas_call | solution.py:162
  1.4 10.0 %collective-permute-start = (bf16[128,512]{1,0:T(8,128)(2,1)S(1)}, bf16[128,512]{1,0:T(8,128)(2,1)S(1)}, u32[]{:S(2)}, u32[]{:S(2)}) collective-permute-start(bf16[128,512]{1,0:T(8,128)(2,1)S(1)} %get-tuple-element.17), channel_id=1, source_target_pairs={{0,1},{1,0},{2,3},{3,2},{4,5},{5,4},{6,7},{7,6},{8,9},{9,8},{10,11... | collective-permute-start | bytes 393224 | tf_op jit(solution)/shard_map/ppermute | solution.py:517
  11.4 1.9 %collective-permute-start.1 = (bf16[128,512]{1,0:T(8,128)(2,1)S(1)}, bf16[128,512]{1,0:T(8,128)(2,1)S(1)}, u32[]{:S(2)}, u32[]{:S(2)}) collective-permute-start(bf16[128,512]{1,0:T(8,128)(2,1)S(1)} %get-tuple-element.18), channel_id=1, source_target_pairs={{1,2},{3,4},{5,6},{7,8},{9,10},{11,12},{13,14},{15,16},{17,18},{19... | collective-permute-start | bytes 393224 | tf_op jit(solution)/shard_map/ppermute | solution.py:544
  13.4 1.4 %prepare.1 = (f32[128,512]{1,0:T(8,128)S(1)}, f32[128,512]{1,0:T(8,128)S(1)}, f32[128,512]{1,0:T(8,128)S(1)}, f32[128,512]{1,0:T(8,128)S(1)}, f32[128,512]{1,0:T...) custom-call(s32[32]{0:T(128)S(1)} %copy-done.13, ...), custom_call_target="tpu_custom_call" | custom-call | tf_op jit(solution)/shard_map/prepare/pallas_call | solution.py:226
  14.8 0.0 collective-permute-done.partner_ref
  14.8 2.9 %collective-permute-done.1.neighbour_ref = bf16[128,512]{1,0:T(8,128)(2,1)S(1)} collective-permute-done((bf16[128,512]{1,0:T(8,128)(2,1)S(1)}, bf16[128,512]{1,0:T(8,128)(2,1)S(1)}, u32[]{:S(2)}, u32[]{:S(2)}) %collective-permute-start.1) | collective-permute-done | bytes 131104 | tf_op jit(solution)/shard_map/ppermute | solution.py:544
  17.7 0.0 copy-done.5
  17.8 0.0 copy-start.12
  17.8 8.1 %images.1 = bf16[4,4096]{1,0:T(4,128)(2,1)S(1)} custom-call(f32[2,4,2,128,512]{4,3,2,1,0:T(8,128)S(1)} %copy-done, bf16[128,512]{1,0:T(8,128)(2,1)S(1)} %collective-permute-done.partner_ref, bf16[128,512]{1,0:T(8,128)(2,1)S(1)} %collective-permute-done.1.neighbour_ref, f32[128,512]{1,0:T(8,128)S(1)} %get-tuple-element.19.mix_ref, ...), custom_call_target="tpu_custom_call" | custom-call | tf_op jit(solution)/shard_map/images/pallas_call | solution.py:465
  25.9 0.1 collective-permute-start.2
  26.1 1.2 %collective-permute-done.2 = bf16[4,4096]{1,0:T(4,128)(2,1)S(1)} collective-permute-done((bf16[4,4096]{1,0:T(4,128)(2,1)S(1)}, bf16[4,4096]{1,0:T(4,128)(2,1)S(1)}, u32[]{:S(2)}, u32[]{:S(2)}) %collective-permute-start.2) | collective-permute-done | bytes 32800 | tf_op jit(solution)/shard_map/ppermute | solution.py:517
  27.3 6.4 %collective-permute-start.4 = (bf16[8,4096]{1,0:T(8,128)(2,1)S(1)}, bf16[8,4096]{1,0:T(8,128)(2,1)S(1)}, u32[]{:S(2)}, u32[]{:S(2)}) collective-permute-start(bf16[8,4096]{1,0:T(8,128)(2,1)S(1)} %pad_maximum_fusion.1), channel_id=1, source_target_pairs={{0,12},{2,14},{4,16},{6,18},{8,20},{10,22},{12,24},{14,26},{16,28}... | collective-permute-start | bytes 196616 | tf_op jit(solution)/shard_map/ppermute | solution.py:524
  33.7 1.4 %collective-permute-start.3 = (bf16[8,4096]{1,0:T(8,128)(2,1)S(1)}, bf16[8,4096]{1,0:T(8,128)(2,1)S(1)}, u32[]{:S(2)}, u32[]{:S(2)}) collective-permute-start(bf16[8,4096]{1,0:T(8,128)(2,1)S(1)} %pad_maximum_fusion.1), channel_id=1, source_target_pairs={{0,6},{2,8},{4,10},{6,12},{8,14},{10,16},{12,18},{14,20},{16,22},{... | collective-permute-start | bytes 196616 | tf_op jit(solution)/shard_map/ppermute | solution.py:524
  35.1 4.4 %collective-permute-done.4 = bf16[8,4096]{1,0:T(8,128)(2,1)S(1)} collective-permute-done((bf16[8,4096]{1,0:T(8,128)(2,1)S(1)}, bf16[8,4096]{1,0:T(8,128)(2,1)S(1)}, u32[]{:S(2)}, u32[]{:S(2)}) %collective-permute-start.4) | collective-permute-done | bytes 65568 | tf_op jit(solution)/shard_map/ppermute | solution.py:524
  39.4 1.4 %collective-permute-done.3 = bf16[8,4096]{1,0:T(8,128)(2,1)S(1)} collective-permute-done((bf16[8,4096]{1,0:T(8,128)(2,1)S(1)}, bf16[8,4096]{1,0:T(8,128)(2,1)S(1)}, u32[]{:S(2)}, u32[]{:S(2)}) %collective-permute-start.3) | collective-permute-done | bytes 65568 | tf_op jit(solution)/shard_map/ppermute | solution.py:524
  40.8 0.1 pad_maximum_fusion
  40.9 4.6 %collective-permute-start.6 = (bf16[24,4096]{1,0:T(8,128)(2,1)S(1)}, bf16[24,4096]{1,0:T(8,128)(2,1)S(1)}, u32[]{:S(2)}, u32[]{:S(2)}) collective-permute-start(bf16[24,4096]{1,0:T(8,128)(2,1)S(1)} %pad_maximum_fusion), channel_id=1, source_target_pairs={{0,4},{2,6},{4,8},{6,10},{8,12},{10,14},{12,16},{14,18},{16,20},{1... | collective-permute-start | bytes 589832 | tf_op jit(solution)/shard_map/ppermute | solution.py:524
  45.5 0.0 collective-permute-start.5
  45.5 3.3 %collective-permute-done.6 = bf16[24,4096]{1,0:T(8,128)(2,1)S(1)} collective-permute-done((bf16[24,4096]{1,0:T(8,128)(2,1)S(1)}, bf16[24,4096]{1,0:T(8,128)(2,1)S(1)}, u32[]{:S(2)}, u32[]{:S(2)}) %collective-permute-start.6) | collective-permute-done | bytes 196640 | tf_op jit(solution)/shard_map/ppermute | solution.py:524
  48.8 2.1 %collective-permute-done.5 = bf16[24,4096]{1,0:T(8,128)(2,1)S(1)} collective-permute-done((bf16[24,4096]{1,0:T(8,128)(2,1)S(1)}, bf16[24,4096]{1,0:T(8,128)(2,1)S(1)}, u32[]{:S(2)}, u32[]{:S(2)}) %collective-permute-start.5) | collective-permute-done | bytes 196640 | tf_op jit(solution)/shard_map/ppermute | solution.py:524
  50.9 0.3 concatenate.13.refs_1_
  51.2 0.9 %collective-permute-start.7 = (bf16[72,4096]{1,0:T(8,128)(2,1)S(1)}, bf16[72,4096]{1,0:T(8,128)(2,1)S(1)}, u32[]{:S(2)}, u32[]{:S(2)}) collective-permute-start(bf16[72,4096]{1,0:T(8,128)(2,1)S(1)} %concatenate.13.refs_1_), channel_id=1, source_target_pairs={{0,1},{1,0},{2,3},{3,2},{4,5},{5,4},{6,7},{7,6},{8,9},{9,8},{10,11... | collective-permute-start | bytes 1769480 | tf_op jit(solution)/shard_map/ppermute | solution.py:517
  52.1 1.6 %collective-permute-done.7.refs_2_ = bf16[72,4096]{1,0:T(8,128)(2,1)S(1)} collective-permute-done((bf16[72,4096]{1,0:T(8,128)(2,1)S(1)}, bf16[72,4096]{1,0:T(8,128)(2,1)S(1)}, u32[]{:S(2)}, u32[]{:S(2)}) %collective-permute-start.7) | collective-permute-done | bytes 589856 | tf_op jit(solution)/shard_map/ppermute | solution.py:517
  53.7 0.0 copy-done.12
  53.7 1.3 %pick.1 = f32[32,4096]{1,0:T(8,128)} custom-call(s32[8,128]{1,0:T(8,128)S(1)} %bitcast.2, bf16[72,4096]{1,0:T(8,128)(2,1)S(1)} %concatenate.13.refs_1_, bf16[72,4096]{1,0:T(8,128)(2,1)S(1)} %collective-permute-done.7.refs_2_), custom_call_target="tpu_custom_call" | custom-call | tf_op jit(solution)/shard_map/pick/pallas_call | solution.py:507
  (21 shorter events, 0.1 us)
Async XLA Ops:
  0.0 17.7 %copy-start.5 = (bf16[288,144]{1,0:T(8,128)(2,1)S(1)}, bf16[288,144]{1,0:T(8,128)(2,1)}, u32[]{:S(2)}) copy-start(bf16[288,144]{1,0:T(8,128)(2,1)} %constant.14.clone.one_ref) | copy-start | bytes 248836
  0.0 17.7 %copy-start.6 = (bf16[256,256]{1,0:T(8,128)(2,1)S(1)}, bf16[256,256]{1,0:T(8,128)(2,1)}, u32[]{:S(2)}) copy-start(bf16[256,256]{1,0:T(8,128)(2,1)} %constant.19.clone.x_across_ref) | copy-start | bytes 393220
  0.0 17.7 %copy-start.7 = (bf16[256,256]{1,0:T(8,128)(2,1)S(1)}, bf16[256,256]{1,0:T(8,128)(2,1)}, u32[]{:S(2)}) copy-start(bf16[256,256]{1,0:T(8,128)(2,1)} %constant.18.clone.x_ref) | copy-start | bytes 393220
  0.0 17.7 %copy-start.8 = (bf16[256,256]{1,0:T(8,128)(2,1)S(1)}, bf16[256,256]{1,0:T(8,128)(2,1)}, u32[]{:S(2)}) copy-start(bf16[256,256]{1,0:T(8,128)(2,1)} %constant.17.clone.xx_across_ref) | copy-start | bytes 393220
  0.0 17.7 %copy-start.9 = (bf16[256,256]{1,0:T(8,128)(2,1)S(1)}, bf16[256,256]{1,0:T(8,128)(2,1)}, u32[]{:S(2)}) copy-start(bf16[256,256]{1,0:T(8,128)(2,1)} %constant.16.clone.xx_ref) | copy-start | bytes 393220
  0.0 17.7 %copy-start.10 = (bf16[256,144]{1,0:T(8,128)(2,1)S(1)}, bf16[256,144]{1,0:T(8,128)(2,1)}, u32[]{:S(2)}) copy-start(bf16[256,144]{1,0:T(8,128)(2,1)} %constant.15.clone.two_ref) | copy-start | bytes 221188
  0.0 17.7 %copy-start.11 = (bf16[128,384]{1,0:T(8,128)(2,1)S(1)}, bf16[128,384]{1,0:T(8,128)(2,1)}, u32[]{:S(2)}) copy-start(bf16[128,384]{1,0:T(8,128)(2,1)} %constant.20.clone.depth_ref) | copy-start | bytes 294916
  0.1 13.3 %copy-start.4 = (f32[128,512]{1,0:T(8,128)S(1)}, f32[128,512]{1,0:T(8,128)}, u32[]{:S(2)}) copy-start(f32[128,512]{1,0:T(8,128)} %tilt_ref.1) | copy-start | bytes 786436
  0.1 13.3 %copy-start.3 = (f32[128,512]{1,0:T(8,128)S(1)}, f32[128,512]{1,0:T(8,128)}, u32[]{:S(2)}) copy-start(f32[128,512]{1,0:T(8,128)} %delta_ref.1) | copy-start | bytes 786436
  0.1 13.3 %copy-start.2 = (f32[128,512]{1,0:T(8,128)S(1)}, f32[128,512]{1,0:T(8,128)}, u32[]{:S(2)}) copy-start(f32[128,512]{1,0:T(8,128)} %eps_ref.1) | copy-start | bytes 786436
  0.1 13.3 %copy-start.1 = (f32[128,512]{1,0:T(8,128)S(1)}, f32[128,512]{1,0:T(8,128)}, u32[]{:S(2)}) copy-start(f32[128,512]{1,0:T(8,128)} %courant_ref.1) | copy-start | bytes 786436
  0.1 17.6 %copy-start = (f32[2,4,2,128,512]{4,3,2,1,0:T(8,128)S(1)}, f32[2,4,2,128,512]{4,3,2,1,0:T(8,128)}, u32[]{:S(2)}) copy-start(f32[2,4,2,128,512]{4,3,2,1,0:T(8,128)} %wave_ref.1) | copy-start | bytes 12582916
  0.1 13.3 %copy-start.14 = (s32[64]{0:T(128)S(1)}, s32[64]{0:T(128)}, u32[]{:S(2)}) copy-start(s32[64]{0:T(128)} %param.22) | copy-start | bytes 772
  0.1 13.3 %copy-start.13 = (s32[32]{0:T(128)S(1)}, s32[32]{0:T(128)}, u32[]{:S(2)}) copy-start(s32[32]{0:T(128)} %counts_ref.1) | copy-start | bytes 388
  1.4 13.4 %collective-permute-start = (bf16[128,512]{1,0:T(8,128)(2,1)S(1)}, bf16[128,512]{1,0:T(8,128)(2,1)S(1)}, u32[]{:S(2)}, u32[]{:S(2)}) collective-permute-start(bf16[128,512]{1,0:T(8,128)(2,1)S(1)} %get-tuple-element.17), channel_id=1, source_target_pairs={{0,1},{1,0},{2,3},{3,2},{4,5},{5,4},{6,7},{7,6},{8,9},{9,8},{10,11... | collective-permute-start | bytes 393224 | tf_op jit(solution)/shard_map/ppermute | solution.py:517
  11.4 6.3 %collective-permute-start.1 = (bf16[128,512]{1,0:T(8,128)(2,1)S(1)}, bf16[128,512]{1,0:T(8,128)(2,1)S(1)}, u32[]{:S(2)}, u32[]{:S(2)}) collective-permute-start(bf16[128,512]{1,0:T(8,128)(2,1)S(1)} %get-tuple-element.18), channel_id=1, source_target_pairs={{1,2},{3,4},{5,6},{7,8},{9,10},{11,12},{13,14},{15,16},{17,18},{19... | collective-permute-start | bytes 393224 | tf_op jit(solution)/shard_map/ppermute | solution.py:544
  17.8 35.9 %copy-start.12 = (s32[1024]{0:T(1024)S(1)}, s32[1024]{0:T(1024)}, u32[]{:S(2)}) copy-start(s32[1024]{0:T(1024)} %param.20) | copy-start | bytes 12292
  25.9 1.3 %collective-permute-start.2 = (bf16[4,4096]{1,0:T(4,128)(2,1)S(1)}, bf16[4,4096]{1,0:T(4,128)(2,1)S(1)}, u32[]{:S(2)}, u32[]{:S(2)}) collective-permute-start(bf16[4,4096]{1,0:T(4,128)(2,1)S(1)} %images.1), channel_id=1, source_target_pairs={{0,1},{1,0},{2,3},{3,2},{4,5},{5,4},{6,7},{7,6},{8,9},{9,8},{10,11... | collective-permute-start | bytes 98312 | tf_op jit(solution)/shard_map/ppermute | solution.py:517
  27.3 12.2 %collective-permute-start.4 = (bf16[8,4096]{1,0:T(8,128)(2,1)S(1)}, bf16[8,4096]{1,0:T(8,128)(2,1)S(1)}, u32[]{:S(2)}, u32[]{:S(2)}) collective-permute-start(bf16[8,4096]{1,0:T(8,128)(2,1)S(1)} %pad_maximum_fusion.1), channel_id=1, source_target_pairs={{0,12},{2,14},{4,16},{6,18},{8,20},{10,22},{12,24},{14,26},{16,28}... | collective-permute-start | bytes 196616 | tf_op jit(solution)/shard_map/ppermute | solution.py:524
  33.7 7.1 %collective-permute-start.3 = (bf16[8,4096]{1,0:T(8,128)(2,1)S(1)}, bf16[8,4096]{1,0:T(8,128)(2,1)S(1)}, u32[]{:S(2)}, u32[]{:S(2)}) collective-permute-start(bf16[8,4096]{1,0:T(8,128)(2,1)S(1)} %pad_maximum_fusion.1), channel_id=1, source_target_pairs={{0,6},{2,8},{4,10},{6,12},{8,14},{10,16},{12,18},{14,20},{16,22},{... | collective-permute-start | bytes 196616 | tf_op jit(solution)/shard_map/ppermute | solution.py:524
  40.9 8.0 %collective-permute-start.6 = (bf16[24,4096]{1,0:T(8,128)(2,1)S(1)}, bf16[24,4096]{1,0:T(8,128)(2,1)S(1)}, u32[]{:S(2)}, u32[]{:S(2)}) collective-permute-start(bf16[24,4096]{1,0:T(8,128)(2,1)S(1)} %pad_maximum_fusion), channel_id=1, source_target_pairs={{0,4},{2,6},{4,8},{6,10},{8,12},{10,14},{12,16},{14,18},{16,20},{1... | collective-permute-start | bytes 589832 | tf_op jit(solution)/shard_map/ppermute | solution.py:524
  45.5 5.4 %collective-permute-start.5 = (bf16[24,4096]{1,0:T(8,128)(2,1)S(1)}, bf16[24,4096]{1,0:T(8,128)(2,1)S(1)}, u32[]{:S(2)}, u32[]{:S(2)}) collective-permute-start(bf16[24,4096]{1,0:T(8,128)(2,1)S(1)} %pad_maximum_fusion), channel_id=1, source_target_pairs={{0,2},{2,4},{4,6},{6,8},{8,10},{10,12},{12,14},{14,16},{16,18},{18... | collective-permute-start | bytes 589832 | tf_op jit(solution)/shard_map/ppermute | solution.py:524
  51.2 2.5 %collective-permute-start.7 = (bf16[72,4096]{1,0:T(8,128)(2,1)S(1)}, bf16[72,4096]{1,0:T(8,128)(2,1)S(1)}, u32[]{:S(2)}, u32[]{:S(2)}) collective-permute-start(bf16[72,4096]{1,0:T(8,128)(2,1)S(1)} %concatenate.13.refs_1_), channel_id=1, source_target_pairs={{0,1},{1,0},{2,3},{3,2},{4,5},{5,4},{6,7},{7,6},{8,9},{9,8},{10,11... | collective-permute-start | bytes 1769480 | tf_op jit(solution)/shard_map/ppermute | solution.py:517

commit v4 on v3

v4 whole, which is shorter than its diff:
```python
import math

import jax
import jax.numpy as jnp
import numpy as np
from jax import lax
from jax.experimental import pallas as pl
from jax.experimental.pallas import tpu as pltpu
from jax.sharding import Mesh
from jax.sharding import PartitionSpec as P

SLAB = ("chip", "core")
GROUPS_SLAB = ("groups", "chip", "core")
LANES = 128
HALF = 4
PITCH = 40
FAR, NEAR = ((0, 3, 6), (0, 1, 2))
SECOND = (-14336.0, 8064.0, -1008.0, 128.0, -9.0)
SECOND_REST = 14.0
SECOND_UNIT = 5040.0
FIRST = (672.0, -168.0, 32.0, -3.0)
FIRST_UNIT = 840.0
BF16 = jnp.bfloat16
F32 = jnp.float32
VMEM_WHOLE = pl.BlockSpec(memory_space=pltpu.VMEM)


def in_vmem(*arrays):
    return [pltpu.with_memory_space_constraint(a, pltpu.VMEM) for a in arrays]


def weight(kind, offset):
    if abs(offset) > HALF:
        return 0.0
    if kind == 2:
        return SECOND[abs(offset)]
    if offset == 0:
        return 0.0
    return FIRST[abs(offset) - 1] * (1.0 if offset > 0 else -1.0)


def band(kind, outputs, inputs):
    table = np.zeros((len(outputs), len(inputs)), np.float32)
    for i, o in enumerate(outputs):
        for j, n in enumerate(inputs):
            if o is not None and n is not None:
                table[i, j] = weight(kind, n - o)
    return table


def row_tables(rows):
    own = list(range(rows))
    inner = list(range(-HALF, 0)) + list(range(rows, rows + HALF))
    outer = list(range(-2 * HALF, -HALF)) + list(range(rows + HALF, rows + 2 * HALF))
    pad = [None] * 8
    ends = own[:8] + own[-8:]
    edge_in = ends + inner + outer + own[8:16] + own[-16:-8]
    edge_out = ends + inner + pad
    second_in = own + inner + pad
    tables = ((own, own), (edge_out, edge_in), (own, second_in))
    return [np.concatenate([band(2, o, i), band(1, o, i)]) for o, i in tables]


def column_tables(kind):
    block = list(range(2 * LANES))
    inside = band(kind, block, block).T
    across = np.zeros((2 * LANES, 2 * LANES), np.float32)
    for i in range(2 * LANES):
        for o in range(2 * LANES):
            if (i < LANES) != (o < LANES):
                across[i, o] = weight(kind, i - o)
    return inside, across


def depth_table(patch, bins):
    k = np.arange(bins)[:, None]
    z = np.arange(patch)[None, :]
    phase = (2.0 * math.pi / patch * np.mod(k * z, patch)).astype(np.float32)
    table = np.concatenate([np.cos(phase), -np.sin(phase)]).astype(np.float32) * np.float32(1.0 / math.sqrt(patch))
    return table.astype(np.float32)


def quarter_turns(quarter, cosine, sine):
    odd = (quarter & 1) == 1
    c = jnp.where(odd, sine, cosine)
    s = jnp.where(odd, cosine, sine)
    c = jnp.where(((quarter + 1) & 2) == 2, -c, c)
    s = jnp.where((quarter & 2) == 2, -s, s)
    return c, s


def small_cos_sin(y):
    y2 = y * y
    s = y * (1.0 + y2 * (-1.6666654611e-1 + y2 * (8.3321608736e-3 + y2 * -1.9515295891e-4)))
    c = 1.0 - 0.5 * y2 + y2 * y2 * (4.166664568298827e-2 + y2 * (-1.388731625493765e-3 + y2 * 2.443315711809948e-5))
    return c, s


def double_angle(theta):
    n = jnp.floor(theta * (4.0 / math.pi) + 0.5)
    y = 2.0 * theta - n * 1.5703125
    y = y - n * 4.837512969970703e-4
    y = y - n * 7.54978995489188216e-8
    c, s = small_cos_sin(y)
    return quarter_turns(n.astype(jnp.int32), c, s)


def pack_kernel(
    w_top, w_bot, c_top, c_bot, e_top, e_bot, d_top, d_bot, t_top, t_bot, partner_ref, neighbour_ref
):
    low = lax.broadcasted_iota(jnp.int32, (8, w_top.shape[-1]), 0) < HALF

    def half_turn(x):
        return pltpu.roll(x, HALF, 0)

    def emit(out, wave, params, upward):
        def join(a, b):
            return jnp.where(low, half_turn(a), b) if upward else jnp.where(low, a, half_turn(b))

        groups = []
        for w in range(wave.shape[0]):
            for s in range(wave.shape[2]):
                groups.append(wave[w, 0, s])
                groups.append(wave[w, 1, s])
                groups.append(join(wave[w, 2, s], wave[w, 3, s]))
        courant, eps, delta, tilt = (p[...] for p in params)
        high = tilt.astype(BF16).astype(F32)
        groups += [join(courant, eps), join(delta, high), tilt - high]
        groups.append(groups[-1])
        for g in range(0, len(groups), 2):
            out[8 * g : 8 * g + 16, :] = jnp.concatenate(groups[g : g + 2], axis=0).astype(BF16)

    tops = (w_top, (c_top, e_top, d_top, t_top))
    bottoms = (w_bot, (c_bot, e_bot, d_bot, t_bot))
    first = lax.axis_index("core") == 0

    @pl.when(first)
    def _():
        emit(partner_ref, *bottoms, True)
        emit(neighbour_ref, *tops, False)

    @pl.when(jnp.logical_not(first))
    def _():
        emit(partner_ref, *tops, False)
        emit(neighbour_ref, *bottoms, True)


def pack(wavefields, params):
    two, four, shots, rows, cols = wavefields.shape
    last = rows // 8 - 1
    groups = 2 * shots * 3 + 4
    wave_block = (two, four, shots, 8, cols)
    specs = [
        pl.BlockSpec(wave_block, lambda i: (0, 0, 0, 0, 0)),
        pl.BlockSpec(wave_block, lambda i: (0, 0, 0, last, 0)),
    ]
    args = [wavefields, wavefields]
    for p in params:
        specs += [pl.BlockSpec((8, cols), lambda i: (0, 0)), pl.BlockSpec((8, cols), lambda i: (last, 0))]
        args += [p, p]
    out = pltpu.VMEM((8 * groups, cols), BF16)
    return pl.pallas_call(
        pack_kernel,
        grid=(1,),
        in_specs=specs,
        out_specs=[VMEM_WHOLE] * 2,
        out_shape=[out, out],
        compiler_params=pltpu.CompilerParams(vmem_limit_bytes=8 << 20),
        name="pack",
    )(*(pltpu.with_memory_space_constraint(a, pltpu.HBM) for a in args))


def coefficients(courant, eps, delta, tilt):
    cosine, sine = double_angle(tilt)
    scaled = courant * (1.0 / SECOND_UNIT)
    return (
        0.5 + 0.5 * cosine,
        sine * (SECOND_UNIT / (FIRST_UNIT * FIRST_UNIT)),
        scaled * (1.0 + 2.0 * eps),
        scaled * jnp.sqrt(1.0 + 2.0 * delta),
        scaled,
    )


def along_columns(out, source, inside, across):
    out[:, LANES : 3 * LANES] = jnp.dot(source[:, LANES : 3 * LANES], across[...], preferred_element_type=F32)
    left = jnp.dot(source[:, : 2 * LANES], inside[...], preferred_element_type=F32)
    out[:, :LANES] = left[:, :LANES]
    out[:, LANES : 2 * LANES] += left[:, LANES:]
    right = jnp.dot(source[:, 2 * LANES :], inside[...], preferred_element_type=F32)
    out[:, 2 * LANES : 3 * LANES] += right[:, :LANES]
    out[:, 3 * LANES :] = right[:, LANES:]


def derive(field, slope, zz, xx, xz, table, columns, fields):
    count = table.shape[0] // 2
    for f in range(2):
        source = field[f]
        product = jnp.dot(table[count:, :], source, preferred_element_type=F32)
        slope[f * count : (f + 1) * count, :] = product.astype(BF16)
        zz[f * count : (f + 1) * count, :] = jnp.dot(table[:count, :], source, preferred_element_type=F32)
    along_columns(xx, fields, columns[0], columns[1])
    along_columns(xz, slope[...], columns[2], columns[3])


def tilted(f, value, zz, xx, xz, mix, twist):
    turn = mix * (xx - zz) - twist * xz
    rest = SECOND_REST * value
    return (zz + turn) - rest if f == 0 else (xx - turn) - rest


def early_kernel(
    counts_ref, wave_ref, courant_ref, eps_ref, delta_ref, tilt_ref, angle_ref, own_ref,
    xx_ref, xx_across_ref, x_ref, x_across_ref,
    mix_ref, twist_ref, a_ref, b_ref, c_ref, low_c, low_s, high_c, high_s, alive_ref, next_ref,
    field_ref, slope_ref, zz_ref, xx_out, xz_out,
):
    rows, cols = courant_ref.shape
    wavefields, _, shots = wave_ref.shape[:3]
    columns = (xx_ref, xx_across_ref, x_ref, x_across_ref)
    items = [(w, s) for w in range(wavefields) for s in range(shots)]

    def matmuls(i):
        w, s = items[i]
        k = i % 2
        for f in range(2):
            field_ref[k, f * rows : (f + 1) * rows, :] = wave_ref[w, f, s].astype(BF16)
        parts = [field_ref.at[k, f * rows : (f + 1) * rows, :][...] for f in range(2)]
        derive(
            parts, slope_ref.at[k], zz_ref.at[k], xx_out.at[k], xz_out.at[k], own_ref, columns,
            field_ref.at[k][...],
        )

    def advance(i):
        w, s = items[i]
        k = i % 2
        for r in range(8, rows - 8, 8):
            at = slice(r, r + 8)
            p, q, p0, q0 = (wave_ref[w, f, s, at, :] for f in range(4))
            mix, twist = (mix_ref[at, :], twist_ref[at, :])

            def operator(f, value):
                here = slice(f * rows + r, f * rows + r + 8)
                return tilted(f, value, zz_ref[k, here, :], xx_out[k, here, :], xz_out[k, here, :], mix, twist)

            across, along = (operator(0, p), operator(1, q))
            a, b, c = (a_ref[at, :], b_ref[at, :], c_ref[at, :])
            next_ref[i, 0, at, :] = (2.0 * p - p0) + (a * across + b * along)
            next_ref[i, 1, at, :] = (2.0 * q - q0) + (b * across + c * along)

    matmuls(0)
    for r in range(0, rows, 8):
        at = slice(r, r + 8)
        values = coefficients(courant_ref[at, :], eps_ref[at, :], delta_ref[at, :], tilt_ref[at, :])
        for ref, value in zip((mix_ref, twist_ref, a_ref, b_ref, c_ref), values, strict=True):
            ref[at, :] = value
    for i in range(1, len(items)):
        matmuls(i)
        advance(i - 1)
    slant_factors(angle_ref, low_c, low_s, high_c, high_s)
    advance(len(items) - 1)
    live = lax.broadcasted_iota(jnp.int32, (8, LANES), 0) < counts_ref[lax.axis_index(SLAB)]
    alive_ref[...] = jnp.where(live, 1.0, 0.0)


def slant_factors(angle_ref, low_c, low_s, high_c, high_s):
    right_half = lax.broadcasted_iota(jnp.int32, (LANES, LANES), 1) >= LANES // 2
    angles = jnp.concatenate([angle_ref[...], angle_ref[...]], axis=1)
    lateral = lax.broadcasted_iota(jnp.int32, (LANES, LANES), 0)
    modulus = 16 * LANES
    turn = (lateral * angles) & (modulus - 1)
    quarter = (turn + modulus // 8) >> int(math.log2(modulus // 4))
    rest = turn - quarter * (modulus // 4)
    c1, s1 = small_cos_sin(rest.astype(F32) * (2.0 * math.pi / modulus))
    c1, s1 = quarter_turns(quarter, c1, s1)

    def times(x, y):
        return (x[0] * y[0] - x[1] * y[1], x[0] * y[1] + x[1] * y[0])

    value = (jnp.ones_like(c1), jnp.zeros_like(c1))
    for j in range(8):
        low_c[j], low_s[j] = value
        value = (c1, s1) if j == 0 else times(value, (c1, s1))
    eighth = value
    scale = 1.0 / math.sqrt(LANES)
    value = (jnp.where(right_half, 0.0, scale), jnp.where(right_half, scale, 0.0))
    for j in range(8):
        high_c[j], high_s[j] = value
        value = times(value, eighth)


def late_kernel(
    wave_ref, partner_ref, neighbour_ref, mix_ref, twist_ref, a_ref, b_ref, c_ref,
    low_c, low_s, high_c, high_s, alive_ref, next_ref,
    edge_table_ref, two_ref, xx_ref, xx_across_ref, x_ref, x_across_ref, depth_ref,
    out_ref,
    edge_z, edge_x, edge_slope, edge_zz, edge_xx, edge_xz, edge_next,
    field_ref, slope_ref, zz_ref, xx_out, xz_out, split_ref, spectra_ref, image_ref,
):
    wavefields, _, shots, rows, cols = wave_ref.shape
    bins = rows // 2
    per_slab = cols // LANES
    columns = (xx_ref, xx_across_ref, x_ref, x_across_ref)
    items = [(w, s) for w in range(wavefields) for s in range(shots)]
    low = lax.broadcasted_iota(jnp.int32, (8, cols), 0) < HALF
    first = lax.axis_index("core") == 0
    coefficient_refs = (mix_ref, twist_ref, a_ref, b_ref, c_ref)

    def half_turn(x):
        return pltpu.roll(x, HALF, 0)

    def group(g):
        at = slice(8 * g, 8 * g + 8)
        a, b = (partner_ref[at, :].astype(F32), neighbour_ref[at, :].astype(F32))
        return jnp.where(first, b, a), jnp.where(first, a, b)

    def first_halves(g):
        u, d = group(g)
        return jnp.where(low, u, half_turn(d))

    def second_halves(g):
        u, d = group(g)
        return jnp.where(low, half_turn(u), d)

    tall = 32
    halos = []
    for i, (w, s) in enumerate(items):
        halo = []
        for f in range(2):
            u, d = group(3 * i + f)
            inner = jnp.where(low, half_turn(u), half_turn(d))
            outer = jnp.where(low, u, d)
            halo.append(inner)
            pieces = (
                wave_ref[w, f, s, 0:8, :], wave_ref[w, f, s, rows - 8 : rows, :], inner, outer,
                wave_ref[w, f, s, 8:16, :], wave_ref[w, f, s, rows - 16 : rows - 8, :],
            )
            for n in range(0, 6, 2):
                pair = jnp.concatenate(pieces[n : n + 2], axis=0).astype(BF16)
                edge_z[i, f, 8 * n : 8 * n + 16, :] = pair
                if n < 4:
                    at = (2 * i + f) * tall + 8 * n
                    edge_x[at : at + 16, :] = pair
        halo += [first_halves(3 * i + 2), second_halves(3 * i + 2)]
        halos.append(halo)
    for i in range(len(items)):
        for f in range(2):
            product = jnp.dot(edge_table_ref[...], edge_z[i, f], preferred_element_type=F32)
            at = (2 * i + f) * tall
            edge_zz[at : at + tall, :] = product[:tall]
            edge_slope[at : at + tall, :] = product[tall:].astype(BF16)
    along_columns(edge_xx, edge_x[...], xx_ref, xx_across_ref)
    along_columns(edge_xz, edge_slope[...], x_ref, x_across_ref)
    g = 3 * len(items)
    beyond = coefficients(
        first_halves(g), second_halves(g), first_halves(g + 1), second_halves(g + 1) + first_halves(g + 2)
    )

    def edge_advance(i):
        w, s = items[i]
        for n, r in enumerate((0, rows - 8, None)):
            if r is None:
                fields = halos[i]
                mix, twist, a, b, c = beyond
            else:
                at = slice(r, r + 8)
                fields = [wave_ref[w, f, s, at, :] for f in range(4)]
                mix, twist, a, b, c = (ref[at, :] for ref in coefficient_refs)
            p, q, p0, q0 = fields

            def operator(f, value):
                here = slice((2 * i + f) * tall + 8 * n, (2 * i + f) * tall + 8 * n + 8)
                return tilted(f, value, edge_zz[here, :], edge_xx[here, :], edge_xz[here, :], mix, twist)

            across, along = (operator(0, p), operator(1, q))
            edge_next[i, 0, 8 * n : 8 * n + 8, :] = (2.0 * p - p0) + (a * across + b * along)
            edge_next[i, 1, 8 * n : 8 * n + 8, :] = (2.0 * q - q0) + (b * across + c * along)

    def current(i, f, r):
        if r == 0:
            return edge_next[i, f, 0:8, :]
        if r == rows - 8:
            return edge_next[i, f, 8:16, :]
        return next_ref[i, f, r : r + 8, :]

    def matmuls(i):
        k = i % 2
        for f in range(2):
            for r in range(0, rows, 16):
                pair = jnp.concatenate([current(i, f, r), current(i, f, r + 8)], axis=0)
                pair = pair.astype(BF16)
                field_ref[k, f * rows + r : f * rows + r + 16, :] = pair
            edge = edge_next[i, f, 16:24, :]
            pair = jnp.concatenate([edge, jnp.zeros_like(edge)], axis=0).astype(BF16)
            field_ref[k, 2 * rows + 16 * f : 2 * rows + 16 * f + 16, :] = pair
        parts = [
            jnp.concatenate(
                [
                    field_ref[k, f * rows : (f + 1) * rows, :],
                    field_ref[k, 2 * rows + 16 * f : 2 * rows + 16 * f + 16, :],
                ],
                axis=0,
            )
            for f in range(2)
        ]
        derive(
            parts, slope_ref.at[k], zz_ref.at[k], xx_out.at[k], xz_out.at[k], two_ref, columns,
            field_ref[k, : 2 * rows, :],
        )

    def advance(i):
        w, s = items[i]
        k = i % 2
        for r in range(0, rows, 16):
            parts = []
            for h in (r, r + 8):
                at = slice(h, h + 8)
                mix, twist, a, b = (ref[at, :] for ref in coefficient_refs[:4])

                def operator(f, value):
                    here = slice(f * rows + h, f * rows + h + 8)
                    return tilted(
                        f, value, zz_ref[k, here, :], xx_out[k, here, :], xz_out[k, here, :], mix, twist
                    )

                p, q = (current(i, f, h) for f in range(2))
                across, along = (operator(0, p), operator(1, q))
                parts.append((2.0 * p - wave_ref[w, 0, s, at, :]) + (a * across + b * along))
            value = jnp.concatenate(parts, axis=0)
            top = value.astype(BF16)
            split_ref[k, r : r + 16, :] = top
            split_ref[k, rows + r : rows + r + 16, :] = (value - top.astype(F32)).astype(BF16)
            split_ref[k, 2 * rows + r : 2 * rows + r + 16, :] = top

    def transform(i):
        spectra = jnp.dot(depth_ref[...], split_ref[i % 2], preferred_element_type=F32)
        for part in range(2):
            for m in range(per_slab):
                start = 16 * part + per_slab * i + m
                spectra_ref[pl.ds(start, bins, stride=PITCH), :] = spectra[
                    part * bins : (part + 1) * bins, m * LANES : (m + 1) * LANES
                ]

    for i in range(len(items)):
        edge_advance(i)
    matmuls(0)
    for i in range(1, len(items)):
        matmuls(i)
        advance(i - 1)
        transform(i - 1)
    advance(len(items) - 1)
    transform(len(items) - 1)

    left_lane = lax.broadcasted_iota(jnp.int32, (8, LANES), 1) < LANES // 2
    alive = alive_ref[...]

    def some(j, carry):
        hc, hs = (high_c[j], high_s[j])
        pair = []
        for i in range(8):
            lc, ls = (low_c[i], low_s[i])
            real = (hc * lc - hs * ls).astype(BF16)
            imag = (hc * ls + hs * lc).astype(BF16)
            at = pl.multiple_of((8 * j + i) * PITCH, 8)
            left = jnp.concatenate(
                [spectra_ref[pl.ds(at, 16), :], spectra_ref[pl.ds(at + 16, 16), :]], axis=1
            ).astype(BF16)
            stack = jnp.dot(left, jnp.concatenate([real, imag], axis=0), preferred_element_type=F32)
            product = stack[:8] * stack[8:]
            pair.append(product + pltpu.roll(product, 4, 0))
            if i % 2 == 1:
                even, odd = pair
                even = even + pltpu.roll(even, LANES // 2, 1)
                odd = odd + pltpu.roll(odd, LANES // 2, 1)
                pair = []
                where_to = pl.multiple_of((4 * j + i // 2) * LANES, LANES)
                image_ref[:, pl.ds(where_to, LANES)] = alive * jnp.where(left_lane, even, odd)
        return carry

    lax.fori_loop(0, bins // 8, some, 0)
    out_ref[...] = image_ref[:per_slab, :].astype(BF16)


def column_operands():
    return [jnp.asarray(t, dtype=BF16) for kind in (2, 1) for t in column_tables(kind)]


def early(wavefields, params, slab_counts, angle_table):
    two, four, shots, rows, cols = wavefields.shape
    field = pltpu.VMEM((rows, cols), F32)
    table = pltpu.VMEM((8, LANES, LANES), F32)
    own = jnp.asarray(row_tables(rows)[0], dtype=BF16)
    args = [wavefields, *params, angle_table.reshape(1, -1), own, *column_operands()]
    outs = [field] * 5 + [table] * 4 + [
        pltpu.VMEM((8, LANES), F32),
        pltpu.VMEM((two * shots, 2, rows, cols), F32),
    ]
    return pl.pallas_call(
        early_kernel,
        in_specs=[pl.BlockSpec(memory_space=pltpu.SMEM)] + [VMEM_WHOLE] * len(args),
        out_specs=[VMEM_WHOLE] * len(outs),
        out_shape=outs,
        scratch_shapes=[
            pltpu.VMEM((2, 2 * rows, cols), BF16),
            pltpu.VMEM((2, 2 * rows, cols), BF16),
            pltpu.VMEM((2, 2 * rows, cols), F32),
            pltpu.VMEM((2, 2 * rows, cols), F32),
            pltpu.VMEM((2, 2 * rows, cols), F32),
        ],
        compiler_params=pltpu.CompilerParams(vmem_limit_bytes=24 << 20),
        name="early",
    )(slab_counts, *in_vmem(*args))


def late(wavefields, partner, neighbour, prepared, angles):
    two, four, shots, rows, cols = wavefields.shape
    bins = rows // 2
    per_slab = cols // rows
    items = two * shots
    _, edge, both = (jnp.asarray(t, dtype=BF16) for t in row_tables(rows))
    depth = depth_table(rows, bins)
    depth_top = depth.astype(jnp.bfloat16)
    depth_low = (depth - depth_top.astype(np.float32)).astype(jnp.bfloat16)
    depth = jnp.asarray(np.concatenate([depth_top, depth_top, depth_low], axis=1), dtype=BF16)
    args = [wavefields, partner, neighbour, *prepared, edge, both, *column_operands(), depth]
    out_shape = (per_slab, bins * angles)
    scratch = [
        pltpu.VMEM((items, 2, 48, cols), BF16),
        pltpu.VMEM((items * 2 * 32, cols), BF16),
        pltpu.VMEM((items * 2 * 32, cols), BF16),
        pltpu.VMEM((items * 2 * 32, cols), F32),
        pltpu.VMEM((items * 2 * 32, cols), F32),
        pltpu.VMEM((items * 2 * 32, cols), F32),
        pltpu.VMEM((items, 2, 24, cols), F32),
        pltpu.VMEM((2, 2 * (rows + 16), cols), BF16),
        pltpu.VMEM((2, 2 * rows, cols), BF16),
        pltpu.VMEM((2, 2 * rows, cols), F32),
        pltpu.VMEM((2, 2 * rows, cols), F32),
        pltpu.VMEM((2, 2 * rows, cols), F32),
        pltpu.VMEM((2, 3 * rows, cols), BF16),
        pltpu.VMEM((PITCH * bins, LANES), F32),
        pltpu.VMEM((8, bins * angles), F32),
    ]
    return pl.pallas_call(
        late_kernel,
        in_specs=[VMEM_WHOLE] * len(args),
        out_specs=VMEM_WHOLE,
        out_shape=pltpu.VMEM(out_shape, BF16),
        scratch_shapes=scratch,
        compiler_params=pltpu.CompilerParams(vmem_limit_bytes=32 << 20),
        name="late",
    )(*in_vmem(*args))


def pick_kernel(loc_ref, own_ref, other_ref, out_ref, *, per_slab):
    slab = lax.axis_index(SLAB)
    chip, core = (lax.axis_index("chip"), lax.axis_index("core"))
    chips = lax.axis_size("chip")
    count = out_ref.shape[0]
    per_row = LANES // count
    loc = loc_ref[pl.ds(slab // per_row, 1), :]
    loc = pltpu.roll(loc, (LANES - (slab % per_row) * count) % LANES, 1)[:, :count]
    held = own_ref.shape[0]
    owner = loc // per_slab
    ahead = lax.rem(owner // 2 - chip + chips, chips)
    up = ahead <= chips // 2
    hops = jnp.where(up, ahead, chips - ahead)
    holder = jnp.where(up, 1, 0)
    place = (hops % len(NEAR)) * len(FAR) + hops // len(NEAR)
    index = (2 * place + jnp.where(owner % 2 == holder, 0, 1)) * per_slab + loc % per_slab
    mine = holder == core
    row = lax.broadcasted_iota(jnp.int32, (held, count), 0)
    hit = row == index
    own_hot = jnp.where(hit & mine, 1.0, 0.0).astype(BF16)
    other_hot = jnp.where(hit & jnp.logical_not(mine), 1.0, 0.0).astype(BF16)

    def choose(hot, ref):
        return lax.dot_general(hot, ref[...], (((0,), (0,)), ((), ())), preferred_element_type=F32)

    out_ref[...] = choose(own_hot, own_ref) + choose(other_hot, other_ref)


def pick(loc_patch, own, other, count, per_slab):
    width = own.shape[1]
    return pl.pallas_call(
        lambda *refs: pick_kernel(*refs, per_slab=per_slab),
        in_specs=[VMEM_WHOLE] * 3,
        out_shape=jax.ShapeDtypeStruct((count, width), F32),
        compiler_params=pltpu.CompilerParams(vmem_limit_bytes=8 << 20),
        name="pick",
    )(*in_vmem(loc_patch.reshape(-1, LANES), own, other))


def swap_cores(array):
    return lax.ppermute(array, "core", [(0, 1), (1, 0)])


def onward(array, hops):
    chips = lax.axis_size("chip")
    pairs = [(2 * i, 2 * ((i + hops) % chips)) for i in range(chips)]
    pairs += [(2 * i + 1, 2 * ((i - hops) % chips) + 1) for i in range(chips)]
    return lax.ppermute(array, SLAB, pairs)


def spread(images):
    held = jnp.concatenate([images, swap_cores(images)])
    for hops in (FAR, NEAR):
        held = jnp.concatenate([held] + [onward(held, h) for h in hops[1:]])
    return held


def per_device(
    wavefields, courant, epsilon, anisotropy_delta, tilt_angle, loc_patch, slab_counts, angle_table
):
    slabs = lax.axis_size(SLAB)
    assert FAR[-1] + NEAR[-1] >= slabs // 4
    per_slab = wavefields.shape[4] // wavefields.shape[3]
    params = (courant, epsilon, anisotropy_delta, tilt_angle)
    to_partner, to_neighbour = pack(wavefields, params)
    partner = swap_cores(to_partner)
    pairs = [(i, i + 1) for i in range(1, slabs - 1, 2)]
    neighbour = lax.ppermute(to_neighbour, SLAB, pairs + [(j, i) for i, j in pairs])
    prepared = early(wavefields, params, slab_counts, angle_table)
    images = late(wavefields, partner, neighbour, prepared, angle_table.shape[0])
    own = spread(images)
    return pick(loc_patch, own, swap_cores(own), loc_patch.shape[0] // slabs, per_slab)


def solution(mesh):
    shape = (mesh.shape["groups"], mesh.shape["slab"] // 2, 2)
    finer = Mesh(mesh.devices.reshape(shape), GROUPS_SLAB)
    in_specs = (
        P(None, None, "groups", SLAB, None),
        P(SLAB, None),
        P(SLAB, None),
        P(SLAB, None),
        P(SLAB, None),
        P(),
        P(),
        P(),
    )
    out_specs = P(GROUPS_SLAB, None)
    return jax.shard_map(
        per_device, mesh=finer, in_specs=in_specs, out_specs=out_specs, check_vma=False
    )
```

time: 55.1 us -> 53.4 us (0.969)
  waiting for transfers between devices: 16.9 us -> 14.4 us
    ppermute x1, waiting for transfers between devices: 2.89 us -> 0.52 us  [per_device(): lax.ppermute(to_neighbour, SLAB, pairs + [(j, i) for i, j in pairs])]
    ppermute x4, starting transfers between devices: 12.4 us -> 13.6 us  [onward(): return lax.ppermute(array, SLAB, pairs)]
    ppermute x3, starting transfers between devices: 11 us -> 10.3 us  [swap_cores(): return lax.ppermute(array, 'core', [(0, 1), (1, 0)])]
  transfers between devices with their start and end apart: 8 -> 8, of which waited for: 7 -> 7; matrix products, arithmetic and copies ran while one was open for 0% -> 0% of each run, Pallas kernels for 3% -> 7%
where the time goes in v4:
time: 53.4 us; the launch traced here: 53.3 us
  starting transfers between devices  25.9 us (49%)
  waiting for transfers between devices  14.4 us (27%)
  Pallas kernels  12.4 us (23%)
    ppermute x4, starting transfers between devices, onward(): return lax.ppermute(array, SLAB, pairs)  13.6 us
    ppermute x4, waiting for transfers between devices, onward(): return lax.ppermute(array, SLAB, pairs)  10.8 us
    ppermute x3, starting transfers between devices, swap_cores(): return lax.ppermute(array, 'core', [(0, 1), (1, 0)])  10.3 us
    pallas_call x1, Pallas kernels, late(): pl.pallas_call(late_kernel, in_specs=[VMEM_WHOLE] * len(args), out_specs=...  6.15 us
    pallas_call x1, Pallas kernels, early(): pl.pallas_call(early_kernel, in_specs=[pl.BlockSpec(memory_space=pltpu.SM...  3.7 us
    ppermute x3, waiting for transfers between devices, swap_cores(): return lax.ppermute(array, 'core', [(0, 1), (1, 0)])  3.1 us
    ppermute x1, starting transfers between devices, per_device(): lax.ppermute(to_neighbour, SLAB, pairs + [(j, i) for i, j in pairs])  1.94 us
    pallas_call x1, Pallas kernels, pick(): pl.pallas_call(lambda *refs: pick_kernel(*refs, per_slab=per_slab), in_sp...  1.29 us
  transfers between devices with their start and end apart: 8, of which 7 were waited for; matrix products, arithmetic and copies ran while one was open for 0% of the time, Pallas kernels for 7%

profile of v4, /device:TPU:69, one launch (start us, length us, event | category | flops | bytes accessed | tf_op | source)
XLA Modules:
  0.0 53.3 jit_solution(9557686552329507147)
XLA Ops:
  0.0 0.0 copy-start.8
  0.0 0.0 copy-start.11
  0.0 0.0 copy-start
  0.0 0.0 copy-start.4
  0.1 0.0 copy-start.3
  0.1 1.2 %pack.1 = (bf16[128,512]{1,0:T(8,128)(2,1)S(1)}, bf16[128,512]{1,0:T(8,128)(2,1)S(1)}) custom-call(f32[2,4,2,128,512]{4,3,2,1,0:T(8,128)} %wave_ref.3, f32[2,4,2,128,512]{4,3,2,1,0:T(8,128)} %wave_ref.3, f32[128,512]{1,0:T(8,128)} %courant_ref.1, f32[128,512]{1,0:T(8,128)} %courant_ref.1, f32[128,512]{1,0:T(8,128)} %eps_ref.1, f32[128,512]{1,0:T(8,128)} %eps_ref.1, ...), custom_call_target="tpu_custom_call" | custom-call | tf_op jit(solution)/shard_map/pack/pallas_call | solution.py:162
  1.4 0.0 copy-start.9
  1.4 0.0 copy-start.10
  1.4 0.0 copy-start.12
  1.4 10.0 %collective-permute-start = (bf16[128,512]{1,0:T(8,128)(2,1)S(1)}, bf16[128,512]{1,0:T(8,128)(2,1)S(1)}, u32[]{:S(2)}, u32[]{:S(2)}) collective-permute-start(bf16[128,512]{1,0:T(8,128)(2,1)S(1)} %get-tuple-element.18), channel_id=1, source_target_pairs={{0,1},{1,0},{2,3},{3,2},{4,5},{5,4},{6,7},{7,6},{8,9},{9,8},{10,11... | collective-permute-start | bytes 393224 | tf_op jit(solution)/shard_map/ppermute | solution.py:595
  11.4 1.9 %collective-permute-start.1 = (bf16[128,512]{1,0:T(8,128)(2,1)S(1)}, bf16[128,512]{1,0:T(8,128)(2,1)S(1)}, u32[]{:S(2)}, u32[]{:S(2)}) collective-permute-start(bf16[128,512]{1,0:T(8,128)(2,1)S(1)} %get-tuple-element.19), channel_id=1, source_target_pairs={{1,2},{3,4},{5,6},{7,8},{9,10},{11,12},{13,14},{15,16},{17,18},{19... | collective-permute-start | bytes 393224 | tf_op jit(solution)/shard_map/ppermute | solution.py:622
  13.5 3.7 %early.1 = (f32[128,512]{1,0:T(8,128)S(1)}, f32[128,512]{1,0:T(8,128)S(1)}, f32[128,512]{1,0:T(8,128)S(1)}, f32[128,512]{1,0:T(8,128)S(1)}, f32[128,512]{1,0:T(8...) custom-call(s32[32]{0:T(128)S(1)} %copy-done.14, ...), custom_call_target="tpu_custom_call" | custom-call | tf_op jit(solution)/shard_map/early/pallas_call | solution.py:498
  17.2 0.0 collective-permute-done.partner_ref
  17.2 0.5 collective-permute-done.1.neighbour_ref
  17.7 0.0 copy-done.9
  17.7 0.0 copy-start.13
  17.7 6.1 %late.1 = bf16[4,4096]{1,0:T(4,128)(2,1)S(1)} custom-call(f32[2,4,2,128,512]{4,3,2,1,0:T(8,128)S(1)} %copy-done, bf16[128,512]{1,0:T(8,128)(2,1)S(1)} %collective-permute-done.partner_ref, bf16[128,512]{1,0:T(8,128)(2,1)S(1)} %collective-permute-done.1.neighbour_ref, f32[128,512]{1,0:T(8,128)S(1)} %get-tuple-element.20.mix_ref, ...), custom_call_target="tpu_custom_call" | custom-call | tf_op jit(solution)/shard_map/late/pallas_call | solution.py:544
  23.9 0.1 collective-permute-start.2
  24.0 1.2 %collective-permute-done.2 = bf16[4,4096]{1,0:T(4,128)(2,1)S(1)} collective-permute-done((bf16[4,4096]{1,0:T(4,128)(2,1)S(1)}, bf16[4,4096]{1,0:T(4,128)(2,1)S(1)}, u32[]{:S(2)}, u32[]{:S(2)}) %collective-permute-start.2) | collective-permute-done | bytes 32800 | tf_op jit(solution)/shard_map/ppermute | solution.py:595
  25.2 6.8 %collective-permute-start.4 = (bf16[8,4096]{1,0:T(8,128)(2,1)S(1)}, bf16[8,4096]{1,0:T(8,128)(2,1)S(1)}, u32[]{:S(2)}, u32[]{:S(2)}) collective-permute-start(bf16[8,4096]{1,0:T(8,128)(2,1)S(1)} %pad_maximum_fusion.1), channel_id=1, source_target_pairs={{0,12},{2,14},{4,16},{6,18},{8,20},{10,22},{12,24},{14,26},{16,28}... | collective-permute-start | bytes 196616 | tf_op jit(solution)/shard_map/ppermute | solution.py:602
  32.1 2.2 %collective-permute-start.3 = (bf16[8,4096]{1,0:T(8,128)(2,1)S(1)}, bf16[8,4096]{1,0:T(8,128)(2,1)S(1)}, u32[]{:S(2)}, u32[]{:S(2)}) collective-permute-start(bf16[8,4096]{1,0:T(8,128)(2,1)S(1)} %pad_maximum_fusion.1), channel_id=1, source_target_pairs={{0,6},{2,8},{4,10},{6,12},{8,14},{10,16},{12,18},{14,20},{16,22},{... | collective-permute-start | bytes 196616 | tf_op jit(solution)/shard_map/ppermute | solution.py:602
  34.3 3.7 %collective-permute-done.4 = bf16[8,4096]{1,0:T(8,128)(2,1)S(1)} collective-permute-done((bf16[8,4096]{1,0:T(8,128)(2,1)S(1)}, bf16[8,4096]{1,0:T(8,128)(2,1)S(1)}, u32[]{:S(2)}, u32[]{:S(2)}) %collective-permute-start.4) | collective-permute-done | bytes 65568 | tf_op jit(solution)/shard_map/ppermute | solution.py:602
  38.0 1.1 %collective-permute-done.3 = bf16[8,4096]{1,0:T(8,128)(2,1)S(1)} collective-permute-done((bf16[8,4096]{1,0:T(8,128)(2,1)S(1)}, bf16[8,4096]{1,0:T(8,128)(2,1)S(1)}, u32[]{:S(2)}, u32[]{:S(2)}) %collective-permute-start.3) | collective-permute-done | bytes 65568 | tf_op jit(solution)/shard_map/ppermute | solution.py:602
  39.1 0.1 pad_maximum_fusion
  39.1 4.1 %collective-permute-start.6 = (bf16[24,4096]{1,0:T(8,128)(2,1)S(1)}, bf16[24,4096]{1,0:T(8,128)(2,1)S(1)}, u32[]{:S(2)}, u32[]{:S(2)}) collective-permute-start(bf16[24,4096]{1,0:T(8,128)(2,1)S(1)} %pad_maximum_fusion), channel_id=1, source_target_pairs={{0,4},{2,6},{4,8},{6,10},{8,12},{10,14},{12,16},{14,18},{16,20},{1... | collective-permute-start | bytes 589832 | tf_op jit(solution)/shard_map/ppermute | solution.py:602
  43.3 0.4 collective-permute-start.5
  43.7 3.9 %collective-permute-done.6 = bf16[24,4096]{1,0:T(8,128)(2,1)S(1)} collective-permute-done((bf16[24,4096]{1,0:T(8,128)(2,1)S(1)}, bf16[24,4096]{1,0:T(8,128)(2,1)S(1)}, u32[]{:S(2)}, u32[]{:S(2)}) %collective-permute-start.6) | collective-permute-done | bytes 196640 | tf_op jit(solution)/shard_map/ppermute | solution.py:602
  47.6 2.1 %collective-permute-done.5 = bf16[24,4096]{1,0:T(8,128)(2,1)S(1)} collective-permute-done((bf16[24,4096]{1,0:T(8,128)(2,1)S(1)}, bf16[24,4096]{1,0:T(8,128)(2,1)S(1)}, u32[]{:S(2)}, u32[]{:S(2)}) %collective-permute-start.5) | collective-permute-done | bytes 196640 | tf_op jit(solution)/shard_map/ppermute | solution.py:602
  49.7 0.2 concatenate.13.refs_1_
  49.9 0.2 collective-permute-start.7
  50.1 1.9 %collective-permute-done.7.refs_2_ = bf16[72,4096]{1,0:T(8,128)(2,1)S(1)} collective-permute-done((bf16[72,4096]{1,0:T(8,128)(2,1)S(1)}, bf16[72,4096]{1,0:T(8,128)(2,1)S(1)}, u32[]{:S(2)}, u32[]{:S(2)}) %collective-permute-start.7) | collective-permute-done | bytes 589856 | tf_op jit(solution)/shard_map/ppermute | solution.py:595
  52.1 1.3 %pick.1 = f32[32,4096]{1,0:T(8,128)} custom-call(s32[8,128]{1,0:T(8,128)S(1)} %bitcast.2, bf16[72,4096]{1,0:T(8,128)(2,1)S(1)} %concatenate.13.refs_1_, bf16[72,4096]{1,0:T(8,128)(2,1)S(1)} %collective-permute-done.7.refs_2_), custom_call_target="tpu_custom_call" | custom-call | tf_op jit(solution)/shard_map/pick/pallas_call | solution.py:585
  (23 shorter events, 0.1 us)
Async XLA Ops:
  0.0 13.4 %copy-start.5 = (bf16[256,256]{1,0:T(8,128)(2,1)S(1)}, bf16[256,256]{1,0:T(8,128)(2,1)}, u32[]{:S(2)}) copy-start(bf16[256,256]{1,0:T(8,128)(2,1)} %constant.20.clone.x_across_ref) | copy-start | bytes 393220
  0.0 13.4 %copy-start.6 = (bf16[256,256]{1,0:T(8,128)(2,1)S(1)}, bf16[256,256]{1,0:T(8,128)(2,1)}, u32[]{:S(2)}) copy-start(bf16[256,256]{1,0:T(8,128)(2,1)} %constant.19.clone.x_ref) | copy-start | bytes 393220
  0.0 13.4 %copy-start.7 = (bf16[256,256]{1,0:T(8,128)(2,1)S(1)}, bf16[256,256]{1,0:T(8,128)(2,1)}, u32[]{:S(2)}) copy-start(bf16[256,256]{1,0:T(8,128)(2,1)} %constant.18.clone.xx_across_ref) | copy-start | bytes 393220
  0.0 13.4 %copy-start.8 = (bf16[256,256]{1,0:T(8,128)(2,1)S(1)}, bf16[256,256]{1,0:T(8,128)(2,1)}, u32[]{:S(2)}) copy-start(bf16[256,256]{1,0:T(8,128)(2,1)} %constant.17.clone.xx_ref) | copy-start | bytes 393220
  0.0 13.4 %copy-start.11 = (bf16[256,128]{1,0:T(8,128)(2,1)S(1)}, bf16[256,128]{1,0:T(8,128)(2,1)}, u32[]{:S(2)}) copy-start(bf16[256,128]{1,0:T(8,128)(2,1)} %constant.16.clone.own_ref) | copy-start | bytes 196612
  0.0 13.4 %copy-start = (f32[2,4,2,128,512]{4,3,2,1,0:T(8,128)S(1)}, f32[2,4,2,128,512]{4,3,2,1,0:T(8,128)}, u32[]{:S(2)}) copy-start(f32[2,4,2,128,512]{4,3,2,1,0:T(8,128)} %wave_ref.3) | copy-start | bytes 12582916
  0.0 13.4 %copy-start.4 = (f32[128,512]{1,0:T(8,128)S(1)}, f32[128,512]{1,0:T(8,128)}, u32[]{:S(2)}) copy-start(f32[128,512]{1,0:T(8,128)} %tilt_ref.1) | copy-start | bytes 786436
  0.1 13.4 %copy-start.3 = (f32[128,512]{1,0:T(8,128)S(1)}, f32[128,512]{1,0:T(8,128)}, u32[]{:S(2)}) copy-start(f32[128,512]{1,0:T(8,128)} %delta_ref.1) | copy-start | bytes 786436
  0.1 13.4 %copy-start.2 = (f32[128,512]{1,0:T(8,128)S(1)}, f32[128,512]{1,0:T(8,128)}, u32[]{:S(2)}) copy-start(f32[128,512]{1,0:T(8,128)} %eps_ref.1) | copy-start | bytes 786436
  0.1 13.4 %copy-start.1 = (f32[128,512]{1,0:T(8,128)S(1)}, f32[128,512]{1,0:T(8,128)}, u32[]{:S(2)}) copy-start(f32[128,512]{1,0:T(8,128)} %courant_ref.1) | copy-start | bytes 786436
  0.1 13.4 %copy-start.15 = (s32[64]{0:T(128)S(1)}, s32[64]{0:T(128)}, u32[]{:S(2)}) copy-start(s32[64]{0:T(128)} %param.27) | copy-start | bytes 772
  0.1 13.4 %copy-start.14 = (s32[32]{0:T(128)S(1)}, s32[32]{0:T(128)}, u32[]{:S(2)}) copy-start(s32[32]{0:T(128)} %counts_ref.1) | copy-start | bytes 388
  1.4 16.4 %copy-start.9 = (bf16[256,144]{1,0:T(8,128)(2,1)S(1)}, bf16[256,144]{1,0:T(8,128)(2,1)}, u32[]{:S(2)}) copy-start(bf16[256,144]{1,0:T(8,128)(2,1)} %constant.22.clone.two_ref) | copy-start | bytes 221188
  1.4 16.3 %copy-start.10 = (bf16[128,384]{1,0:T(8,128)(2,1)S(1)}, bf16[128,384]{1,0:T(8,128)(2,1)}, u32[]{:S(2)}) copy-start(bf16[128,384]{1,0:T(8,128)(2,1)} %constant.23.clone.depth_ref) | copy-start | bytes 294916
  1.4 16.3 %copy-start.12 = (bf16[64,48]{1,0:T(8,128)(2,1)S(1)}, bf16[64,48]{1,0:T(8,128)(2,1)}, u32[]{:S(2)}) copy-start(bf16[64,48]{1,0:T(8,128)(2,1)} %constant.21.clone.edge_table_ref) | copy-start | bytes 18436
  1.4 15.8 %collective-permute-start = (bf16[128,512]{1,0:T(8,128)(2,1)S(1)}, bf16[128,512]{1,0:T(8,128)(2,1)S(1)}, u32[]{:S(2)}, u32[]{:S(2)}) collective-permute-start(bf16[128,512]{1,0:T(8,128)(2,1)S(1)} %get-tuple-element.18), channel_id=1, source_target_pairs={{0,1},{1,0},{2,3},{3,2},{4,5},{5,4},{6,7},{7,6},{8,9},{9,8},{10,11... | collective-permute-start | bytes 393224 | tf_op jit(solution)/shard_map/ppermute | solution.py:595
  11.4 6.3 %collective-permute-start.1 = (bf16[128,512]{1,0:T(8,128)(2,1)S(1)}, bf16[128,512]{1,0:T(8,128)(2,1)S(1)}, u32[]{:S(2)}, u32[]{:S(2)}) collective-permute-start(bf16[128,512]{1,0:T(8,128)(2,1)S(1)} %get-tuple-element.19), channel_id=1, source_target_pairs={{1,2},{3,4},{5,6},{7,8},{9,10},{11,12},{13,14},{15,16},{17,18},{19... | collective-permute-start | bytes 393224 | tf_op jit(solution)/shard_map/ppermute | solution.py:622
  17.7 34.3 %copy-start.13 = (s32[1024]{0:T(1024)S(1)}, s32[1024]{0:T(1024)}, u32[]{:S(2)}) copy-start(s32[1024]{0:T(1024)} %param.25) | copy-start | bytes 12292
  23.9 1.3 %collective-permute-start.2 = (bf16[4,4096]{1,0:T(4,128)(2,1)S(1)}, bf16[4,4096]{1,0:T(4,128)(2,1)S(1)}, u32[]{:S(2)}, u32[]{:S(2)}) collective-permute-start(bf16[4,4096]{1,0:T(4,128)(2,1)S(1)} %late.1), channel_id=1, source_target_pairs={{0,1},{1,0},{2,3},{3,2},{4,5},{5,4},{6,7},{7,6},{8,9},{9,8},{10,11... | collective-permute-start | bytes 98312 | tf_op jit(solution)/shard_map/ppermute | solution.py:595
  25.2 12.7 %collective-permute-start.4 = (bf16[8,4096]{1,0:T(8,128)(2,1)S(1)}, bf16[8,4096]{1,0:T(8,128)(2,1)S(1)}, u32[]{:S(2)}, u32[]{:S(2)}) collective-permute-start(bf16[8,4096]{1,0:T(8,128)(2,1)S(1)} %pad_maximum_fusion.1), channel_id=1, source_target_pairs={{0,12},{2,14},{4,16},{6,18},{8,20},{10,22},{12,24},{14,26},{16,28}... | collective-permute-start | bytes 196616 | tf_op jit(solution)/shard_map/ppermute | solution.py:602
  32.1 7.0 %collective-permute-start.3 = (bf16[8,4096]{1,0:T(8,128)(2,1)S(1)}, bf16[8,4096]{1,0:T(8,128)(2,1)S(1)}, u32[]{:S(2)}, u32[]{:S(2)}) collective-permute-start(bf16[8,4096]{1,0:T(8,128)(2,1)S(1)} %pad_maximum_fusion.1), channel_id=1, source_target_pairs={{0,6},{2,8},{4,10},{6,12},{8,14},{10,16},{12,18},{14,20},{16,22},{... | collective-permute-start | bytes 196616 | tf_op jit(solution)/shard_map/ppermute | solution.py:602
  39.1 8.4 %collective-permute-start.6 = (bf16[24,4096]{1,0:T(8,128)(2,1)S(1)}, bf16[24,4096]{1,0:T(8,128)(2,1)S(1)}, u32[]{:S(2)}, u32[]{:S(2)}) collective-permute-start(bf16[24,4096]{1,0:T(8,128)(2,1)S(1)} %pad_maximum_fusion), channel_id=1, source_target_pairs={{0,4},{2,6},{4,8},{6,10},{8,12},{10,14},{12,16},{14,18},{16,20},{1... | collective-permute-start | bytes 589832 | tf_op jit(solution)/shard_map/ppermute | solution.py:602
  43.3 6.4 %collective-permute-start.5 = (bf16[24,4096]{1,0:T(8,128)(2,1)S(1)}, bf16[24,4096]{1,0:T(8,128)(2,1)S(1)}, u32[]{:S(2)}, u32[]{:S(2)}) collective-permute-start(bf16[24,4096]{1,0:T(8,128)(2,1)S(1)} %pad_maximum_fusion), channel_id=1, source_target_pairs={{0,2},{2,4},{4,6},{6,8},{8,10},{10,12},{12,14},{14,16},{16,18},{18... | collective-permute-start | bytes 589832 | tf_op jit(solution)/shard_map/ppermute | solution.py:602
  49.9 2.1 %collective-permute-start.7 = (bf16[72,4096]{1,0:T(8,128)(2,1)S(1)}, bf16[72,4096]{1,0:T(8,128)(2,1)S(1)}, u32[]{:S(2)}, u32[]{:S(2)}) collective-permute-start(bf16[72,4096]{1,0:T(8,128)(2,1)S(1)} %concatenate.13.refs_1_), channel_id=1, source_target_pairs={{0,1},{1,0},{2,3},{3,2},{4,5},{5,4},{6,7},{7,6},{8,9},{9,8},{10,11... | collective-permute-start | bytes 1769480 | tf_op jit(solution)/shard_map/ppermute | solution.py:595

commit v5 on v4

--- a/solution.py
+++ b/solution.py
@@ -13,6 +13,7 @@
 GROUPS_SLAB = ("groups", "chip", "core")
 LANES = 128
 HALF = 4
+RUN = 8
 PITCH = 40
 FAR, NEAR = ((0, 3, 6), (0, 1, 2))
 SECOND = (-14336.0, 8064.0, -1008.0, 128.0, -9.0)
@@ -173,11 +174,12 @@
 def coefficients(courant, eps, delta, tilt):
     cosine, sine = double_angle(tilt)
     scaled = courant * (1.0 / SECOND_UNIT)
+    stretch = 1.0 + 2.0 * delta
     return (
         0.5 + 0.5 * cosine,
         sine * (SECOND_UNIT / (FIRST_UNIT * FIRST_UNIT)),
         scaled * (1.0 + 2.0 * eps),
-        scaled * jnp.sqrt(1.0 + 2.0 * delta),
+        scaled * (stretch * lax.rsqrt(stretch)),
         scaled,
     )
 
@@ -277,16 +279,15 @@
     def times(x, y):
         return (x[0] * y[0] - x[1] * y[1], x[0] * y[1] + x[1] * y[0])
 
-    value = (jnp.ones_like(c1), jnp.zeros_like(c1))
-    for j in range(8):
-        low_c[j], low_s[j] = value
-        value = (c1, s1) if j == 0 else times(value, (c1, s1))
-    eighth = value
+    low_c[...], low_s[...] = (c1, s1)
+    stride = (c1, s1)
+    for _ in range(int(math.log2(RUN))):
+        stride = times(stride, stride)
     scale = 1.0 / math.sqrt(LANES)
     value = (jnp.where(right_half, 0.0, scale), jnp.where(right_half, scale, 0.0))
-    for j in range(8):
+    for j in range(high_c.shape[0]):
         high_c[j], high_s[j] = value
-        value = times(value, eighth)
+        value = times(value, stride)
 
 
 def late_kernel(
@@ -295,7 +296,7 @@
     edge_table_ref, two_ref, xx_ref, xx_across_ref, x_ref, x_across_ref, depth_ref,
     out_ref,
     edge_z, edge_x, edge_slope, edge_zz, edge_xx, edge_xz, edge_next,
-    field_ref, slope_ref, zz_ref, xx_out, xz_out, split_ref, spectra_ref, image_ref,
+    field_ref, slope_ref, zz_ref, xx_out, xz_out, split_ref, spectra_ref, image_ref, slant_ref,
 ):
     wavefields, _, shots, rows, cols = wave_ref.shape
     bins = rows // 2
@@ -453,19 +454,25 @@
 
     left_lane = lax.broadcasted_iota(jnp.int32, (8, LANES), 1) < LANES // 2
     alive = alive_ref[...]
-
-    def some(j, carry):
-        hc, hs = (high_c[j], high_s[j])
+    for j in range(bins // RUN):
+        slot = j % 2
+        for r in range(0, LANES, 16):
+            at = slice(r, r + 16)
+            one = (low_c[at, :], low_s[at, :])
+            back = (high_c[j, at, :], high_s[j, at, :])
+            here = (back[0] * one[0] - back[1] * one[1], back[0] * one[1] + back[1] * one[0])
+            twice = 2.0 * one[0]
+            for i in range(RUN):
+                slant_ref[slot, i, at, :] = back[0].astype(BF16)
+                slant_ref[slot, i, LANES + r : LANES + r + 16, :] = back[1].astype(BF16)
+                back, here = here, tuple(twice * x - y for x, y in zip(here, back, strict=True))
         pair = []
-        for i in range(8):
-            lc, ls = (low_c[i], low_s[i])
-            real = (hc * lc - hs * ls).astype(BF16)
-            imag = (hc * ls + hs * lc).astype(BF16)
-            at = pl.multiple_of((8 * j + i) * PITCH, 8)
+        for i in range(RUN):
+            at = (RUN * j + i) * PITCH
             left = jnp.concatenate(
-                [spectra_ref[pl.ds(at, 16), :], spectra_ref[pl.ds(at + 16, 16), :]], axis=1
+                [spectra_ref[at : at + 16, :], spectra_ref[at + 16 : at + 32, :]], axis=1
             ).astype(BF16)
-            stack = jnp.dot(left, jnp.concatenate([real, imag], axis=0), preferred_element_type=F32)
+            stack = jnp.dot(left, slant_ref[slot, i], preferred_element_type=F32)
             product = stack[:8] * stack[8:]
             pair.append(product + pltpu.roll(product, 4, 0))
             if i % 2 == 1:
@@ -473,11 +480,8 @@
                 even = even + pltpu.roll(even, LANES // 2, 1)
                 odd = odd + pltpu.roll(odd, LANES // 2, 1)
                 pair = []
-                where_to = pl.multiple_of((4 * j + i // 2) * LANES, LANES)
-                image_ref[:, pl.ds(where_to, LANES)] = alive * jnp.where(left_lane, even, odd)
-        return carry
-
-    lax.fori_loop(0, bins // 8, some, 0)
+                where_to = (RUN * j + i) // 2 * LANES
+                image_ref[:, where_to : where_to + LANES] = alive * jnp.where(left_lane, even, odd)
     out_ref[...] = image_ref[:per_slab, :].astype(BF16)
 
 
@@ -488,10 +492,10 @@
 def early(wavefields, params, slab_counts, angle_table):
     two, four, shots, rows, cols = wavefields.shape
     field = pltpu.VMEM((rows, cols), F32)
-    table = pltpu.VMEM((8, LANES, LANES), F32)
+    table = pltpu.VMEM((rows // 2 // RUN, LANES, LANES), F32)
     own = jnp.asarray(row_tables(rows)[0], dtype=BF16)
     args = [wavefields, *params, angle_table.reshape(1, -1), own, *column_operands()]
-    outs = [field] * 5 + [table] * 4 + [
+    outs = [field] * 5 + [pltpu.VMEM((LANES, LANES), F32)] * 2 + [table] * 2 + [
         pltpu.VMEM((8, LANES), F32),
         pltpu.VMEM((two * shots, 2, rows, cols), F32),
     ]
@@ -540,6 +544,7 @@
         pltpu.VMEM((2, 3 * rows, cols), BF16),
         pltpu.VMEM((PITCH * bins, LANES), F32),
         pltpu.VMEM((8, bins * angles), F32),
+        pltpu.VMEM((2, RUN, 2 * LANES, LANES), BF16),
     ]
     return pl.pallas_call(
         late_kernel,
@@ -552,43 +557,46 @@
     )(*in_vmem(*args))
 
 
-def pick_kernel(loc_ref, own_ref, other_ref, out_ref, *, per_slab):
+def pick_kernel(loc_ref, *refs, per_slab):
+    held_refs, (mine_ref, theirs_ref) = (refs[:-2], refs[-2:])
     slab = lax.axis_index(SLAB)
     chip, core = (lax.axis_index("chip"), lax.axis_index("core"))
     chips = lax.axis_size("chip")
-    count = out_ref.shape[0]
+    count = mine_ref.shape[0]
     per_row = LANES // count
-    loc = loc_ref[pl.ds(slab // per_row, 1), :]
-    loc = pltpu.roll(loc, (LANES - (slab % per_row) * count) % LANES, 1)[:, :count]
-    held = own_ref.shape[0]
+    row = loc_ref[pl.ds(slab // per_row, 1), :]
+    spot = slab % per_row
+    partner = spot + 1 - 2 * core
+    loc = jnp.concatenate(
+        [pltpu.roll(row, (LANES - s * count) % LANES, 1)[:, :count] for s in (spot, partner)], axis=1
+    )
     owner = loc // per_slab
     ahead = lax.rem(owner // 2 - chip + chips, chips)
     up = ahead <= chips // 2
     hops = jnp.where(up, ahead, chips - ahead)
     holder = jnp.where(up, 1, 0)
-    place = (hops % len(NEAR)) * len(FAR) + hops // len(NEAR)
-    index = (2 * place + jnp.where(owner % 2 == holder, 0, 1)) * per_slab + loc % per_slab
-    mine = holder == core
-    row = lax.broadcasted_iota(jnp.int32, (held, count), 0)
-    hit = row == index
-    own_hot = jnp.where(hit & mine, 1.0, 0.0).astype(BF16)
-    other_hot = jnp.where(hit & jnp.logical_not(mine), 1.0, 0.0).astype(BF16)
-
-    def choose(hot, ref):
-        return lax.dot_general(hot, ref[...], (((0,), (0,)), ((), ())), preferred_element_type=F32)
-
-    out_ref[...] = choose(own_hot, own_ref) + choose(other_hot, other_ref)
-
-
-def pick(loc_patch, own, other, count, per_slab):
-    width = own.shape[1]
+    index = (2 * (hops // len(NEAR)) + jnp.where(owner % 2 == holder, 0, 1)) * per_slab + loc % per_slab
+    total = None
+    for near, ref in enumerate(held_refs):
+        held = lax.broadcasted_iota(jnp.int32, (ref.shape[0], 2 * count), 0)
+        hit = (held == index) & (holder == core) & (hops % len(NEAR) == near)
+        hot = jnp.where(hit, 1.0, 0.0).astype(BF16)
+        part = lax.dot_general(hot, ref[...], (((0,), (0,)), ((), ())), preferred_element_type=F32)
+        total = part if total is None else total + part
+    mine_ref[...] = total[:count]
+    theirs_ref[...] = total[count:].astype(BF16)
+
+
+def pick(loc_patch, held, count, per_slab):
+    width = held[0].shape[1]
     return pl.pallas_call(
         lambda *refs: pick_kernel(*refs, per_slab=per_slab),
-        in_specs=[VMEM_WHOLE] * 3,
-        out_shape=jax.ShapeDtypeStruct((count, width), F32),
+        in_specs=[VMEM_WHOLE] * (1 + len(held)),
+        out_specs=[VMEM_WHOLE] * 2,
+        out_shape=[pltpu.VMEM((count, width), F32), pltpu.VMEM((count, width), BF16)],
         compiler_params=pltpu.CompilerParams(vmem_limit_bytes=8 << 20),
         name="pick",
-    )(*in_vmem(loc_patch.reshape(-1, LANES), own, other))
+    )(*in_vmem(loc_patch.reshape(-1, LANES), *held))
 
 
 def swap_cores(array):
@@ -604,9 +612,8 @@
 
 def spread(images):
     held = jnp.concatenate([images, swap_cores(images)])
-    for hops in (FAR, NEAR):
-        held = jnp.concatenate([held] + [onward(held, h) for h in hops[1:]])
-    return held
+    held = jnp.concatenate([held] + [onward(held, h) for h in FAR[1:]])
+    return [held] + [onward(held, h) for h in NEAR[1:]]
 
 
 def per_device(
@@ -622,8 +629,8 @@
     neighbour = lax.ppermute(to_neighbour, SLAB, pairs + [(j, i) for i, j in pairs])
     prepared = early(wavefields, params, slab_counts, angle_table)
     images = late(wavefields, partner, neighbour, prepared, angle_table.shape[0])
-    own = spread(images)
-    return pick(loc_patch, own, swap_cores(own), loc_patch.shape[0] // slabs, per_slab)
+    mine, theirs = pick(loc_patch, spread(images), loc_patch.shape[0] // slabs, per_slab)
+    return mine + swap_cores(theirs).astype(F32)
 
 
 def solution(mesh):

time: 53.4 us -> 51.5 us (0.964)
  Pallas kernels: 12.4 us -> 10.5 us
  other arithmetic: 0.1 us -> 0.93 us
  waiting for transfers between devices: 14.4 us -> 13.6 us
    pallas_call x1, Pallas kernels: 6.15 us -> 4.93 us  [late(): pl.pallas_call(late_kernel, in_specs=[VMEM_WHOLE] * len(args), out_specs=...]
    add x0 -> x1, other arithmetic: none -> 0.84 us  [per_device(): return mine + swap_cores(theirs).astype(F32)]
    ppermute x3, waiting for transfers between devices: 3.1 us -> 2.35 us  [swap_cores(): return lax.ppermute(array, 'core', [(0, 1), (1, 0)])]
where the time goes in v5:
time: 51.5 us; the launch traced here: 51.4 us
  starting transfers between devices  26.1 us (51%)
  waiting for transfers between devices  13.6 us (26%)
  Pallas kernels  10.5 us (20%)
  other arithmetic  0.93 us (2%)
    ppermute x4, starting transfers between devices, onward(): return lax.ppermute(array, SLAB, pairs)  13.3 us
    ppermute x3, starting transfers between devices, swap_cores(): return lax.ppermute(array, 'core', [(0, 1), (1, 0)])  10.8 us
    ppermute x4, waiting for transfers between devices, onward(): return lax.ppermute(array, SLAB, pairs)  10.6 us
    pallas_call x1, Pallas kernels, late(): pl.pallas_call(late_kernel, in_specs=[VMEM_WHOLE] * len(args), out_specs=...  4.93 us
    pallas_call x1, Pallas kernels, early(): pl.pallas_call(early_kernel, in_specs=[pl.BlockSpec(memory_space=pltpu.SM...  3.54 us
    ppermute x3, waiting for transfers between devices, swap_cores(): return lax.ppermute(array, 'core', [(0, 1), (1, 0)])  2.35 us
    ppermute x1, starting transfers between devices, per_device(): lax.ppermute(to_neighbour, SLAB, pairs + [(j, i) for i, j in pairs])  1.94 us
    pallas_call x1, Pallas kernels, pack(): pl.pallas_call(pack_kernel, grid=(1,), in_specs=specs, out_specs=[VMEM_WH...  1.25 us
  transfers between devices with their start and end apart: 8, of which 7 were waited for; matrix products, arithmetic and copies ran while one was open for 0% of the time, Pallas kernels for 7%

profile of v5, /device:TPU:69, one launch (start us, length us, event | category | flops | bytes accessed | tf_op | source)
XLA Modules:
  0.0 51.4 jit_solution(13920199138519838721)
XLA Ops:
  0.0 0.0 copy-start.8
  0.0 0.0 copy-start.11
  0.0 0.0 copy-start
  0.0 0.0 copy-start.4
  0.1 0.0 copy-start.3
  0.1 0.0 copy-start.2
  0.1 1.2 %pack.1 = (bf16[128,512]{1,0:T(8,128)(2,1)S(1)}, bf16[128,512]{1,0:T(8,128)(2,1)S(1)}) custom-call(f32[2,4,2,128,512]{4,3,2,1,0:T(8,128)} %wave_ref.3, f32[2,4,2,128,512]{4,3,2,1,0:T(8,128)} %wave_ref.3, f32[128,512]{1,0:T(8,128)} %courant_ref.1, f32[128,512]{1,0:T(8,128)} %courant_ref.1, f32[128,512]{1,0:T(8,128)} %eps_ref.1, f32[128,512]{1,0:T(8,128)} %eps_ref.1, ...), custom_call_target="tpu_custom_call" | custom-call | tf_op jit(solution)/shard_map/pack/pallas_call | solution.py:163
  1.4 0.0 copy-start.9
  1.4 0.0 copy-start.10
  1.4 0.0 copy-start.12
  1.4 10.0 %collective-permute-start = (bf16[128,512]{1,0:T(8,128)(2,1)S(1)}, bf16[128,512]{1,0:T(8,128)(2,1)S(1)}, u32[]{:S(2)}, u32[]{:S(2)}) collective-permute-start(bf16[128,512]{1,0:T(8,128)(2,1)S(1)} %get-tuple-element.20), channel_id=1, source_target_pairs={{0,1},{1,0},{2,3},{3,2},{4,5},{5,4},{6,7},{7,6},{8,9},{9,8},{10,11... | collective-permute-start | bytes 393224 | tf_op jit(solution)/shard_map/ppermute | solution.py:603
  11.4 1.9 %collective-permute-start.1 = (bf16[128,512]{1,0:T(8,128)(2,1)S(1)}, bf16[128,512]{1,0:T(8,128)(2,1)S(1)}, u32[]{:S(2)}, u32[]{:S(2)}) collective-permute-start(bf16[128,512]{1,0:T(8,128)(2,1)S(1)} %get-tuple-element.21), channel_id=1, source_target_pairs={{1,2},{3,4},{5,6},{7,8},{9,10},{11,12},{13,14},{15,16},{17,18},{19... | collective-permute-start | bytes 393224 | tf_op jit(solution)/shard_map/ppermute | solution.py:629
  13.5 3.5 %early.1 = (f32[128,512]{1,0:T(8,128)S(1)}, f32[128,512]{1,0:T(8,128)S(1)}, f32[128,512]{1,0:T(8,128)S(1)}, f32[128,512]{1,0:T(8,128)S(1)}, f32[128,512]{1,0:T(8...) custom-call(s32[32]{0:T(128)S(1)} %copy-done.14, ...), custom_call_target="tpu_custom_call" | custom-call | tf_op jit(solution)/shard_map/early/pallas_call | solution.py:502
  17.0 0.0 collective-permute-done.partner_ref
  17.0 0.7 %collective-permute-done.1.neighbour_ref = bf16[128,512]{1,0:T(8,128)(2,1)S(1)} collective-permute-done((bf16[128,512]{1,0:T(8,128)(2,1)S(1)}, bf16[128,512]{1,0:T(8,128)(2,1)S(1)}, u32[]{:S(2)}, u32[]{:S(2)}) %collective-permute-start.1) | collective-permute-done | bytes 131104 | tf_op jit(solution)/shard_map/ppermute | solution.py:629
  17.7 0.0 copy-start.13
  17.7 4.9 %late.1 = bf16[4,4096]{1,0:T(4,128)(2,1)S(1)} custom-call(f32[2,4,2,128,512]{4,3,2,1,0:T(8,128)S(1)} %copy-done, bf16[128,512]{1,0:T(8,128)(2,1)S(1)} %collective-permute-done.partner_ref, bf16[128,512]{1,0:T(8,128)(2,1)S(1)} %collective-permute-done.1.neighbour_ref, f32[128,512]{1,0:T(8,128)S(1)} %get-tuple-element.22.mix_ref, ...), custom_call_target="tpu_custom_call" | custom-call | tf_op jit(solution)/shard_map/late/pallas_call | solution.py:549
  22.7 0.1 collective-permute-start.2
  22.8 1.2 %collective-permute-done.2 = bf16[4,4096]{1,0:T(4,128)(2,1)S(1)} collective-permute-done((bf16[4,4096]{1,0:T(4,128)(2,1)S(1)}, bf16[4,4096]{1,0:T(4,128)(2,1)S(1)}, u32[]{:S(2)}, u32[]{:S(2)}) %collective-permute-start.2) | collective-permute-done | bytes 32800 | tf_op jit(solution)/shard_map/ppermute | solution.py:603
  24.0 6.6 %collective-permute-start.4 = (bf16[8,4096]{1,0:T(8,128)(2,1)S(1)}, bf16[8,4096]{1,0:T(8,128)(2,1)S(1)}, u32[]{:S(2)}, u32[]{:S(2)}) collective-permute-start(bf16[8,4096]{1,0:T(8,128)(2,1)S(1)} %pad_maximum_fusion.1), channel_id=1, source_target_pairs={{0,12},{2,14},{4,16},{6,18},{8,20},{10,22},{12,24},{14,26},{16,28}... | collective-permute-start | bytes 196616 | tf_op jit(solution)/shard_map/ppermute | solution.py:610
  30.7 2.2 %collective-permute-start.3 = (bf16[8,4096]{1,0:T(8,128)(2,1)S(1)}, bf16[8,4096]{1,0:T(8,128)(2,1)S(1)}, u32[]{:S(2)}, u32[]{:S(2)}) collective-permute-start(bf16[8,4096]{1,0:T(8,128)(2,1)S(1)} %pad_maximum_fusion.1), channel_id=1, source_target_pairs={{0,6},{2,8},{4,10},{6,12},{8,14},{10,16},{12,18},{14,20},{16,22},{... | collective-permute-start | bytes 196616 | tf_op jit(solution)/shard_map/ppermute | solution.py:610
  32.9 3.8 %collective-permute-done.4 = bf16[8,4096]{1,0:T(8,128)(2,1)S(1)} collective-permute-done((bf16[8,4096]{1,0:T(8,128)(2,1)S(1)}, bf16[8,4096]{1,0:T(8,128)(2,1)S(1)}, u32[]{:S(2)}, u32[]{:S(2)}) %collective-permute-start.4) | collective-permute-done | bytes 65568 | tf_op jit(solution)/shard_map/ppermute | solution.py:610
  36.7 1.0 %collective-permute-done.3 = bf16[8,4096]{1,0:T(8,128)(2,1)S(1)} collective-permute-done((bf16[8,4096]{1,0:T(8,128)(2,1)S(1)}, bf16[8,4096]{1,0:T(8,128)(2,1)S(1)}, u32[]{:S(2)}, u32[]{:S(2)}) %collective-permute-start.3) | collective-permute-done | bytes 65568 | tf_op jit(solution)/shard_map/ppermute | solution.py:610
  37.7 0.1 pad_maximum_fusion.refs_1_
  37.7 4.4 %collective-permute-start.6 = (bf16[24,4096]{1,0:T(8,128)(2,1)S(1)}, bf16[24,4096]{1,0:T(8,128)(2,1)S(1)}, u32[]{:S(2)}, u32[]{:S(2)}) collective-permute-start(bf16[24,4096]{1,0:T(8,128)(2,1)S(1)} %pad_maximum_fusion.refs_1_), channel_id=1, source_target_pairs={{0,4},{2,6},{4,8},{6,10},{8,12},{10,14},{12,16},{14,18},{16,20},{1... | collective-permute-start | bytes 589832 | tf_op jit(solution)/shard_map/ppermute | solution.py:610
  42.1 0.1 collective-permute-start.5
  42.2 3.7 %collective-permute-done.6.refs_3_ = bf16[24,4096]{1,0:T(8,128)(2,1)S(1)} collective-permute-done((bf16[24,4096]{1,0:T(8,128)(2,1)S(1)}, bf16[24,4096]{1,0:T(8,128)(2,1)S(1)}, u32[]{:S(2)}, u32[]{:S(2)}) %collective-permute-start.6) | collective-permute-done | bytes 196640 | tf_op jit(solution)/shard_map/ppermute | solution.py:610
  45.8 2.1 %collective-permute-done.5.refs_2_ = bf16[24,4096]{1,0:T(8,128)(2,1)S(1)} collective-permute-done((bf16[24,4096]{1,0:T(8,128)(2,1)S(1)}, bf16[24,4096]{1,0:T(8,128)(2,1)S(1)}, u32[]{:S(2)}, u32[]{:S(2)}) %collective-permute-start.5) | collective-permute-done | bytes 196640 | tf_op jit(solution)/shard_map/ppermute | solution.py:610
  48.0 0.8 %pick.1 = (f32[32,4096]{1,0:T(8,128)S(1)}, bf16[32,4096]{1,0:T(8,128)(2,1)S(1)}) custom-call(s32[8,128]{1,0:T(8,128)S(1)} %bitcast.2, bf16[24,4096]{1,0:T(8,128)(2,1)S(1)} %pad_maximum_fusion.refs_1_, bf16[24,4096]{1,0:T(8,128)(2,1)S(1)} %collective-permute-done.5.refs_2_, bf16[24,4096]{1,0:T(8,128)(2,1)S(1)} %collective-permute-done.6.refs_3_), custom_call_target="tpu_custom_call" | custom-call | tf_op jit(solution)/shard_map/pick/pallas_call | solution.py:592
  48.7 0.7 %collective-permute-start.7 = (bf16[32,4096]{1,0:T(8,128)(2,1)S(1)}, bf16[32,4096]{1,0:T(8,128)(2,1)S(1)}, u32[]{:S(2)}, u32[]{:S(2)}) collective-permute-start(bf16[32,4096]{1,0:T(8,128)(2,1)S(1)} %get-tuple-element.34), channel_id=1, source_target_pairs={{0,1},{1,0},{2,3},{3,2},{4,5},{5,4},{6,7},{7,6},{8,9},{9,8},{10,11... | collective-permute-start | bytes 786440 | tf_op jit(solution)/shard_map/ppermute | solution.py:603
  49.4 1.2 %collective-permute-done.7 = bf16[32,4096]{1,0:T(8,128)(2,1)S(1)} collective-permute-done((bf16[32,4096]{1,0:T(8,128)(2,1)S(1)}, bf16[32,4096]{1,0:T(8,128)(2,1)S(1)}, u32[]{:S(2)}, u32[]{:S(2)}) %collective-permute-start.7) | collective-permute-done | bytes 262176 | tf_op jit(solution)/shard_map/ppermute | solution.py:603
  50.6 0.8 %convert_add_fusion = f32[32,4096]{1,0:T(8,128)} fusion(f32[32,4096]{1,0:T(8,128)S(1)} %get-tuple-element.33, bf16[32,4096]{1,0:T(8,128)(2,1)S(1)} %collective-permute-done.7), kind=kLoop, calls=%fused_computation | loop fusion | flops 262144 | bytes 1310720 | tf_op jit(solution)/shard_map/add | solution.py:633
  (23 shorter events, 0.1 us)
Async XLA Ops:
  0.0 13.4 %copy-start.5 = (bf16[256,256]{1,0:T(8,128)(2,1)S(1)}, bf16[256,256]{1,0:T(8,128)(2,1)}, u32[]{:S(2)}) copy-start(bf16[256,256]{1,0:T(8,128)(2,1)} %constant.20.clone.x_across_ref) | copy-start | bytes 393220
  0.0 13.4 %copy-start.6 = (bf16[256,256]{1,0:T(8,128)(2,1)S(1)}, bf16[256,256]{1,0:T(8,128)(2,1)}, u32[]{:S(2)}) copy-start(bf16[256,256]{1,0:T(8,128)(2,1)} %constant.19.clone.x_ref) | copy-start | bytes 393220
  0.0 13.4 %copy-start.7 = (bf16[256,256]{1,0:T(8,128)(2,1)S(1)}, bf16[256,256]{1,0:T(8,128)(2,1)}, u32[]{:S(2)}) copy-start(bf16[256,256]{1,0:T(8,128)(2,1)} %constant.18.clone.xx_across_ref) | copy-start | bytes 393220
  0.0 13.4 %copy-start.8 = (bf16[256,256]{1,0:T(8,128)(2,1)S(1)}, bf16[256,256]{1,0:T(8,128)(2,1)}, u32[]{:S(2)}) copy-start(bf16[256,256]{1,0:T(8,128)(2,1)} %constant.17.clone.xx_ref) | copy-start | bytes 393220
  0.0 13.4 %copy-start.11 = (bf16[256,128]{1,0:T(8,128)(2,1)S(1)}, bf16[256,128]{1,0:T(8,128)(2,1)}, u32[]{:S(2)}) copy-start(bf16[256,128]{1,0:T(8,128)(2,1)} %constant.16.clone.own_ref) | copy-start | bytes 196612
  0.0 13.4 %copy-start = (f32[2,4,2,128,512]{4,3,2,1,0:T(8,128)S(1)}, f32[2,4,2,128,512]{4,3,2,1,0:T(8,128)}, u32[]{:S(2)}) copy-start(f32[2,4,2,128,512]{4,3,2,1,0:T(8,128)} %wave_ref.3) | copy-start | bytes 12582916
  0.0 13.4 %copy-start.4 = (f32[128,512]{1,0:T(8,128)S(1)}, f32[128,512]{1,0:T(8,128)}, u32[]{:S(2)}) copy-start(f32[128,512]{1,0:T(8,128)} %tilt_ref.1) | copy-start | bytes 786436
  0.1 13.4 %copy-start.3 = (f32[128,512]{1,0:T(8,128)S(1)}, f32[128,512]{1,0:T(8,128)}, u32[]{:S(2)}) copy-start(f32[128,512]{1,0:T(8,128)} %delta_ref.1) | copy-start | bytes 786436
  0.1 13.4 %copy-start.2 = (f32[128,512]{1,0:T(8,128)S(1)}, f32[128,512]{1,0:T(8,128)}, u32[]{:S(2)}) copy-start(f32[128,512]{1,0:T(8,128)} %eps_ref.1) | copy-start | bytes 786436
  0.1 13.4 %copy-start.1 = (f32[128,512]{1,0:T(8,128)S(1)}, f32[128,512]{1,0:T(8,128)}, u32[]{:S(2)}) copy-start(f32[128,512]{1,0:T(8,128)} %courant_ref.1) | copy-start | bytes 786436
  0.1 13.4 %copy-start.15 = (s32[64]{0:T(128)S(1)}, s32[64]{0:T(128)}, u32[]{:S(2)}) copy-start(s32[64]{0:T(128)} %param.27) | copy-start | bytes 772
  0.1 13.4 %copy-start.14 = (s32[32]{0:T(128)S(1)}, s32[32]{0:T(128)}, u32[]{:S(2)}) copy-start(s32[32]{0:T(128)} %counts_ref.1) | copy-start | bytes 388
  1.4 16.4 %copy-start.9 = (bf16[256,144]{1,0:T(8,128)(2,1)S(1)}, bf16[256,144]{1,0:T(8,128)(2,1)}, u32[]{:S(2)}) copy-start(bf16[256,144]{1,0:T(8,128)(2,1)} %constant.22.clone.two_ref) | copy-start | bytes 221188
  1.4 16.3 %copy-start.10 = (bf16[128,384]{1,0:T(8,128)(2,1)S(1)}, bf16[128,384]{1,0:T(8,128)(2,1)}, u32[]{:S(2)}) copy-start(bf16[128,384]{1,0:T(8,128)(2,1)} %constant.23.clone.depth_ref) | copy-start | bytes 294916
  1.4 16.3 %copy-start.12 = (bf16[64,48]{1,0:T(8,128)(2,1)S(1)}, bf16[64,48]{1,0:T(8,128)(2,1)}, u32[]{:S(2)}) copy-start(bf16[64,48]{1,0:T(8,128)(2,1)} %constant.21.clone.edge_table_ref) | copy-start | bytes 18436
  1.4 15.6 %collective-permute-start = (bf16[128,512]{1,0:T(8,128)(2,1)S(1)}, bf16[128,512]{1,0:T(8,128)(2,1)S(1)}, u32[]{:S(2)}, u32[]{:S(2)}) collective-permute-start(bf16[128,512]{1,0:T(8,128)(2,1)S(1)} %get-tuple-element.20), channel_id=1, source_target_pairs={{0,1},{1,0},{2,3},{3,2},{4,5},{5,4},{6,7},{7,6},{8,9},{9,8},{10,11... | collective-permute-start | bytes 393224 | tf_op jit(solution)/shard_map/ppermute | solution.py:603
  11.4 6.3 %collective-permute-start.1 = (bf16[128,512]{1,0:T(8,128)(2,1)S(1)}, bf16[128,512]{1,0:T(8,128)(2,1)S(1)}, u32[]{:S(2)}, u32[]{:S(2)}) collective-permute-start(bf16[128,512]{1,0:T(8,128)(2,1)S(1)} %get-tuple-element.21), channel_id=1, source_target_pairs={{1,2},{3,4},{5,6},{7,8},{9,10},{11,12},{13,14},{15,16},{17,18},{19... | collective-permute-start | bytes 393224 | tf_op jit(solution)/shard_map/ppermute | solution.py:629
  17.7 30.2 %copy-start.13 = (s32[1024]{0:T(1024)S(1)}, s32[1024]{0:T(1024)}, u32[]{:S(2)}) copy-start(s32[1024]{0:T(1024)} %param.25) | copy-start | bytes 12292
  22.7 1.3 %collective-permute-start.2 = (bf16[4,4096]{1,0:T(4,128)(2,1)S(1)}, bf16[4,4096]{1,0:T(4,128)(2,1)S(1)}, u32[]{:S(2)}, u32[]{:S(2)}) collective-permute-start(bf16[4,4096]{1,0:T(4,128)(2,1)S(1)} %late.1), channel_id=1, source_target_pairs={{0,1},{1,0},{2,3},{3,2},{4,5},{5,4},{6,7},{7,6},{8,9},{9,8},{10,11... | collective-permute-start | bytes 98312 | tf_op jit(solution)/shard_map/ppermute | solution.py:603
  24.0 12.6 %collective-permute-start.4 = (bf16[8,4096]{1,0:T(8,128)(2,1)S(1)}, bf16[8,4096]{1,0:T(8,128)(2,1)S(1)}, u32[]{:S(2)}, u32[]{:S(2)}) collective-permute-start(bf16[8,4096]{1,0:T(8,128)(2,1)S(1)} %pad_maximum_fusion.1), channel_id=1, source_target_pairs={{0,12},{2,14},{4,16},{6,18},{8,20},{10,22},{12,24},{14,26},{16,28}... | collective-permute-start | bytes 196616 | tf_op jit(solution)/shard_map/ppermute | solution.py:610
  30.7 7.0 %collective-permute-start.3 = (bf16[8,4096]{1,0:T(8,128)(2,1)S(1)}, bf16[8,4096]{1,0:T(8,128)(2,1)S(1)}, u32[]{:S(2)}, u32[]{:S(2)}) collective-permute-start(bf16[8,4096]{1,0:T(8,128)(2,1)S(1)} %pad_maximum_fusion.1), channel_id=1, source_target_pairs={{0,6},{2,8},{4,10},{6,12},{8,14},{10,16},{12,18},{14,20},{16,22},{... | collective-permute-start | bytes 196616 | tf_op jit(solution)/shard_map/ppermute | solution.py:610
  37.7 8.1 %collective-permute-start.6 = (bf16[24,4096]{1,0:T(8,128)(2,1)S(1)}, bf16[24,4096]{1,0:T(8,128)(2,1)S(1)}, u32[]{:S(2)}, u32[]{:S(2)}) collective-permute-start(bf16[24,4096]{1,0:T(8,128)(2,1)S(1)} %pad_maximum_fusion.refs_1_), channel_id=1, source_target_pairs={{0,4},{2,6},{4,8},{6,10},{8,12},{10,14},{12,16},{14,18},{16,20},{1... | collective-permute-start | bytes 589832 | tf_op jit(solution)/shard_map/ppermute | solution.py:610
  42.1 5.9 %collective-permute-start.5 = (bf16[24,4096]{1,0:T(8,128)(2,1)S(1)}, bf16[24,4096]{1,0:T(8,128)(2,1)S(1)}, u32[]{:S(2)}, u32[]{:S(2)}) collective-permute-start(bf16[24,4096]{1,0:T(8,128)(2,1)S(1)} %pad_maximum_fusion.refs_1_), channel_id=1, source_target_pairs={{0,2},{2,4},{4,6},{6,8},{8,10},{10,12},{12,14},{14,16},{16,18},{18... | collective-permute-start | bytes 589832 | tf_op jit(solution)/shard_map/ppermute | solution.py:610
  48.7 1.9 %collective-permute-start.7 = (bf16[32,4096]{1,0:T(8,128)(2,1)S(1)}, bf16[32,4096]{1,0:T(8,128)(2,1)S(1)}, u32[]{:S(2)}, u32[]{:S(2)}) collective-permute-start(bf16[32,4096]{1,0:T(8,128)(2,1)S(1)} %get-tuple-element.34), channel_id=1, source_target_pairs={{0,1},{1,0},{2,3},{3,2},{4,5},{5,4},{6,7},{7,6},{8,9},{9,8},{10,11... | collective-permute-start | bytes 786440 | tf_op jit(solution)/shard_map/ppermute | solution.py:603

commit v6 on v5

--- a/solution.py
+++ b/solution.py
@@ -8,6 +8,7 @@
 from jax.experimental.pallas import tpu as pltpu
 from jax.sharding import Mesh
 from jax.sharding import PartitionSpec as P
+
 
 SLAB = ("chip", "core")
 GROUPS_SLAB = ("groups", "chip", "core")
@@ -217,7 +218,7 @@
     mix_ref, twist_ref, a_ref, b_ref, c_ref, low_c, low_s, high_c, high_s, alive_ref, next_ref,
     field_ref, slope_ref, zz_ref, xx_out, xz_out,
 ):
-    rows, cols = courant_ref.shape
+    rows, _ = courant_ref.shape
     wavefields, _, shots = wave_ref.shape[:3]
     columns = (xx_ref, xx_across_ref, x_ref, x_across_ref)
     items = [(w, s) for w in range(wavefields) for s in range(shots)]
@@ -490,7 +491,7 @@
 
 
 def early(wavefields, params, slab_counts, angle_table):
-    two, four, shots, rows, cols = wavefields.shape
+    two, _, shots, rows, cols = wavefields.shape
     field = pltpu.VMEM((rows, cols), F32)
     table = pltpu.VMEM((rows // 2 // RUN, LANES, LANES), F32)
     own = jnp.asarray(row_tables(rows)[0], dtype=BF16)
@@ -517,7 +518,7 @@
 
 
 def late(wavefields, partner, neighbour, prepared, angles):
-    two, four, shots, rows, cols = wavefields.shape
+    two, _, shots, rows, cols = wavefields.shape
     bins = rows // 2
     per_slab = cols // rows
     items = two * shots
@@ -574,7 +575,7 @@
     ahead = lax.rem(owner // 2 - chip + chips, chips)
     up = ahead <= chips // 2
     hops = jnp.where(up, ahead, chips - ahead)
-    holder = jnp.where(up, 1, 0)
+    holder = jnp.where(hops == chips // 2, owner % 2, jnp.where(up, 1, 0))
     index = (2 * (hops // len(NEAR)) + jnp.where(owner % 2 == holder, 0, 1)) * per_slab + loc % per_slab
     total = None
     for near, ref in enumerate(held_refs):
@@ -613,20 +614,21 @@
 def spread(images):
     held = jnp.concatenate([images, swap_cores(images)])
     held = jnp.concatenate([held] + [onward(held, h) for h in FAR[1:]])
-    return [held] + [onward(held, h) for h in NEAR[1:]]
+    short = held[: held.shape[0] - images.shape[0]]
+    return [held] + [onward(short if h == NEAR[-1] else held, h) for h in NEAR[1:]]
 
 
 def per_device(
     wavefields, courant, epsilon, anisotropy_delta, tilt_angle, loc_patch, slab_counts, angle_table
 ):
     slabs = lax.axis_size(SLAB)
-    assert FAR[-1] + NEAR[-1] >= slabs // 4
+    assert FAR[-1] + NEAR[-1] == slabs // 4
     per_slab = wavefields.shape[4] // wavefields.shape[3]
     params = (courant, epsilon, anisotropy_delta, tilt_angle)
     to_partner, to_neighbour = pack(wavefields, params)
-    partner = swap_cores(to_partner)
     pairs = [(i, i + 1) for i in range(1, slabs - 1, 2)]
     neighbour = lax.ppermute(to_neighbour, SLAB, pairs + [(j, i) for i, j in pairs])
+    partner = swap_cores(to_partner)
     prepared = early(wavefields, params, slab_counts, angle_table)
     images = late(wavefields, partner, neighbour, prepared, angle_table.shape[0])
     mine, theirs = pick(loc_patch, spread(images), loc_patch.shape[0] // slabs, per_slab)

time: 51.5 us -> 54.9 us (1.066)
  starting transfers between devices: 26.1 us -> 29.1 us
    ppermute x3, starting transfers between devices: 10.8 us -> 13.8 us  [swap_cores(): return lax.ppermute(array, 'core', [(0, 1), (1, 0)])]
  transfers between devices with their start and end apart: 8 -> 8, of which waited for: 7 -> 6; matrix products, arithmetic and copies ran while one was open for 0% -> 0% of each run, Pallas kernels for 7% -> 6%
where the time goes in v6:
time: 54.9 us; the launch traced here: 54.8 us
  starting transfers between devices  29.1 us (53%)
  waiting for transfers between devices  13.9 us (25%)
  Pallas kernels  10.5 us (19%)
  other arithmetic  0.93 us (2%)
    ppermute x3, starting transfers between devices, swap_cores(): return lax.ppermute(array, 'core', [(0, 1), (1, 0)])  13.8 us
    ppermute x4, starting transfers between devices, onward(): return lax.ppermute(array, SLAB, pairs)  13.4 us
    ppermute x4, waiting for transfers between devices, onward(): return lax.ppermute(array, SLAB, pairs)  10.9 us
    pallas_call x1, Pallas kernels, late(): pl.pallas_call(late_kernel, in_specs=[VMEM_WHOLE] * len(args), out_specs=...  4.93 us
    pallas_call x1, Pallas kernels, early(): pl.pallas_call(early_kernel, in_specs=[pl.BlockSpec(memory_space=pltpu.SM...  3.54 us
    ppermute x3, waiting for transfers between devices, swap_cores(): return lax.ppermute(array, 'core', [(0, 1), (1, 0)])  2.35 us
    ppermute x1, starting transfers between devices, per_device(): lax.ppermute(to_neighbour, SLAB, pairs + [(j, i) for i, j in pairs])  1.94 us
    pallas_call x1, Pallas kernels, pack(): pl.pallas_call(pack_kernel, grid=(1,), in_specs=specs, out_specs=[VMEM_WH...  1.25 us
  transfers between devices with their start and end apart: 8, of which 6 were waited for; matrix products, arithmetic and copies ran while one was open for 0% of the time, Pallas kernels for 6%

profile of v6, /device:TPU:69, one launch (start us, length us, event | category | flops | bytes accessed | tf_op | source)
XLA Modules:
  0.0 54.8 jit_solution(6879723338008970053)
XLA Ops:
  0.0 0.0 copy-start.8
  0.0 0.0 copy-start.11
  0.0 0.0 copy-start
  0.0 0.0 copy-start.4
  0.1 0.0 copy-start.3
  0.1 0.0 copy-start.2
  0.1 1.2 %pack.1 = (bf16[128,512]{1,0:T(8,128)(2,1)S(1)}, bf16[128,512]{1,0:T(8,128)(2,1)S(1)}) custom-call(f32[2,4,2,128,512]{4,3,2,1,0:T(8,128)} %wave_ref.3, f32[2,4,2,128,512]{4,3,2,1,0:T(8,128)} %wave_ref.3, f32[128,512]{1,0:T(8,128)} %courant_ref.1, f32[128,512]{1,0:T(8,128)} %courant_ref.1, f32[128,512]{1,0:T(8,128)} %eps_ref.1, f32[128,512]{1,0:T(8,128)} %eps_ref.1, ...), custom_call_target="tpu_custom_call" | custom-call | tf_op jit(solution)/shard_map/pack/pallas_call | solution.py:164
  1.4 0.0 copy-start.9
  1.4 0.0 copy-start.10
  1.4 0.0 copy-start.12
  1.4 10.0 %collective-permute-start = (bf16[128,512]{1,0:T(8,128)(2,1)S(1)}, bf16[128,512]{1,0:T(8,128)(2,1)S(1)}, u32[]{:S(2)}, u32[]{:S(2)}) collective-permute-start(bf16[128,512]{1,0:T(8,128)(2,1)S(1)} %get-tuple-element.20), channel_id=1, source_target_pairs={{0,1},{1,0},{2,3},{3,2},{4,5},{5,4},{6,7},{7,6},{8,9},{9,8},{10,11... | collective-permute-start | bytes 393224 | tf_op jit(solution)/shard_map/ppermute | solution.py:604
  11.4 1.9 %collective-permute-start.1 = (bf16[128,512]{1,0:T(8,128)(2,1)S(1)}, bf16[128,512]{1,0:T(8,128)(2,1)S(1)}, u32[]{:S(2)}, u32[]{:S(2)}) collective-permute-start(bf16[128,512]{1,0:T(8,128)(2,1)S(1)} %get-tuple-element.21), channel_id=1, source_target_pairs={{1,2},{3,4},{5,6},{7,8},{9,10},{11,12},{13,14},{15,16},{17,18},{19... | collective-permute-start | bytes 393224 | tf_op jit(solution)/shard_map/ppermute | solution.py:630
  13.5 3.5 %early.1 = (f32[128,512]{1,0:T(8,128)S(1)}, f32[128,512]{1,0:T(8,128)S(1)}, f32[128,512]{1,0:T(8,128)S(1)}, f32[128,512]{1,0:T(8,128)S(1)}, f32[128,512]{1,0:T(8...) custom-call(s32[32]{0:T(128)S(1)} %copy-done.14, ...), custom_call_target="tpu_custom_call" | custom-call | tf_op jit(solution)/shard_map/early/pallas_call | solution.py:503
  17.0 0.0 collective-permute-done.partner_ref
  17.0 0.7 %collective-permute-done.1.neighbour_ref = bf16[128,512]{1,0:T(8,128)(2,1)S(1)} collective-permute-done((bf16[128,512]{1,0:T(8,128)(2,1)S(1)}, bf16[128,512]{1,0:T(8,128)(2,1)S(1)}, u32[]{:S(2)}, u32[]{:S(2)}) %collective-permute-start.1) | collective-permute-done | bytes 131104 | tf_op jit(solution)/shard_map/ppermute | solution.py:630
  17.7 0.0 copy-start.13
  17.7 4.9 %late.1 = bf16[4,4096]{1,0:T(4,128)(2,1)S(1)} custom-call(f32[2,4,2,128,512]{4,3,2,1,0:T(8,128)S(1)} %copy-done, bf16[128,512]{1,0:T(8,128)(2,1)S(1)} %collective-permute-done.partner_ref, bf16[128,512]{1,0:T(8,128)(2,1)S(1)} %collective-permute-done.1.neighbour_ref, f32[128,512]{1,0:T(8,128)S(1)} %get-tuple-element.22.mix_ref, ...), custom_call_target="tpu_custom_call" | custom-call | tf_op jit(solution)/shard_map/late/pallas_call | solution.py:550
  22.7 0.1 collective-permute-start.2
  22.8 1.2 %collective-permute-done.2 = bf16[4,4096]{1,0:T(4,128)(2,1)S(1)} collective-permute-done((bf16[4,4096]{1,0:T(4,128)(2,1)S(1)}, bf16[4,4096]{1,0:T(4,128)(2,1)S(1)}, u32[]{:S(2)}, u32[]{:S(2)}) %collective-permute-start.2) | collective-permute-done | bytes 32800 | tf_op jit(solution)/shard_map/ppermute | solution.py:604
  24.0 6.6 %collective-permute-start.4 = (bf16[8,4096]{1,0:T(8,128)(2,1)S(1)}, bf16[8,4096]{1,0:T(8,128)(2,1)S(1)}, u32[]{:S(2)}, u32[]{:S(2)}) collective-permute-start(bf16[8,4096]{1,0:T(8,128)(2,1)S(1)} %pad_maximum_fusion.1), channel_id=1, source_target_pairs={{0,12},{2,14},{4,16},{6,18},{8,20},{10,22},{12,24},{14,26},{16,28}... | collective-permute-start | bytes 196616 | tf_op jit(solution)/shard_map/ppermute | solution.py:611
  30.7 2.2 %collective-permute-start.3 = (bf16[8,4096]{1,0:T(8,128)(2,1)S(1)}, bf16[8,4096]{1,0:T(8,128)(2,1)S(1)}, u32[]{:S(2)}, u32[]{:S(2)}) collective-permute-start(bf16[8,4096]{1,0:T(8,128)(2,1)S(1)} %pad_maximum_fusion.1), channel_id=1, source_target_pairs={{0,6},{2,8},{4,10},{6,12},{8,14},{10,16},{12,18},{14,20},{16,22},{... | collective-permute-start | bytes 196616 | tf_op jit(solution)/shard_map/ppermute | solution.py:611
  32.9 3.8 %collective-permute-done.4 = bf16[8,4096]{1,0:T(8,128)(2,1)S(1)} collective-permute-done((bf16[8,4096]{1,0:T(8,128)(2,1)S(1)}, bf16[8,4096]{1,0:T(8,128)(2,1)S(1)}, u32[]{:S(2)}, u32[]{:S(2)}) %collective-permute-start.4) | collective-permute-done | bytes 65568 | tf_op jit(solution)/shard_map/ppermute | solution.py:611
  36.7 1.0 %collective-permute-done.3 = bf16[8,4096]{1,0:T(8,128)(2,1)S(1)} collective-permute-done((bf16[8,4096]{1,0:T(8,128)(2,1)S(1)}, bf16[8,4096]{1,0:T(8,128)(2,1)S(1)}, u32[]{:S(2)}, u32[]{:S(2)}) %collective-permute-start.3) | collective-permute-done | bytes 65568 | tf_op jit(solution)/shard_map/ppermute | solution.py:611
  37.7 0.1 pad_maximum_fusion.refs_1_
  37.7 0.9 %collective-permute-start.5 = (bf16[24,4096]{1,0:T(8,128)(2,1)S(1)}, bf16[24,4096]{1,0:T(8,128)(2,1)S(1)}, u32[]{:S(2)}, u32[]{:S(2)}) collective-permute-start(bf16[24,4096]{1,0:T(8,128)(2,1)S(1)} %pad_maximum_fusion.refs_1_), channel_id=1, source_target_pairs={{0,2},{2,4},{4,6},{6,8},{8,10},{10,12},{12,14},{14,16},{16,18},{18... | collective-permute-start | bytes 589832 | tf_op jit(solution)/shard_map/ppermute | solution.py:611
  38.6 3.7 %collective-permute-start.6 = (bf16[20,4096]{1,0:T(8,128)(2,1)S(1)}, bf16[20,4096]{1,0:T(8,128)(2,1)S(1)}, u32[]{:S(2)}, u32[]{:S(2)}) collective-permute-start(bf16[20,4096]{1,0:T(8,128)(2,1)S(1)} %bitcast.3), channel_id=1, source_target_pairs={{0,4},{2,6},{4,8},{6,10},{8,12},{10,14},{12,16},{14,18},{16,20},{1... | collective-permute-start | bytes 491528 | tf_op jit(solution)/shard_map/ppermute | solution.py:611
  42.2 6.1 %collective-permute-done.6.refs_3_ = bf16[20,4096]{1,0:T(8,128)(2,1)S(1)} collective-permute-done((bf16[20,4096]{1,0:T(8,128)(2,1)S(1)}, bf16[20,4096]{1,0:T(8,128)(2,1)S(1)}, u32[]{:S(2)}, u32[]{:S(2)}) %collective-permute-start.6) | collective-permute-done | bytes 163872 | tf_op jit(solution)/shard_map/ppermute | solution.py:611
  48.3 0.0 collective-permute-done.5.refs_2_
  48.3 0.8 %pick.1 = (f32[32,4096]{1,0:T(8,128)S(1)}, bf16[32,4096]{1,0:T(8,128)(2,1)S(1)}) custom-call(s32[8,128]{1,0:T(8,128)S(1)} %bitcast.4, bf16[24,4096]{1,0:T(8,128)(2,1)S(1)} %pad_maximum_fusion.refs_1_, bf16[24,4096]{1,0:T(8,128)(2,1)S(1)} %collective-permute-done.5.refs_2_, bf16[20,4096]{1,0:T(8,128)(2,1)S(1)} %collective-permute-done.6.refs_3_), custom_call_target="tpu_custom_call" | custom-call | tf_op jit(solution)/shard_map/pick/pallas_call | solution.py:593
  49.1 3.7 %collective-permute-start.7 = (bf16[32,4096]{1,0:T(8,128)(2,1)S(1)}, bf16[32,4096]{1,0:T(8,128)(2,1)S(1)}, u32[]{:S(2)}, u32[]{:S(2)}) collective-permute-start(bf16[32,4096]{1,0:T(8,128)(2,1)S(1)} %get-tuple-element.34), channel_id=1, source_target_pairs={{0,1},{1,0},{2,3},{3,2},{4,5},{5,4},{6,7},{7,6},{8,9},{9,8},{10,11... | collective-permute-start | bytes 786440 | tf_op jit(solution)/shard_map/ppermute | solution.py:604
  52.8 1.2 %collective-permute-done.7 = bf16[32,4096]{1,0:T(8,128)(2,1)S(1)} collective-permute-done((bf16[32,4096]{1,0:T(8,128)(2,1)S(1)}, bf16[32,4096]{1,0:T(8,128)(2,1)S(1)}, u32[]{:S(2)}, u32[]{:S(2)}) %collective-permute-start.7) | collective-permute-done | bytes 262176 | tf_op jit(solution)/shard_map/ppermute | solution.py:604
  53.9 0.8 %convert_add_fusion = f32[32,4096]{1,0:T(8,128)} fusion(f32[32,4096]{1,0:T(8,128)S(1)} %get-tuple-element.33, bf16[32,4096]{1,0:T(8,128)(2,1)S(1)} %collective-permute-done.7), kind=kLoop, calls=%fused_computation | loop fusion | flops 262144 | bytes 1310720 | tf_op jit(solution)/shard_map/add | solution.py:635
  (23 shorter events, 0.1 us)
Async XLA Ops:
  0.0 13.4 %copy-start.5 = (bf16[256,256]{1,0:T(8,128)(2,1)S(1)}, bf16[256,256]{1,0:T(8,128)(2,1)}, u32[]{:S(2)}) copy-start(bf16[256,256]{1,0:T(8,128)(2,1)} %constant.20.clone.x_across_ref) | copy-start | bytes 393220
  0.0 13.4 %copy-start.6 = (bf16[256,256]{1,0:T(8,128)(2,1)S(1)}, bf16[256,256]{1,0:T(8,128)(2,1)}, u32[]{:S(2)}) copy-start(bf16[256,256]{1,0:T(8,128)(2,1)} %constant.19.clone.x_ref) | copy-start | bytes 393220
  0.0 13.4 %copy-start.7 = (bf16[256,256]{1,0:T(8,128)(2,1)S(1)}, bf16[256,256]{1,0:T(8,128)(2,1)}, u32[]{:S(2)}) copy-start(bf16[256,256]{1,0:T(8,128)(2,1)} %constant.18.clone.xx_across_ref) | copy-start | bytes 393220
  0.0 13.4 %copy-start.8 = (bf16[256,256]{1,0:T(8,128)(2,1)S(1)}, bf16[256,256]{1,0:T(8,128)(2,1)}, u32[]{:S(2)}) copy-start(bf16[256,256]{1,0:T(8,128)(2,1)} %constant.17.clone.xx_ref) | copy-start | bytes 393220
  0.0 13.4 %copy-start.11 = (bf16[256,128]{1,0:T(8,128)(2,1)S(1)}, bf16[256,128]{1,0:T(8,128)(2,1)}, u32[]{:S(2)}) copy-start(bf16[256,128]{1,0:T(8,128)(2,1)} %constant.16.clone.own_ref) | copy-start | bytes 196612
  0.0 13.4 %copy-start = (f32[2,4,2,128,512]{4,3,2,1,0:T(8,128)S(1)}, f32[2,4,2,128,512]{4,3,2,1,0:T(8,128)}, u32[]{:S(2)}) copy-start(f32[2,4,2,128,512]{4,3,2,1,0:T(8,128)} %wave_ref.3) | copy-start | bytes 12582916
  0.0 13.4 %copy-start.4 = (f32[128,512]{1,0:T(8,128)S(1)}, f32[128,512]{1,0:T(8,128)}, u32[]{:S(2)}) copy-start(f32[128,512]{1,0:T(8,128)} %tilt_ref.1) | copy-start | bytes 786436
  0.1 13.4 %copy-start.3 = (f32[128,512]{1,0:T(8,128)S(1)}, f32[128,512]{1,0:T(8,128)}, u32[]{:S(2)}) copy-start(f32[128,512]{1,0:T(8,128)} %delta_ref.1) | copy-start | bytes 786436
  0.1 13.4 %copy-start.2 = (f32[128,512]{1,0:T(8,128)S(1)}, f32[128,512]{1,0:T(8,128)}, u32[]{:S(2)}) copy-start(f32[128,512]{1,0:T(8,128)} %eps_ref.1) | copy-start | bytes 786436
  0.1 13.4 %copy-start.1 = (f32[128,512]{1,0:T(8,128)S(1)}, f32[128,512]{1,0:T(8,128)}, u32[]{:S(2)}) copy-start(f32[128,512]{1,0:T(8,128)} %courant_ref.1) | copy-start | bytes 786436
  0.1 13.4 %copy-start.15 = (s32[64]{0:T(128)S(1)}, s32[64]{0:T(128)}, u32[]{:S(2)}) copy-start(s32[64]{0:T(128)} %param.27) | copy-start | bytes 772
  0.1 13.4 %copy-start.14 = (s32[32]{0:T(128)S(1)}, s32[32]{0:T(128)}, u32[]{:S(2)}) copy-start(s32[32]{0:T(128)} %counts_ref.1) | copy-start | bytes 388
  1.4 16.4 %copy-start.9 = (bf16[256,144]{1,0:T(8,128)(2,1)S(1)}, bf16[256,144]{1,0:T(8,128)(2,1)}, u32[]{:S(2)}) copy-start(bf16[256,144]{1,0:T(8,128)(2,1)} %constant.22.clone.two_ref) | copy-start | bytes 221188
  1.4 16.3 %copy-start.10 = (bf16[128,384]{1,0:T(8,128)(2,1)S(1)}, bf16[128,384]{1,0:T(8,128)(2,1)}, u32[]{:S(2)}) copy-start(bf16[128,384]{1,0:T(8,128)(2,1)} %constant.23.clone.depth_ref) | copy-start | bytes 294916
  1.4 16.3 %copy-start.12 = (bf16[64,48]{1,0:T(8,128)(2,1)S(1)}, bf16[64,48]{1,0:T(8,128)(2,1)}, u32[]{:S(2)}) copy-start(bf16[64,48]{1,0:T(8,128)(2,1)} %constant.21.clone.edge_table_ref) | copy-start | bytes 18436
  1.4 15.6 %collective-permute-start = (bf16[128,512]{1,0:T(8,128)(2,1)S(1)}, bf16[128,512]{1,0:T(8,128)(2,1)S(1)}, u32[]{:S(2)}, u32[]{:S(2)}) collective-permute-start(bf16[128,512]{1,0:T(8,128)(2,1)S(1)} %get-tuple-element.20), channel_id=1, source_target_pairs={{0,1},{1,0},{2,3},{3,2},{4,5},{5,4},{6,7},{7,6},{8,9},{9,8},{10,11... | collective-permute-start | bytes 393224 | tf_op jit(solution)/shard_map/ppermute | solution.py:604
  11.4 6.3 %collective-permute-start.1 = (bf16[128,512]{1,0:T(8,128)(2,1)S(1)}, bf16[128,512]{1,0:T(8,128)(2,1)S(1)}, u32[]{:S(2)}, u32[]{:S(2)}) collective-permute-start(bf16[128,512]{1,0:T(8,128)(2,1)S(1)} %get-tuple-element.21), channel_id=1, source_target_pairs={{1,2},{3,4},{5,6},{7,8},{9,10},{11,12},{13,14},{15,16},{17,18},{19... | collective-permute-start | bytes 393224 | tf_op jit(solution)/shard_map/ppermute | solution.py:630
  17.7 30.6 %copy-start.13 = (s32[1024]{0:T(1024)S(1)}, s32[1024]{0:T(1024)}, u32[]{:S(2)}) copy-start(s32[1024]{0:T(1024)} %param.25) | copy-start | bytes 12292
  22.7 1.3 %collective-permute-start.2 = (bf16[4,4096]{1,0:T(4,128)(2,1)S(1)}, bf16[4,4096]{1,0:T(4,128)(2,1)S(1)}, u32[]{:S(2)}, u32[]{:S(2)}) collective-permute-start(bf16[4,4096]{1,0:T(4,128)(2,1)S(1)} %late.1), channel_id=1, source_target_pairs={{0,1},{1,0},{2,3},{3,2},{4,5},{5,4},{6,7},{7,6},{8,9},{9,8},{10,11... | collective-permute-start | bytes 98312 | tf_op jit(solution)/shard_map/ppermute | solution.py:604
  24.0 12.6 %collective-permute-start.4 = (bf16[8,4096]{1,0:T(8,128)(2,1)S(1)}, bf16[8,4096]{1,0:T(8,128)(2,1)S(1)}, u32[]{:S(2)}, u32[]{:S(2)}) collective-permute-start(bf16[8,4096]{1,0:T(8,128)(2,1)S(1)} %pad_maximum_fusion.1), channel_id=1, source_target_pairs={{0,12},{2,14},{4,16},{6,18},{8,20},{10,22},{12,24},{14,26},{16,28}... | collective-permute-start | bytes 196616 | tf_op jit(solution)/shard_map/ppermute | solution.py:611
  30.7 7.0 %collective-permute-start.3 = (bf16[8,4096]{1,0:T(8,128)(2,1)S(1)}, bf16[8,4096]{1,0:T(8,128)(2,1)S(1)}, u32[]{:S(2)}, u32[]{:S(2)}) collective-permute-start(bf16[8,4096]{1,0:T(8,128)(2,1)S(1)} %pad_maximum_fusion.1), channel_id=1, source_target_pairs={{0,6},{2,8},{4,10},{6,12},{8,14},{10,16},{12,18},{14,20},{16,22},{... | collective-permute-start | bytes 196616 | tf_op jit(solution)/shard_map/ppermute | solution.py:611
  37.7 10.6 %collective-permute-start.5 = (bf16[24,4096]{1,0:T(8,128)(2,1)S(1)}, bf16[24,4096]{1,0:T(8,128)(2,1)S(1)}, u32[]{:S(2)}, u32[]{:S(2)}) collective-permute-start(bf16[24,4096]{1,0:T(8,128)(2,1)S(1)} %pad_maximum_fusion.refs_1_), channel_id=1, source_target_pairs={{0,2},{2,4},{4,6},{6,8},{8,10},{10,12},{12,14},{14,16},{16,18},{18... | collective-permute-start | bytes 589832 | tf_op jit(solution)/shard_map/ppermute | solution.py:611
  38.6 9.7 %collective-permute-start.6 = (bf16[20,4096]{1,0:T(8,128)(2,1)S(1)}, bf16[20,4096]{1,0:T(8,128)(2,1)S(1)}, u32[]{:S(2)}, u32[]{:S(2)}) collective-permute-start(bf16[20,4096]{1,0:T(8,128)(2,1)S(1)} %bitcast.3), channel_id=1, source_target_pairs={{0,4},{2,6},{4,8},{6,10},{8,12},{10,14},{12,16},{14,18},{16,20},{1... | collective-permute-start | bytes 491528 | tf_op jit(solution)/shard_map/ppermute | solution.py:611
  49.1 4.8 %collective-permute-start.7 = (bf16[32,4096]{1,0:T(8,128)(2,1)S(1)}, bf16[32,4096]{1,0:T(8,128)(2,1)S(1)}, u32[]{:S(2)}, u32[]{:S(2)}) collective-permute-start(bf16[32,4096]{1,0:T(8,128)(2,1)S(1)} %get-tuple-element.34), channel_id=1, source_target_pairs={{0,1},{1,0},{2,3},{3,2},{4,5},{5,4},{6,7},{7,6},{8,9},{9,8},{10,11... | collective-permute-start | bytes 786440 | tf_op jit(solution)/shard_map/ppermute | solution.py:604

commit v7 on v6

--- a/solution.py
+++ b/solution.py
@@ -185,25 +185,47 @@
     )
 
 
-def along_columns(out, source, inside, across):
+class Filler:
+    def __init__(self, jobs, points):
+        self.jobs, self.points, self.done, self.calls = (jobs, points, 0, 0)
+
+    def __call__(self):
+        self.calls += 1
+        self.upto(-(-len(self.jobs) * self.calls // self.points))
+
+    def upto(self, count):
+        for job in self.jobs[self.done : count]:
+            job()
+        self.done = max(self.done, min(count, len(self.jobs)))
+
+    def finish(self):
+        self.upto(len(self.jobs))
+
+
+def along_columns(out, source, inside, across, fill):
     out[:, LANES : 3 * LANES] = jnp.dot(source[:, LANES : 3 * LANES], across[...], preferred_element_type=F32)
+    fill()
     left = jnp.dot(source[:, : 2 * LANES], inside[...], preferred_element_type=F32)
     out[:, :LANES] = left[:, :LANES]
     out[:, LANES : 2 * LANES] += left[:, LANES:]
+    fill()
     right = jnp.dot(source[:, 2 * LANES :], inside[...], preferred_element_type=F32)
     out[:, 2 * LANES : 3 * LANES] += right[:, :LANES]
     out[:, 3 * LANES :] = right[:, LANES:]
-
-
-def derive(field, slope, zz, xx, xz, table, columns, fields):
+    fill()
+
+
+def derive(field, slope, zz, xx, xz, table, columns, fields, fill):
     count = table.shape[0] // 2
     for f in range(2):
         source = field[f]
         product = jnp.dot(table[count:, :], source, preferred_element_type=F32)
         slope[f * count : (f + 1) * count, :] = product.astype(BF16)
+        fill()
         zz[f * count : (f + 1) * count, :] = jnp.dot(table[:count, :], source, preferred_element_type=F32)
-    along_columns(xx, fields, columns[0], columns[1])
-    along_columns(xz, slope[...], columns[2], columns[3])
+        fill()
+    along_columns(xx, fields, columns[0], columns[1], fill)
+    along_columns(xz, slope[...], columns[2], columns[3], fill)
 
 
 def tilted(f, value, zz, xx, xz, mix, twist):
@@ -223,6 +245,17 @@
     columns = (xx_ref, xx_across_ref, x_ref, x_across_ref)
     items = [(w, s) for w in range(wavefields) for s in range(shots)]
 
+    def coefficient_job(r):
+        def job():
+            at = slice(r, r + 8)
+            values = coefficients(courant_ref[at, :], eps_ref[at, :], delta_ref[at, :], tilt_ref[at, :])
+            for ref, value in zip((mix_ref, twist_ref, a_ref, b_ref, c_ref), values, strict=True):
+                ref[at, :] = value
+
+        return job
+
+    fill = Filler([coefficient_job(r) for r in range(0, rows, 8)], 20)
+
     def matmuls(i):
         w, s = items[i]
         k = i % 2
@@ -231,7 +264,7 @@
         parts = [field_ref.at[k, f * rows : (f + 1) * rows, :][...] for f in range(2)]
         derive(
             parts, slope_ref.at[k], zz_ref.at[k], xx_out.at[k], xz_out.at[k], own_ref, columns,
-            field_ref.at[k][...],
+            field_ref.at[k][...], fill,
         )
 
     def advance(i):
@@ -251,16 +284,24 @@
             next_ref[i, 0, at, :] = (2.0 * p - p0) + (a * across + b * along)
             next_ref[i, 1, at, :] = (2.0 * q - q0) + (b * across + c * along)
 
-    matmuls(0)
-    for r in range(0, rows, 8):
-        at = slice(r, r + 8)
-        values = coefficients(courant_ref[at, :], eps_ref[at, :], delta_ref[at, :], tilt_ref[at, :])
-        for ref, value in zip((mix_ref, twist_ref, a_ref, b_ref, c_ref), values, strict=True):
-            ref[at, :] = value
-    for i in range(1, len(items)):
-        matmuls(i)
-        advance(i - 1)
-    slant_factors(angle_ref, low_c, low_s, high_c, high_s)
+    @pl.when(lax.axis_index("core") >= 0)
+    def _():
+        matmuls(0)
+        matmuls(1)
+        fill.finish()
+        slant_factors(angle_ref, low_c, low_s, high_c, high_s)
+
+    @pl.when(lax.axis_index("core") >= 0)
+    def _():
+        advance(0)
+        matmuls(2)
+
+    @pl.when(lax.axis_index("core") >= 0)
+    def _():
+        advance(1)
+        matmuls(3)
+
+    advance(2)
     advance(len(items) - 1)
     live = lax.broadcasted_iota(jnp.int32, (8, LANES), 0) < counts_ref[lax.axis_index(SLAB)]
     alive_ref[...] = jnp.where(live, 1.0, 0.0)
@@ -324,59 +365,22 @@
         u, d = group(g)
         return jnp.where(low, half_turn(u), d)
 
-    tall = 32
-    halos = []
-    for i, (w, s) in enumerate(items):
-        halo = []
-        for f in range(2):
-            u, d = group(3 * i + f)
-            inner = jnp.where(low, half_turn(u), half_turn(d))
-            outer = jnp.where(low, u, d)
-            halo.append(inner)
-            pieces = (
-                wave_ref[w, f, s, 0:8, :], wave_ref[w, f, s, rows - 8 : rows, :], inner, outer,
-                wave_ref[w, f, s, 8:16, :], wave_ref[w, f, s, rows - 16 : rows - 8, :],
-            )
-            for n in range(0, 6, 2):
-                pair = jnp.concatenate(pieces[n : n + 2], axis=0).astype(BF16)
-                edge_z[i, f, 8 * n : 8 * n + 16, :] = pair
-                if n < 4:
-                    at = (2 * i + f) * tall + 8 * n
-                    edge_x[at : at + 16, :] = pair
-        halo += [first_halves(3 * i + 2), second_halves(3 * i + 2)]
-        halos.append(halo)
-    for i in range(len(items)):
-        for f in range(2):
-            product = jnp.dot(edge_table_ref[...], edge_z[i, f], preferred_element_type=F32)
-            at = (2 * i + f) * tall
-            edge_zz[at : at + tall, :] = product[:tall]
-            edge_slope[at : at + tall, :] = product[tall:].astype(BF16)
-    along_columns(edge_xx, edge_x[...], xx_ref, xx_across_ref)
-    along_columns(edge_xz, edge_slope[...], x_ref, x_across_ref)
-    g = 3 * len(items)
-    beyond = coefficients(
-        first_halves(g), second_halves(g), first_halves(g + 1), second_halves(g + 1) + first_halves(g + 2)
-    )
-
-    def edge_advance(i):
-        w, s = items[i]
-        for n, r in enumerate((0, rows - 8, None)):
-            if r is None:
-                fields = halos[i]
-                mix, twist, a, b, c = beyond
-            else:
-                at = slice(r, r + 8)
-                fields = [wave_ref[w, f, s, at, :] for f in range(4)]
-                mix, twist, a, b, c = (ref[at, :] for ref in coefficient_refs)
-            p, q, p0, q0 = fields
-
-            def operator(f, value):
-                here = slice((2 * i + f) * tall + 8 * n, (2 * i + f) * tall + 8 * n + 8)
-                return tilted(f, value, edge_zz[here, :], edge_xx[here, :], edge_xz[here, :], mix, twist)
-
-            across, along = (operator(0, p), operator(1, q))
-            edge_next[i, 0, 8 * n : 8 * n + 8, :] = (2.0 * p - p0) + (a * across + b * along)
-            edge_next[i, 1, 8 * n : 8 * n + 8, :] = (2.0 * q - q0) + (b * across + c * along)
+    def slant_job(j, r):
+        def job():
+            at = slice(r, r + 16)
+            one = (low_c[at, :], low_s[at, :])
+            back = (high_c[j, at, :], high_s[j, at, :])
+            here = (back[0] * one[0] - back[1] * one[1], back[0] * one[1] + back[1] * one[0])
+            twice = 2.0 * one[0]
+            for i in range(RUN):
+                slant_ref[RUN * j + i, at, :] = back[0].astype(BF16)
+                slant_ref[RUN * j + i, LANES + r : LANES + r + 16, :] = back[1].astype(BF16)
+                back, here = here, tuple(twice * x - y for x, y in zip(here, back, strict=True))
+
+        return job
+
+    jobs = [slant_job(j, r) for j in range(bins // RUN) for r in range(0, LANES, 16)]
+    fill = Filler(jobs, 6 + 10 * len(items))
 
     def current(i, f, r):
         if r == 0:
@@ -407,7 +411,7 @@
         ]
         derive(
             parts, slope_ref.at[k], zz_ref.at[k], xx_out.at[k], xz_out.at[k], two_ref, columns,
-            field_ref[k, : 2 * rows, :],
+            field_ref[k, : 2 * rows, :], fill,
         )
 
     def advance(i):
@@ -443,10 +447,72 @@
                     part * bins : (part + 1) * bins, m * LANES : (m + 1) * LANES
                 ]
 
-    for i in range(len(items)):
-        edge_advance(i)
-    matmuls(0)
-    for i in range(1, len(items)):
+    @pl.when(lax.axis_index("core") >= 0)
+    def _():
+        tall = 32
+        halos = []
+        for i, (w, s) in enumerate(items):
+            halo = []
+            for f in range(2):
+                u, d = group(3 * i + f)
+                inner = jnp.where(low, half_turn(u), half_turn(d))
+                outer = jnp.where(low, u, d)
+                halo.append(inner)
+                pieces = (
+                    wave_ref[w, f, s, 0:8, :], wave_ref[w, f, s, rows - 8 : rows, :], inner, outer,
+                    wave_ref[w, f, s, 8:16, :], wave_ref[w, f, s, rows - 16 : rows - 8, :],
+                )
+                for n in range(0, 6, 2):
+                    pair = jnp.concatenate(pieces[n : n + 2], axis=0).astype(BF16)
+                    edge_z[i, f, 8 * n : 8 * n + 16, :] = pair
+                    if n < 4:
+                        at = (2 * i + f) * tall + 8 * n
+                        edge_x[at : at + 16, :] = pair
+            halo += [first_halves(3 * i + 2), second_halves(3 * i + 2)]
+            halos.append(halo)
+        for i in range(len(items)):
+            for f in range(2):
+                product = jnp.dot(edge_table_ref[...], edge_z[i, f], preferred_element_type=F32)
+                at = (2 * i + f) * tall
+                edge_zz[at : at + tall, :] = product[:tall]
+                edge_slope[at : at + tall, :] = product[tall:].astype(BF16)
+        along_columns(edge_xx, edge_x[...], xx_ref, xx_across_ref, fill)
+        along_columns(edge_xz, edge_slope[...], x_ref, x_across_ref, fill)
+        g = 3 * len(items)
+        beyond = coefficients(
+            first_halves(g), second_halves(g), first_halves(g + 1), second_halves(g + 1) + first_halves(g + 2)
+        )
+
+        def edge_advance(i):
+            w, s = items[i]
+            for n, r in enumerate((0, rows - 8, None)):
+                if r is None:
+                    fields = halos[i]
+                    mix, twist, a, b, c = beyond
+                else:
+                    at = slice(r, r + 8)
+                    fields = [wave_ref[w, f, s, at, :] for f in range(4)]
+                    mix, twist, a, b, c = (ref[at, :] for ref in coefficient_refs)
+                p, q, p0, q0 = fields
+
+                def operator(f, value):
+                    here = slice((2 * i + f) * tall + 8 * n, (2 * i + f) * tall + 8 * n + 8)
+                    return tilted(f, value, edge_zz[here, :], edge_xx[here, :], edge_xz[here, :], mix, twist)
+
+                across, along = (operator(0, p), operator(1, q))
+                edge_next[i, 0, 8 * n : 8 * n + 8, :] = (2.0 * p - p0) + (a * across + b * along)
+                edge_next[i, 1, 8 * n : 8 * n + 8, :] = (2.0 * q - q0) + (b * across + c * along)
+
+        for i in range(len(items)):
+            edge_advance(i)
+        matmuls(0)
+        for i in range(1, 4):
+            matmuls(i)
+            advance(i - 1)
+            transform(i - 1)
+        fill.finish()
+
+    for i in range(4, len(items)):
         matmuls(i)
         advance(i - 1)
         transform(i - 1)
@@ -456,24 +522,13 @@
     left_lane = lax.broadcasted_iota(jnp.int32, (8, LANES), 1) < LANES // 2
     alive = alive_ref[...]
     for j in range(bins // RUN):
-        slot = j % 2
-        for r in range(0, LANES, 16):
-            at = slice(r, r + 16)
-            one = (low_c[at, :], low_s[at, :])
-            back = (high_c[j, at, :], high_s[j, at, :])
-            here = (back[0] * one[0] - back[1] * one[1], back[0] * one[1] + back[1] * one[0])
-            twice = 2.0 * one[0]
-            for i in range(RUN):
-                slant_ref[slot, i, at, :] = back[0].astype(BF16)
-                slant_ref[slot, i, LANES + r : LANES + r + 16, :] = back[1].astype(BF16)
-                back, here = here, tuple(twice * x - y for x, y in zip(here, back, strict=True))
         pair = []
         for i in range(RUN):
             at = (RUN * j + i) * PITCH
             left = jnp.concatenate(
                 [spectra_ref[at : at + 16, :], spectra_ref[at + 16 : at + 32, :]], axis=1
             ).astype(BF16)
-            stack = jnp.dot(left, slant_ref[slot, i], preferred_element_type=F32)
+            stack = jnp.dot(left, slant_ref[RUN * j + i], preferred_element_type=F32)
             product = stack[:8] * stack[8:]
             pair.append(product + pltpu.roll(product, 4, 0))
             if i % 2 == 1:
@@ -545,7 +600,7 @@
         pltpu.VMEM((2, 3 * rows, cols), BF16),
         pltpu.VMEM((PITCH * bins, LANES), F32),
         pltpu.VMEM((8, bins * angles), F32),
-        pltpu.VMEM((2, RUN, 2 * LANES, LANES), BF16),
+        pltpu.VMEM((bins, 2 * LANES, LANES), BF16),
     ]
     return pl.pallas_call(
         late_kernel,
@@ -553,7 +608,7 @@
         out_specs=VMEM_WHOLE,
         out_shape=pltpu.VMEM(out_shape, BF16),
         scratch_shapes=scratch,
-        compiler_params=pltpu.CompilerParams(vmem_limit_bytes=32 << 20),
+        compiler_params=pltpu.CompilerParams(vmem_limit_bytes=36 << 20),
         name="late",
     )(*in_vmem(*args))
 

time: 54.9 us -> 54.6 us (level)
  no operation moved by 1% of the time
where the time goes in v7:
time: 54.6 us; the launch traced here: 54.5 us
  starting transfers between devices  29.3 us (54%)
  waiting for transfers between devices  14 us (26%)
  Pallas kernels  9.98 us (18%)
  other arithmetic  0.93 us (2%)
    ppermute x3, starting transfers between devices, swap_cores(): return lax.ppermute(array, 'core', [(0, 1), (1, 0)])  13.9 us
    ppermute x4, starting transfers between devices, onward(): return lax.ppermute(array, SLAB, pairs)  13.4 us
    ppermute x4, waiting for transfers between devices, onward(): return lax.ppermute(array, SLAB, pairs)  10.7 us
    pallas_call x1, Pallas kernels, late(): pl.pallas_call(late_kernel, in_specs=[VMEM_WHOLE] * len(args), out_specs=...  4.63 us
    pallas_call x1, Pallas kernels, early(): pl.pallas_call(early_kernel, in_specs=[pl.BlockSpec(memory_space=pltpu.SM...  3.33 us
    ppermute x3, waiting for transfers between devices, swap_cores(): return lax.ppermute(array, 'core', [(0, 1), (1, 0)])  2.35 us
    ppermute x1, starting transfers between devices, per_device(): lax.ppermute(to_neighbour, SLAB, pairs + [(j, i) for i, j in pairs])  1.94 us
    pallas_call x1, Pallas kernels, pack(): pl.pallas_call(pack_kernel, grid=(1,), in_specs=specs, out_specs=[VMEM_WH...  1.25 us
  transfers between devices with their start and end apart: 8, of which 6 were waited for; matrix products, arithmetic and copies ran while one was open for 0% of the time, Pallas kernels for 6%

profile of v7, /device:TPU:69, one launch (start us, length us, event | category | flops | bytes accessed | tf_op | source)
XLA Modules:
  0.0 54.5 jit_solution(9142956661746246993)
XLA Ops:
  0.0 0.0 copy-start.8
  0.0 0.0 copy-start.11
  0.0 0.0 copy-start
  0.0 0.0 copy-start.4
  0.1 0.0 copy-start.3
  0.1 0.0 copy-start.2
  0.1 1.2 %pack.1 = (bf16[128,512]{1,0:T(8,128)(2,1)S(1)}, bf16[128,512]{1,0:T(8,128)(2,1)S(1)}) custom-call(f32[2,4,2,128,512]{4,3,2,1,0:T(8,128)} %wave_ref.3, f32[2,4,2,128,512]{4,3,2,1,0:T(8,128)} %wave_ref.3, f32[128,512]{1,0:T(8,128)} %courant_ref.1, f32[128,512]{1,0:T(8,128)} %courant_ref.1, f32[128,512]{1,0:T(8,128)} %eps_ref.1, f32[128,512]{1,0:T(8,128)} %eps_ref.1, ...), custom_call_target="tpu_custom_call" | custom-call | tf_op jit(solution)/shard_map/pack/pallas_call | solution.py:164
  1.4 0.0 copy-start.9
  1.4 0.0 copy-start.10
  1.4 0.0 copy-start.12
  1.4 10.0 %collective-permute-start = (bf16[128,512]{1,0:T(8,128)(2,1)S(1)}, bf16[128,512]{1,0:T(8,128)(2,1)S(1)}, u32[]{:S(2)}, u32[]{:S(2)}) collective-permute-start(bf16[128,512]{1,0:T(8,128)(2,1)S(1)} %get-tuple-element.20), channel_id=1, source_target_pairs={{0,1},{1,0},{2,3},{3,2},{4,5},{5,4},{6,7},{7,6},{8,9},{9,8},{10,11... | collective-permute-start | bytes 393224 | tf_op jit(solution)/shard_map/ppermute | solution.py:659
  11.4 1.9 %collective-permute-start.1 = (bf16[128,512]{1,0:T(8,128)(2,1)S(1)}, bf16[128,512]{1,0:T(8,128)(2,1)S(1)}, u32[]{:S(2)}, u32[]{:S(2)}) collective-permute-start(bf16[128,512]{1,0:T(8,128)(2,1)S(1)} %get-tuple-element.21), channel_id=1, source_target_pairs={{1,2},{3,4},{5,6},{7,8},{9,10},{11,12},{13,14},{15,16},{17,18},{19... | collective-permute-start | bytes 393224 | tf_op jit(solution)/shard_map/ppermute | solution.py:685
  13.5 3.3 %early.1 = (f32[128,512]{1,0:T(8,128)S(1)}, f32[128,512]{1,0:T(8,128)S(1)}, f32[128,512]{1,0:T(8,128)S(1)}, f32[128,512]{1,0:T(8,128)S(1)}, f32[128,512]{1,0:T(8...) custom-call(s32[32]{0:T(128)S(1)} %copy-done.14, ...), custom_call_target="tpu_custom_call" | custom-call | tf_op jit(solution)/shard_map/early/pallas_call | solution.py:558
  16.8 0.0 collective-permute-done.partner_ref
  16.8 0.9 %collective-permute-done.1.neighbour_ref = bf16[128,512]{1,0:T(8,128)(2,1)S(1)} collective-permute-done((bf16[128,512]{1,0:T(8,128)(2,1)S(1)}, bf16[128,512]{1,0:T(8,128)(2,1)S(1)}, u32[]{:S(2)}, u32[]{:S(2)}) %collective-permute-start.1) | collective-permute-done | bytes 131104 | tf_op jit(solution)/shard_map/ppermute | solution.py:685
  17.7 0.0 copy-start.13
  17.7 4.6 %late.1 = bf16[4,4096]{1,0:T(4,128)(2,1)S(1)} custom-call(f32[2,4,2,128,512]{4,3,2,1,0:T(8,128)S(1)} %copy-done, bf16[128,512]{1,0:T(8,128)(2,1)S(1)} %collective-permute-done.partner_ref, bf16[128,512]{1,0:T(8,128)(2,1)S(1)} %collective-permute-done.1.neighbour_ref, f32[128,512]{1,0:T(8,128)S(1)} %get-tuple-element.22.mix_ref, ...), custom_call_target="tpu_custom_call" | custom-call | tf_op jit(solution)/shard_map/late/pallas_call | solution.py:605
  22.4 0.1 collective-permute-start.2
  22.5 1.2 %collective-permute-done.2 = bf16[4,4096]{1,0:T(4,128)(2,1)S(1)} collective-permute-done((bf16[4,4096]{1,0:T(4,128)(2,1)S(1)}, bf16[4,4096]{1,0:T(4,128)(2,1)S(1)}, u32[]{:S(2)}, u32[]{:S(2)}) %collective-permute-start.2) | collective-permute-done | bytes 32800 | tf_op jit(solution)/shard_map/ppermute | solution.py:659
  23.7 6.4 %collective-permute-start.4 = (bf16[8,4096]{1,0:T(8,128)(2,1)S(1)}, bf16[8,4096]{1,0:T(8,128)(2,1)S(1)}, u32[]{:S(2)}, u32[]{:S(2)}) collective-permute-start(bf16[8,4096]{1,0:T(8,128)(2,1)S(1)} %pad_maximum_fusion.1), channel_id=1, source_target_pairs={{0,12},{2,14},{4,16},{6,18},{8,20},{10,22},{12,24},{14,26},{16,28}... | collective-permute-start | bytes 196616 | tf_op jit(solution)/shard_map/ppermute | solution.py:666
  30.1 2.2 %collective-permute-start.3 = (bf16[8,4096]{1,0:T(8,128)(2,1)S(1)}, bf16[8,4096]{1,0:T(8,128)(2,1)S(1)}, u32[]{:S(2)}, u32[]{:S(2)}) collective-permute-start(bf16[8,4096]{1,0:T(8,128)(2,1)S(1)} %pad_maximum_fusion.1), channel_id=1, source_target_pairs={{0,6},{2,8},{4,10},{6,12},{8,14},{10,16},{12,18},{14,20},{16,22},{... | collective-permute-start | bytes 196616 | tf_op jit(solution)/shard_map/ppermute | solution.py:666
  32.4 3.9 %collective-permute-done.4 = bf16[8,4096]{1,0:T(8,128)(2,1)S(1)} collective-permute-done((bf16[8,4096]{1,0:T(8,128)(2,1)S(1)}, bf16[8,4096]{1,0:T(8,128)(2,1)S(1)}, u32[]{:S(2)}, u32[]{:S(2)}) %collective-permute-start.4) | collective-permute-done | bytes 65568 | tf_op jit(solution)/shard_map/ppermute | solution.py:666
  36.3 0.8 %collective-permute-done.3 = bf16[8,4096]{1,0:T(8,128)(2,1)S(1)} collective-permute-done((bf16[8,4096]{1,0:T(8,128)(2,1)S(1)}, bf16[8,4096]{1,0:T(8,128)(2,1)S(1)}, u32[]{:S(2)}, u32[]{:S(2)}) %collective-permute-start.3) | collective-permute-done | bytes 65568 | tf_op jit(solution)/shard_map/ppermute | solution.py:666
  37.1 0.1 pad_maximum_fusion.refs_1_
  37.2 1.1 %collective-permute-start.5 = (bf16[24,4096]{1,0:T(8,128)(2,1)S(1)}, bf16[24,4096]{1,0:T(8,128)(2,1)S(1)}, u32[]{:S(2)}, u32[]{:S(2)}) collective-permute-start(bf16[24,4096]{1,0:T(8,128)(2,1)S(1)} %pad_maximum_fusion.refs_1_), channel_id=1, source_target_pairs={{0,2},{2,4},{4,6},{6,8},{8,10},{10,12},{12,14},{14,16},{16,18},{18... | collective-permute-start | bytes 589832 | tf_op jit(solution)/shard_map/ppermute | solution.py:666
  38.2 3.7 %collective-permute-start.6 = (bf16[20,4096]{1,0:T(8,128)(2,1)S(1)}, bf16[20,4096]{1,0:T(8,128)(2,1)S(1)}, u32[]{:S(2)}, u32[]{:S(2)}) collective-permute-start(bf16[20,4096]{1,0:T(8,128)(2,1)S(1)} %bitcast.3), channel_id=1, source_target_pairs={{0,4},{2,6},{4,8},{6,10},{8,12},{10,14},{12,16},{14,18},{16,20},{1... | collective-permute-start | bytes 491528 | tf_op jit(solution)/shard_map/ppermute | solution.py:666
  41.9 6.0 %collective-permute-done.6.refs_3_ = bf16[20,4096]{1,0:T(8,128)(2,1)S(1)} collective-permute-done((bf16[20,4096]{1,0:T(8,128)(2,1)S(1)}, bf16[20,4096]{1,0:T(8,128)(2,1)S(1)}, u32[]{:S(2)}, u32[]{:S(2)}) %collective-permute-start.6) | collective-permute-done | bytes 163872 | tf_op jit(solution)/shard_map/ppermute | solution.py:666
  48.0 0.0 collective-permute-done.5.refs_2_
  48.0 0.8 %pick.1 = (f32[32,4096]{1,0:T(8,128)S(1)}, bf16[32,4096]{1,0:T(8,128)(2,1)S(1)}) custom-call(s32[8,128]{1,0:T(8,128)S(1)} %bitcast.4, bf16[24,4096]{1,0:T(8,128)(2,1)S(1)} %pad_maximum_fusion.refs_1_, bf16[24,4096]{1,0:T(8,128)(2,1)S(1)} %collective-permute-done.5.refs_2_, bf16[20,4096]{1,0:T(8,128)(2,1)S(1)} %collective-permute-done.6.refs_3_), custom_call_target="tpu_custom_call" | custom-call | tf_op jit(solution)/shard_map/pick/pallas_call | solution.py:648
  48.7 3.8 %collective-permute-start.7 = (bf16[32,4096]{1,0:T(8,128)(2,1)S(1)}, bf16[32,4096]{1,0:T(8,128)(2,1)S(1)}, u32[]{:S(2)}, u32[]{:S(2)}) collective-permute-start(bf16[32,4096]{1,0:T(8,128)(2,1)S(1)} %get-tuple-element.34), channel_id=1, source_target_pairs={{0,1},{1,0},{2,3},{3,2},{4,5},{5,4},{6,7},{7,6},{8,9},{9,8},{10,11... | collective-permute-start | bytes 786440 | tf_op jit(solution)/shard_map/ppermute | solution.py:659
  52.5 1.2 %collective-permute-done.7 = bf16[32,4096]{1,0:T(8,128)(2,1)S(1)} collective-permute-done((bf16[32,4096]{1,0:T(8,128)(2,1)S(1)}, bf16[32,4096]{1,0:T(8,128)(2,1)S(1)}, u32[]{:S(2)}, u32[]{:S(2)}) %collective-permute-start.7) | collective-permute-done | bytes 262176 | tf_op jit(solution)/shard_map/ppermute | solution.py:659
  53.7 0.8 %convert_add_fusion = f32[32,4096]{1,0:T(8,128)} fusion(f32[32,4096]{1,0:T(8,128)S(1)} %get-tuple-element.33, bf16[32,4096]{1,0:T(8,128)(2,1)S(1)} %collective-permute-done.7), kind=kLoop, calls=%fused_computation | loop fusion | flops 262144 | bytes 1310720 | tf_op jit(solution)/shard_map/add | solution.py:690
  (23 shorter events, 0.1 us)
Async XLA Ops:
  0.0 13.4 %copy-start.5 = (bf16[256,256]{1,0:T(8,128)(2,1)S(1)}, bf16[256,256]{1,0:T(8,128)(2,1)}, u32[]{:S(2)}) copy-start(bf16[256,256]{1,0:T(8,128)(2,1)} %constant.20.clone.x_across_ref) | copy-start | bytes 393220
  0.0 13.4 %copy-start.6 = (bf16[256,256]{1,0:T(8,128)(2,1)S(1)}, bf16[256,256]{1,0:T(8,128)(2,1)}, u32[]{:S(2)}) copy-start(bf16[256,256]{1,0:T(8,128)(2,1)} %constant.19.clone.x_ref) | copy-start | bytes 393220
  0.0 13.4 %copy-start.7 = (bf16[256,256]{1,0:T(8,128)(2,1)S(1)}, bf16[256,256]{1,0:T(8,128)(2,1)}, u32[]{:S(2)}) copy-start(bf16[256,256]{1,0:T(8,128)(2,1)} %constant.18.clone.xx_across_ref) | copy-start | bytes 393220
  0.0 13.4 %copy-start.8 = (bf16[256,256]{1,0:T(8,128)(2,1)S(1)}, bf16[256,256]{1,0:T(8,128)(2,1)}, u32[]{:S(2)}) copy-start(bf16[256,256]{1,0:T(8,128)(2,1)} %constant.17.clone.xx_ref) | copy-start | bytes 393220
  0.0 13.4 %copy-start.11 = (bf16[256,128]{1,0:T(8,128)(2,1)S(1)}, bf16[256,128]{1,0:T(8,128)(2,1)}, u32[]{:S(2)}) copy-start(bf16[256,128]{1,0:T(8,128)(2,1)} %constant.16.clone.own_ref) | copy-start | bytes 196612
  0.0 13.4 %copy-start = (f32[2,4,2,128,512]{4,3,2,1,0:T(8,128)S(1)}, f32[2,4,2,128,512]{4,3,2,1,0:T(8,128)}, u32[]{:S(2)}) copy-start(f32[2,4,2,128,512]{4,3,2,1,0:T(8,128)} %wave_ref.3) | copy-start | bytes 12582916
  0.0 13.4 %copy-start.4 = (f32[128,512]{1,0:T(8,128)S(1)}, f32[128,512]{1,0:T(8,128)}, u32[]{:S(2)}) copy-start(f32[128,512]{1,0:T(8,128)} %tilt_ref.1) | copy-start | bytes 786436
  0.1 13.4 %copy-start.3 = (f32[128,512]{1,0:T(8,128)S(1)}, f32[128,512]{1,0:T(8,128)}, u32[]{:S(2)}) copy-start(f32[128,512]{1,0:T(8,128)} %delta_ref.1) | copy-start | bytes 786436
  0.1 13.4 %copy-start.2 = (f32[128,512]{1,0:T(8,128)S(1)}, f32[128,512]{1,0:T(8,128)}, u32[]{:S(2)}) copy-start(f32[128,512]{1,0:T(8,128)} %eps_ref.1) | copy-start | bytes 786436
  0.1 13.4 %copy-start.1 = (f32[128,512]{1,0:T(8,128)S(1)}, f32[128,512]{1,0:T(8,128)}, u32[]{:S(2)}) copy-start(f32[128,512]{1,0:T(8,128)} %courant_ref.1) | copy-start | bytes 786436
  0.1 13.4 %copy-start.15 = (s32[64]{0:T(128)S(1)}, s32[64]{0:T(128)}, u32[]{:S(2)}) copy-start(s32[64]{0:T(128)} %param.27) | copy-start | bytes 772
  0.1 13.4 %copy-start.14 = (s32[32]{0:T(128)S(1)}, s32[32]{0:T(128)}, u32[]{:S(2)}) copy-start(s32[32]{0:T(128)} %counts_ref.1) | copy-start | bytes 388
  1.4 16.4 %copy-start.9 = (bf16[256,144]{1,0:T(8,128)(2,1)S(1)}, bf16[256,144]{1,0:T(8,128)(2,1)}, u32[]{:S(2)}) copy-start(bf16[256,144]{1,0:T(8,128)(2,1)} %constant.22.clone.two_ref) | copy-start | bytes 221188
  1.4 16.3 %copy-start.10 = (bf16[128,384]{1,0:T(8,128)(2,1)S(1)}, bf16[128,384]{1,0:T(8,128)(2,1)}, u32[]{:S(2)}) copy-start(bf16[128,384]{1,0:T(8,128)(2,1)} %constant.23.clone.depth_ref) | copy-start | bytes 294916
  1.4 16.3 %copy-start.12 = (bf16[64,48]{1,0:T(8,128)(2,1)S(1)}, bf16[64,48]{1,0:T(8,128)(2,1)}, u32[]{:S(2)}) copy-start(bf16[64,48]{1,0:T(8,128)(2,1)} %constant.21.clone.edge_table_ref) | copy-start | bytes 18436
  1.4 15.4 %collective-permute-start = (bf16[128,512]{1,0:T(8,128)(2,1)S(1)}, bf16[128,512]{1,0:T(8,128)(2,1)S(1)}, u32[]{:S(2)}, u32[]{:S(2)}) collective-permute-start(bf16[128,512]{1,0:T(8,128)(2,1)S(1)} %get-tuple-element.20), channel_id=1, source_target_pairs={{0,1},{1,0},{2,3},{3,2},{4,5},{5,4},{6,7},{7,6},{8,9},{9,8},{10,11... | collective-permute-start | bytes 393224 | tf_op jit(solution)/shard_map/ppermute | solution.py:659
  11.4 6.3 %collective-permute-start.1 = (bf16[128,512]{1,0:T(8,128)(2,1)S(1)}, bf16[128,512]{1,0:T(8,128)(2,1)S(1)}, u32[]{:S(2)}, u32[]{:S(2)}) collective-permute-start(bf16[128,512]{1,0:T(8,128)(2,1)S(1)} %get-tuple-element.21), channel_id=1, source_target_pairs={{1,2},{3,4},{5,6},{7,8},{9,10},{11,12},{13,14},{15,16},{17,18},{19... | collective-permute-start | bytes 393224 | tf_op jit(solution)/shard_map/ppermute | solution.py:685
  17.7 30.2 %copy-start.13 = (s32[1024]{0:T(1024)S(1)}, s32[1024]{0:T(1024)}, u32[]{:S(2)}) copy-start(s32[1024]{0:T(1024)} %param.25) | copy-start | bytes 12292
  22.4 1.3 %collective-permute-start.2 = (bf16[4,4096]{1,0:T(4,128)(2,1)S(1)}, bf16[4,4096]{1,0:T(4,128)(2,1)S(1)}, u32[]{:S(2)}, u32[]{:S(2)}) collective-permute-start(bf16[4,4096]{1,0:T(4,128)(2,1)S(1)} %late.1), channel_id=1, source_target_pairs={{0,1},{1,0},{2,3},{3,2},{4,5},{5,4},{6,7},{7,6},{8,9},{9,8},{10,11... | collective-permute-start | bytes 98312 | tf_op jit(solution)/shard_map/ppermute | solution.py:659
  23.7 12.5 %collective-permute-start.4 = (bf16[8,4096]{1,0:T(8,128)(2,1)S(1)}, bf16[8,4096]{1,0:T(8,128)(2,1)S(1)}, u32[]{:S(2)}, u32[]{:S(2)}) collective-permute-start(bf16[8,4096]{1,0:T(8,128)(2,1)S(1)} %pad_maximum_fusion.1), channel_id=1, source_target_pairs={{0,12},{2,14},{4,16},{6,18},{8,20},{10,22},{12,24},{14,26},{16,28}... | collective-permute-start | bytes 196616 | tf_op jit(solution)/shard_map/ppermute | solution.py:666
  30.1 7.0 %collective-permute-start.3 = (bf16[8,4096]{1,0:T(8,128)(2,1)S(1)}, bf16[8,4096]{1,0:T(8,128)(2,1)S(1)}, u32[]{:S(2)}, u32[]{:S(2)}) collective-permute-start(bf16[8,4096]{1,0:T(8,128)(2,1)S(1)} %pad_maximum_fusion.1), channel_id=1, source_target_pairs={{0,6},{2,8},{4,10},{6,12},{8,14},{10,16},{12,18},{14,20},{16,22},{... | collective-permute-start | bytes 196616 | tf_op jit(solution)/shard_map/ppermute | solution.py:666
  37.2 10.8 %collective-permute-start.5 = (bf16[24,4096]{1,0:T(8,128)(2,1)S(1)}, bf16[24,4096]{1,0:T(8,128)(2,1)S(1)}, u32[]{:S(2)}, u32[]{:S(2)}) collective-permute-start(bf16[24,4096]{1,0:T(8,128)(2,1)S(1)} %pad_maximum_fusion.refs_1_), channel_id=1, source_target_pairs={{0,2},{2,4},{4,6},{6,8},{8,10},{10,12},{12,14},{14,16},{16,18},{18... | collective-permute-start | bytes 589832 | tf_op jit(solution)/shard_map/ppermute | solution.py:666
  38.2 9.7 %collective-permute-start.6 = (bf16[20,4096]{1,0:T(8,128)(2,1)S(1)}, bf16[20,4096]{1,0:T(8,128)(2,1)S(1)}, u32[]{:S(2)}, u32[]{:S(2)}) collective-permute-start(bf16[20,4096]{1,0:T(8,128)(2,1)S(1)} %bitcast.3), channel_id=1, source_target_pairs={{0,4},{2,6},{4,8},{6,10},{8,12},{10,14},{12,16},{14,18},{16,20},{1... | collective-permute-start | bytes 491528 | tf_op jit(solution)/shard_map/ppermute | solution.py:666
  48.7 4.9 %collective-permute-start.7 = (bf16[32,4096]{1,0:T(8,128)(2,1)S(1)}, bf16[32,4096]{1,0:T(8,128)(2,1)S(1)}, u32[]{:S(2)}, u32[]{:S(2)}) collective-permute-start(bf16[32,4096]{1,0:T(8,128)(2,1)S(1)} %get-tuple-element.34), channel_id=1, source_target_pairs={{0,1},{1,0},{2,3},{3,2},{4,5},{5,4},{6,7},{7,6},{8,9},{9,8},{10,11... | collective-permute-start | bytes 786440 | tf_op jit(solution)/shard_map/ppermute | solution.py:659

commit v8 on v7

--- a/solution.py
+++ b/solution.py
@@ -613,12 +613,11 @@
     )(*in_vmem(*args))
 
 
-def pick_kernel(loc_ref, *refs, per_slab):
-    held_refs, (mine_ref, theirs_ref) = (refs[:-2], refs[-2:])
+def pick_kernel(loc_ref, *refs, per_slab, count, pieces, begun):
+    held_refs, rest = (refs[: len(pieces)], refs[len(pieces) :])
     slab = lax.axis_index(SLAB)
     chip, core = (lax.axis_index("chip"), lax.axis_index("core"))
     chips = lax.axis_size("chip")
-    count = mine_ref.shape[0]
     per_row = LANES // count
     row = loc_ref[pl.ds(slab // per_row, 1), :]
     spot = slab % per_row
@@ -631,28 +630,42 @@
     up = ahead <= chips // 2
     hops = jnp.where(up, ahead, chips - ahead)
     holder = jnp.where(hops == chips // 2, owner % 2, jnp.where(up, 1, 0))
-    index = (2 * (hops // len(NEAR)) + jnp.where(owner % 2 == holder, 0, 1)) * per_slab + loc % per_slab
-    total = None
-    for near, ref in enumerate(held_refs):
+    far_hops, near_hops = (hops // len(NEAR), hops % len(NEAR))
+    block = 2 * per_slab
+    index = jnp.where(owner % 2 == holder, 0, per_slab) + loc % per_slab
+    index = index + jnp.where(far_hops > 0, far_hops - 1, 0) * block
+    total = rest[0][...] if begun else None
+    for (near, by_far), ref in zip(pieces, held_refs, strict=True):
         held = lax.broadcasted_iota(jnp.int32, (ref.shape[0], 2 * count), 0)
-        hit = (held == index) & (holder == core) & (hops % len(NEAR) == near)
+        hit = (held == index) & (holder == core) & (near_hops == near) & ((far_hops > 0) == by_far)
         hot = jnp.where(hit, 1.0, 0.0).astype(BF16)
         part = lax.dot_general(hot, ref[...], (((0,), (0,)), ((), ())), preferred_element_type=F32)
         total = part if total is None else total + part
-    mine_ref[...] = total[:count]
-    theirs_ref[...] = total[count:].astype(BF16)
-
-
-def pick(loc_patch, held, count, per_slab):
-    width = held[0].shape[1]
+    if begun:
+        mine_ref, theirs_ref = rest[1:]
+        mine_ref[...] = total[:count]
+        theirs_ref[...] = total[count:].astype(BF16)
+    else:
+        rest[0][...] = total
+
+
+def pick(loc_patch, held, count, per_slab, begun=None):
+    width = held[0][2].shape[1]
+    pieces = [h[:2] for h in held]
+    args = [loc_patch.reshape(-1, LANES)] + [h[2] for h in held] + ([] if begun is None else [begun])
+    outs = [pltpu.VMEM((2 * count, width), F32)]
+    if begun is not None:
+        outs = [pltpu.VMEM((count, width), F32), pltpu.VMEM((count, width), BF16)]
     return pl.pallas_call(
-        lambda *refs: pick_kernel(*refs, per_slab=per_slab),
-        in_specs=[VMEM_WHOLE] * (1 + len(held)),
-        out_specs=[VMEM_WHOLE] * 2,
-        out_shape=[pltpu.VMEM((count, width), F32), pltpu.VMEM((count, width), BF16)],
+        lambda *refs: pick_kernel(
+            *refs, per_slab=per_slab, count=count, pieces=pieces, begun=begun is not None
+        ),
+        in_specs=[VMEM_WHOLE] * len(args),
+        out_specs=[VMEM_WHOLE] * len(outs),
+        out_shape=outs,
         compiler_params=pltpu.CompilerParams(vmem_limit_bytes=8 << 20),
         name="pick",
-    )(*in_vmem(loc_patch.reshape(-1, LANES), *held))
+    )(*in_vmem(*args))
 
 
 def swap_cores(array):
@@ -667,10 +680,17 @@
 
 
 def spread(images):
-    held = jnp.concatenate([images, swap_cores(images)])
-    held = jnp.concatenate([held] + [onward(held, h) for h in FAR[1:]])
-    short = held[: held.shape[0] - images.shape[0]]
-    return [held] + [onward(short if h == NEAR[-1] else held, h) for h in NEAR[1:]]
+    count = images.shape[0]
+    chip = jnp.concatenate([images, swap_cores(images)])
+    far = [onward(chip, h) for h in FAR[1:]]
+    near = [onward(chip, h) for h in NEAR[1:]]
+    came = jnp.concatenate(far)
+    short = came[: came.shape[0] - count]
+    both = [onward(short if h == NEAR[-1] else came, h) for h in NEAR[1:]]
+    return (
+        [(n, False, a) for n, a in enumerate([chip] + near)],
+        [(n, True, a) for n, a in enumerate([came] + both)],
+    )
 
 
 def per_device(
@@ -686,7 +706,10 @@
     partner = swap_cores(to_partner)
     prepared = early(wavefields, params, slab_counts, angle_table)
     images = late(wavefields, partner, neighbour, prepared, angle_table.shape[0])
-    mine, theirs = pick(loc_patch, spread(images), loc_patch.shape[0] // slabs, per_slab)
+    close, distant = spread(images)
+    count = loc_patch.shape[0] // slabs
+    (begun,) = pick(loc_patch, close, count, per_slab)
+    mine, theirs = pick(loc_patch, distant, count, per_slab, begun)
     return mine + swap_cores(theirs).astype(F32)
 
 

time: 54.6 us -> 55 us (level)
  starting transfers between devices: 29.3 us -> 27.7 us
  waiting for transfers between devices: 14 us -> 15.2 us
  Pallas kernels: 9.98 us -> 10.8 us
    ppermute x3, starting transfers between devices: 13.9 us -> 10.6 us  [swap_cores(): return lax.ppermute(array, 'core', [(0, 1), (1, 0)])]
    ppermute x4 -> x6, starting transfers between devices: 13.4 us -> 15.1 us  [onward(): return lax.ppermute(array, SLAB, pairs)]
    ppermute x4 -> x6, waiting for transfers between devices: 10.7 us -> 12 us  [onward(): return lax.ppermute(array, SLAB, pairs)]
    pallas_call x1 -> x2, Pallas kernels: 0.77 us -> 1.55 us  [pick(): pl.pallas_call(lambda *refs: pick_kernel(*refs, per_slab=per_slab, count=...]
  transfers between devices with their start and end apart: 8 -> 10, of which waited for: 6 -> 6; matrix products, arithmetic and copies ran while one was open for 0% -> 0% of each run, Pallas kernels for 6% -> 7%
where the time goes in v8:
time: 55 us; the launch traced here: 54.9 us
  starting transfers between devices  27.7 us (50%)
  waiting for transfers between devices  15.2 us (28%)
  Pallas kernels  10.8 us (20%)
  other arithmetic  0.88 us (2%)
    ppermute x6, starting transfers between devices, onward(): return lax.ppermute(array, SLAB, pairs)  15.1 us
    ppermute x6, waiting for transfers between devices, onward(): return lax.ppermute(array, SLAB, pairs)  12 us
    ppermute x3, starting transfers between devices, swap_cores(): return lax.ppermute(array, 'core', [(0, 1), (1, 0)])  10.6 us
    pallas_call x1, Pallas kernels, late(): pl.pallas_call(late_kernel, in_specs=[VMEM_WHOLE] * len(args), out_specs=...  4.63 us
    pallas_call x1, Pallas kernels, early(): pl.pallas_call(early_kernel, in_specs=[pl.BlockSpec(memory_space=pltpu.SM...  3.33 us
    ppermute x3, waiting for transfers between devices, swap_cores(): return lax.ppermute(array, 'core', [(0, 1), (1, 0)])  2.35 us
    ppermute x1, starting transfers between devices, per_device(): lax.ppermute(to_neighbour, SLAB, pairs + [(j, i) for i, j in pairs])  1.94 us
    pallas_call x2, Pallas kernels, pick(): pl.pallas_call(lambda *refs: pick_kernel(*refs, per_slab=per_slab, count=...  1.55 us
  transfers between devices with their start and end apart: 10, of which 6 were waited for; matrix products, arithmetic and copies ran while one was open for 0% of the time, Pallas kernels for 7%

profile of v8, /device:TPU:69, one launch (start us, length us, event | category | flops | bytes accessed | tf_op | source)
XLA Modules:
  0.0 54.9 jit_solution(18082099578767093254)
XLA Ops:
  0.0 0.0 copy-start.8
  0.0 0.0 copy-start.11
  0.1 1.2 %pack.1 = (bf16[128,512]{1,0:T(8,128)(2,1)S(1)}, bf16[128,512]{1,0:T(8,128)(2,1)S(1)}) custom-call(f32[2,4,2,128,512]{4,3,2,1,0:T(8,128)} %wave_ref.3, f32[2,4,2,128,512]{4,3,2,1,0:T(8,128)} %wave_ref.3, f32[128,512]{1,0:T(8,128)} %courant_ref.1, f32[128,512]{1,0:T(8,128)} %courant_ref.1, f32[128,512]{1,0:T(8,128)} %eps_ref.1, f32[128,512]{1,0:T(8,128)} %eps_ref.1, ...), custom_call_target="tpu_custom_call" | custom-call | tf_op jit(solution)/shard_map/pack/pallas_call | solution.py:164
  1.4 0.0 copy-start.9
  1.4 0.0 copy-start.10
  1.4 0.0 copy-start.12
  1.4 10.0 %collective-permute-start = (bf16[128,512]{1,0:T(8,128)(2,1)S(1)}, bf16[128,512]{1,0:T(8,128)(2,1)S(1)}, u32[]{:S(2)}, u32[]{:S(2)}) collective-permute-start(bf16[128,512]{1,0:T(8,128)(2,1)S(1)} %get-tuple-element.20), channel_id=1, source_target_pairs={{0,1},{1,0},{2,3},{3,2},{4,5},{5,4},{6,7},{7,6},{8,9},{9,8},{10,11... | collective-permute-start | bytes 393224 | tf_op jit(solution)/shard_map/ppermute | solution.py:672
  11.4 1.9 %collective-permute-start.1 = (bf16[128,512]{1,0:T(8,128)(2,1)S(1)}, bf16[128,512]{1,0:T(8,128)(2,1)S(1)}, u32[]{:S(2)}, u32[]{:S(2)}) collective-permute-start(bf16[128,512]{1,0:T(8,128)(2,1)S(1)} %get-tuple-element.21), channel_id=1, source_target_pairs={{1,2},{3,4},{5,6},{7,8},{9,10},{11,12},{13,14},{15,16},{17,18},{19... | collective-permute-start | bytes 393224 | tf_op jit(solution)/shard_map/ppermute | solution.py:705
  13.5 3.3 %early.1 = (f32[128,512]{1,0:T(8,128)S(1)}, f32[128,512]{1,0:T(8,128)S(1)}, f32[128,512]{1,0:T(8,128)S(1)}, f32[128,512]{1,0:T(8,128)S(1)}, f32[128,512]{1,0:T(8...) custom-call(s32[32]{0:T(128)S(1)} %copy-done.14, ...), custom_call_target="tpu_custom_call" | custom-call | tf_op jit(solution)/shard_map/early/pallas_call | solution.py:558
  16.8 0.0 collective-permute-done.partner_ref
  16.8 0.9 %collective-permute-done.1.neighbour_ref = bf16[128,512]{1,0:T(8,128)(2,1)S(1)} collective-permute-done((bf16[128,512]{1,0:T(8,128)(2,1)S(1)}, bf16[128,512]{1,0:T(8,128)(2,1)S(1)}, u32[]{:S(2)}, u32[]{:S(2)}) %collective-permute-start.1) | collective-permute-done | bytes 131104 | tf_op jit(solution)/shard_map/ppermute | solution.py:705
  17.7 0.0 copy-start.13
  17.7 4.6 %late.1 = bf16[4,4096]{1,0:T(4,128)(2,1)S(1)} custom-call(f32[2,4,2,128,512]{4,3,2,1,0:T(8,128)S(1)} %copy-done, bf16[128,512]{1,0:T(8,128)(2,1)S(1)} %collective-permute-done.partner_ref, bf16[128,512]{1,0:T(8,128)(2,1)S(1)} %collective-permute-done.1.neighbour_ref, f32[128,512]{1,0:T(8,128)S(1)} %get-tuple-element.22.mix_ref, ...), custom_call_target="tpu_custom_call" | custom-call | tf_op jit(solution)/shard_map/late/pallas_call | solution.py:605
  22.4 0.1 collective-permute-start.2
  22.5 1.2 %collective-permute-done.2 = bf16[4,4096]{1,0:T(4,128)(2,1)S(1)} collective-permute-done((bf16[4,4096]{1,0:T(4,128)(2,1)S(1)}, bf16[4,4096]{1,0:T(4,128)(2,1)S(1)}, u32[]{:S(2)}, u32[]{:S(2)}) %collective-permute-start.2) | collective-permute-done | bytes 32800 | tf_op jit(solution)/shard_map/ppermute | solution.py:672
  23.7 4.5 %collective-permute-start.3 = (bf16[8,4096]{1,0:T(8,128)(2,1)S(1)}, bf16[8,4096]{1,0:T(8,128)(2,1)S(1)}, u32[]{:S(2)}, u32[]{:S(2)}) collective-permute-start(bf16[8,4096]{1,0:T(8,128)(2,1)S(1)} %pad_maximum_fusion.refs_1_), channel_id=1, source_target_pairs={{0,6},{2,8},{4,10},{6,12},{8,14},{10,16},{12,18},{14,20},{16,22},{... | collective-permute-start | bytes 196616 | tf_op jit(solution)/shard_map/ppermute | solution.py:679
  28.2 4.1 %collective-permute-start.4 = (bf16[8,4096]{1,0:T(8,128)(2,1)S(1)}, bf16[8,4096]{1,0:T(8,128)(2,1)S(1)}, u32[]{:S(2)}, u32[]{:S(2)}) collective-permute-start(bf16[8,4096]{1,0:T(8,128)(2,1)S(1)} %pad_maximum_fusion.refs_1_), channel_id=1, source_target_pairs={{0,12},{2,14},{4,16},{6,18},{8,20},{10,22},{12,24},{14,26},{16,28}... | collective-permute-start | bytes 196616 | tf_op jit(solution)/shard_map/ppermute | solution.py:679
  32.4 0.0 collective-permute-done.3
  32.4 6.5 %collective-permute-done.4 = bf16[8,4096]{1,0:T(8,128)(2,1)S(1)} collective-permute-done((bf16[8,4096]{1,0:T(8,128)(2,1)S(1)}, bf16[8,4096]{1,0:T(8,128)(2,1)S(1)}, u32[]{:S(2)}, u32[]{:S(2)}) %collective-permute-start.4) | collective-permute-done | bytes 65568 | tf_op jit(solution)/shard_map/ppermute | solution.py:679
  38.9 4.2 %collective-permute-start.5 = (bf16[16,4096]{1,0:T(8,128)(2,1)S(1)}, bf16[16,4096]{1,0:T(8,128)(2,1)S(1)}, u32[]{:S(2)}, u32[]{:S(2)}) collective-permute-start(bf16[16,4096]{1,0:T(8,128)(2,1)S(1)} %constant_dynamic-update-slice_fusion.refs_1_), channel_id=1, source_target_pairs={{0,2},{2,4},{4,6},{6,8},{8,10},{10,12},{12,14},{14,16},{16,18},{18... | collective-permute-start | bytes 393224 | tf_op jit(solution)/shard_map/ppermute | solution.py:679
  43.1 0.4 collective-permute-start.6
  43.5 0.1 collective-permute-start.8
  43.7 1.7 %collective-permute-start.7 = (bf16[8,4096]{1,0:T(8,128)(2,1)S(1)}, bf16[8,4096]{1,0:T(8,128)(2,1)S(1)}, u32[]{:S(2)}, u32[]{:S(2)}) collective-permute-start(bf16[8,4096]{1,0:T(8,128)(2,1)S(1)} %pad_maximum_fusion.refs_1_), channel_id=1, source_target_pairs={{0,2},{2,4},{4,6},{6,8},{8,10},{10,12},{12,14},{14,16},{16,18},{18... | collective-permute-start | bytes 196616 | tf_op jit(solution)/shard_map/ppermute | solution.py:679
  45.4 4.4 %collective-permute-done.8.refs_3_ = bf16[8,4096]{1,0:T(8,128)(2,1)S(1)} collective-permute-done((bf16[8,4096]{1,0:T(8,128)(2,1)S(1)}, bf16[8,4096]{1,0:T(8,128)(2,1)S(1)}, u32[]{:S(2)}, u32[]{:S(2)}) %collective-permute-start.8) | collective-permute-done | bytes 65568 | tf_op jit(solution)/shard_map/ppermute | solution.py:679
  49.8 1.0 %collective-permute-done.7.refs_2_ = bf16[8,4096]{1,0:T(8,128)(2,1)S(1)} collective-permute-done((bf16[8,4096]{1,0:T(8,128)(2,1)S(1)}, bf16[8,4096]{1,0:T(8,128)(2,1)S(1)}, u32[]{:S(2)}, u32[]{:S(2)}) %collective-permute-start.7) | collective-permute-done | bytes 65568 | tf_op jit(solution)/shard_map/ppermute | solution.py:679
  50.8 0.8 %pick.2.refs_4_ = f32[64,4096]{1,0:T(8,128)S(1)} custom-call(s32[8,128]{1,0:T(8,128)S(1)} %bitcast.4, bf16[8,4096]{1,0:T(8,128)(2,1)S(1)} %pad_maximum_fusion.refs_1_, bf16[8,4096]{1,0:T(8,128)(2,1)S(1)} %collective-permute-done.7.refs_2_, bf16[8,4096]{1,0:T(8,128)(2,1)S(1)} %collective-permute-done.8.refs_3_), custom_call_target="tpu_custom_call" | custom-call | tf_op jit(solution)/shard_map/pick/pallas_call | solution.py:659
  51.6 0.0 collective-permute-done.6.refs_3_
  51.6 0.0 collective-permute-done.5.refs_2_
  51.6 0.8 %pick.3 = (f32[32,4096]{1,0:T(8,128)S(1)}, bf16[32,4096]{1,0:T(8,128)(2,1)S(1)}) custom-call(s32[8,128]{1,0:T(8,128)S(1)} %bitcast.5, bf16[16,4096]{1,0:T(8,128)(2,1)S(1)} %constant_dynamic-update-slice_fusion.refs_1_, bf16[16,4096]{1,0:T(8,128)(2,1)S(1)} %collective-permute-done.5.refs_2_, bf16[12,4096]{1,0:T(8,128)(2,1)S(1)} %collective-permute-done.6.refs_3_, ...), custom_call_target="tpu_custom_call" | custom-call | tf_op jit(solution)/shard_map/pick/pallas_call | solution.py:659
  52.4 0.5 collective-permute-start.9
  52.9 1.2 %collective-permute-done.9 = bf16[32,4096]{1,0:T(8,128)(2,1)S(1)} collective-permute-done((bf16[32,4096]{1,0:T(8,128)(2,1)S(1)}, bf16[32,4096]{1,0:T(8,128)(2,1)S(1)}, u32[]{:S(2)}, u32[]{:S(2)}) %collective-permute-start.9) | collective-permute-done | bytes 262176 | tf_op jit(solution)/shard_map/ppermute | solution.py:672
  54.0 0.8 %convert_add_fusion = f32[32,4096]{1,0:T(8,128)} fusion(f32[32,4096]{1,0:T(8,128)S(1)} %get-tuple-element.33, bf16[32,4096]{1,0:T(8,128)(2,1)S(1)} %collective-permute-done.9), kind=kLoop, calls=%fused_computation | loop fusion | flops 262144 | bytes 1310720 | tf_op jit(solution)/shard_map/add | solution.py:713
  (29 shorter events, 0.1 us)
Async XLA Ops:
  0.0 13.4 %copy-start.5 = (bf16[256,256]{1,0:T(8,128)(2,1)S(1)}, bf16[256,256]{1,0:T(8,128)(2,1)}, u32[]{:S(2)}) copy-start(bf16[256,256]{1,0:T(8,128)(2,1)} %constant.20.clone.x_across_ref) | copy-start | bytes 393220
  0.0 13.4 %copy-start.6 = (bf16[256,256]{1,0:T(8,128)(2,1)S(1)}, bf16[256,256]{1,0:T(8,128)(2,1)}, u32[]{:S(2)}) copy-start(bf16[256,256]{1,0:T(8,128)(2,1)} %constant.19.clone.x_ref) | copy-start | bytes 393220
  0.0 13.4 %copy-start.7 = (bf16[256,256]{1,0:T(8,128)(2,1)S(1)}, bf16[256,256]{1,0:T(8,128)(2,1)}, u32[]{:S(2)}) copy-start(bf16[256,256]{1,0:T(8,128)(2,1)} %constant.18.clone.xx_across_ref) | copy-start | bytes 393220
  0.0 13.4 %copy-start.8 = (bf16[256,256]{1,0:T(8,128)(2,1)S(1)}, bf16[256,256]{1,0:T(8,128)(2,1)}, u32[]{:S(2)}) copy-start(bf16[256,256]{1,0:T(8,128)(2,1)} %constant.17.clone.xx_ref) | copy-start | bytes 393220
  0.0 13.4 %copy-start.11 = (bf16[256,128]{1,0:T(8,128)(2,1)S(1)}, bf16[256,128]{1,0:T(8,128)(2,1)}, u32[]{:S(2)}) copy-start(bf16[256,128]{1,0:T(8,128)(2,1)} %constant.16.clone.own_ref) | copy-start | bytes 196612
  0.0 13.4 %copy-start = (f32[2,4,2,128,512]{4,3,2,1,0:T(8,128)S(1)}, f32[2,4,2,128,512]{4,3,2,1,0:T(8,128)}, u32[]{:S(2)}) copy-start(f32[2,4,2,128,512]{4,3,2,1,0:T(8,128)} %wave_ref.3) | copy-start | bytes 12582916
  0.0 13.4 %copy-start.4 = (f32[128,512]{1,0:T(8,128)S(1)}, f32[128,512]{1,0:T(8,128)}, u32[]{:S(2)}) copy-start(f32[128,512]{1,0:T(8,128)} %tilt_ref.1) | copy-start | bytes 786436
  0.1 13.4 %copy-start.3 = (f32[128,512]{1,0:T(8,128)S(1)}, f32[128,512]{1,0:T(8,128)}, u32[]{:S(2)}) copy-start(f32[128,512]{1,0:T(8,128)} %delta_ref.1) | copy-start | bytes 786436
  0.1 13.4 %copy-start.2 = (f32[128,512]{1,0:T(8,128)S(1)}, f32[128,512]{1,0:T(8,128)}, u32[]{:S(2)}) copy-start(f32[128,512]{1,0:T(8,128)} %eps_ref.1) | copy-start | bytes 786436
  0.1 13.4 %copy-start.1 = (f32[128,512]{1,0:T(8,128)S(1)}, f32[128,512]{1,0:T(8,128)}, u32[]{:S(2)}) copy-start(f32[128,512]{1,0:T(8,128)} %courant_ref.1) | copy-start | bytes 786436
  0.1 13.4 %copy-start.15 = (s32[64]{0:T(128)S(1)}, s32[64]{0:T(128)}, u32[]{:S(2)}) copy-start(s32[64]{0:T(128)} %param.27) | copy-start | bytes 772
  0.1 13.4 %copy-start.14 = (s32[32]{0:T(128)S(1)}, s32[32]{0:T(128)}, u32[]{:S(2)}) copy-start(s32[32]{0:T(128)} %counts_ref.1) | copy-start | bytes 388
  1.4 16.4 %copy-start.9 = (bf16[256,144]{1,0:T(8,128)(2,1)S(1)}, bf16[256,144]{1,0:T(8,128)(2,1)}, u32[]{:S(2)}) copy-start(bf16[256,144]{1,0:T(8,128)(2,1)} %constant.22.clone.two_ref) | copy-start | bytes 221188
  1.4 16.3 %copy-start.10 = (bf16[128,384]{1,0:T(8,128)(2,1)S(1)}, bf16[128,384]{1,0:T(8,128)(2,1)}, u32[]{:S(2)}) copy-start(bf16[128,384]{1,0:T(8,128)(2,1)} %constant.23.clone.depth_ref) | copy-start | bytes 294916
  1.4 16.3 %copy-start.12 = (bf16[64,48]{1,0:T(8,128)(2,1)S(1)}, bf16[64,48]{1,0:T(8,128)(2,1)}, u32[]{:S(2)}) copy-start(bf16[64,48]{1,0:T(8,128)(2,1)} %constant.21.clone.edge_table_ref) | copy-start | bytes 18436
  1.4 15.4 %collective-permute-start = (bf16[128,512]{1,0:T(8,128)(2,1)S(1)}, bf16[128,512]{1,0:T(8,128)(2,1)S(1)}, u32[]{:S(2)}, u32[]{:S(2)}) collective-permute-start(bf16[128,512]{1,0:T(8,128)(2,1)S(1)} %get-tuple-element.20), channel_id=1, source_target_pairs={{0,1},{1,0},{2,3},{3,2},{4,5},{5,4},{6,7},{7,6},{8,9},{9,8},{10,11... | collective-permute-start | bytes 393224 | tf_op jit(solution)/shard_map/ppermute | solution.py:672
  11.4 6.3 %collective-permute-start.1 = (bf16[128,512]{1,0:T(8,128)(2,1)S(1)}, bf16[128,512]{1,0:T(8,128)(2,1)S(1)}, u32[]{:S(2)}, u32[]{:S(2)}) collective-permute-start(bf16[128,512]{1,0:T(8,128)(2,1)S(1)} %get-tuple-element.21), channel_id=1, source_target_pairs={{1,2},{3,4},{5,6},{7,8},{9,10},{11,12},{13,14},{15,16},{17,18},{19... | collective-permute-start | bytes 393224 | tf_op jit(solution)/shard_map/ppermute | solution.py:705
  17.7 33.1 %copy-start.13 = (s32[1024]{0:T(1024)S(1)}, s32[1024]{0:T(1024)}, u32[]{:S(2)}) copy-start(s32[1024]{0:T(1024)} %param.25) | copy-start | bytes 12292
  22.4 1.3 %collective-permute-start.2 = (bf16[4,4096]{1,0:T(4,128)(2,1)S(1)}, bf16[4,4096]{1,0:T(4,128)(2,1)S(1)}, u32[]{:S(2)}, u32[]{:S(2)}) collective-permute-start(bf16[4,4096]{1,0:T(4,128)(2,1)S(1)} %late.1), channel_id=1, source_target_pairs={{0,1},{1,0},{2,3},{3,2},{4,5},{5,4},{6,7},{7,6},{8,9},{9,8},{10,11... | collective-permute-start | bytes 98312 | tf_op jit(solution)/shard_map/ppermute | solution.py:672
  23.7 8.7 %collective-permute-start.3 = (bf16[8,4096]{1,0:T(8,128)(2,1)S(1)}, bf16[8,4096]{1,0:T(8,128)(2,1)S(1)}, u32[]{:S(2)}, u32[]{:S(2)}) collective-permute-start(bf16[8,4096]{1,0:T(8,128)(2,1)S(1)} %pad_maximum_fusion.refs_1_), channel_id=1, source_target_pairs={{0,6},{2,8},{4,10},{6,12},{8,14},{10,16},{12,18},{14,20},{16,22},{... | collective-permute-start | bytes 196616 | tf_op jit(solution)/shard_map/ppermute | solution.py:679
  28.2 10.7 %collective-permute-start.4 = (bf16[8,4096]{1,0:T(8,128)(2,1)S(1)}, bf16[8,4096]{1,0:T(8,128)(2,1)S(1)}, u32[]{:S(2)}, u32[]{:S(2)}) collective-permute-start(bf16[8,4096]{1,0:T(8,128)(2,1)S(1)} %pad_maximum_fusion.refs_1_), channel_id=1, source_target_pairs={{0,12},{2,14},{4,16},{6,18},{8,20},{10,22},{12,24},{14,26},{16,28}... | collective-permute-start | bytes 196616 | tf_op jit(solution)/shard_map/ppermute | solution.py:679
  38.9 12.7 %collective-permute-start.5 = (bf16[16,4096]{1,0:T(8,128)(2,1)S(1)}, bf16[16,4096]{1,0:T(8,128)(2,1)S(1)}, u32[]{:S(2)}, u32[]{:S(2)}) collective-permute-start(bf16[16,4096]{1,0:T(8,128)(2,1)S(1)} %constant_dynamic-update-slice_fusion.refs_1_), channel_id=1, source_target_pairs={{0,2},{2,4},{4,6},{6,8},{8,10},{10,12},{12,14},{14,16},{16,18},{18... | collective-permute-start | bytes 393224 | tf_op jit(solution)/shard_map/ppermute | solution.py:679
  43.1 8.4 %collective-permute-start.6 = (bf16[12,4096]{1,0:T(8,128)(2,1)S(1)}, bf16[12,4096]{1,0:T(8,128)(2,1)S(1)}, u32[]{:S(2)}, u32[]{:S(2)}) collective-permute-start(bf16[12,4096]{1,0:T(8,128)(2,1)S(1)} %bitcast.3), channel_id=1, source_target_pairs={{0,4},{2,6},{4,8},{6,10},{8,12},{10,14},{12,16},{14,18},{16,20},{1... | collective-permute-start | bytes 294920 | tf_op jit(solution)/shard_map/ppermute | solution.py:679
  43.5 6.2 %collective-permute-start.8 = (bf16[8,4096]{1,0:T(8,128)(2,1)S(1)}, bf16[8,4096]{1,0:T(8,128)(2,1)S(1)}, u32[]{:S(2)}, u32[]{:S(2)}) collective-permute-start(bf16[8,4096]{1,0:T(8,128)(2,1)S(1)} %pad_maximum_fusion.refs_1_), channel_id=1, source_target_pairs={{0,4},{2,6},{4,8},{6,10},{8,12},{10,14},{12,16},{14,18},{16,20},{1... | collective-permute-start | bytes 196616 | tf_op jit(solution)/shard_map/ppermute | solution.py:679
  43.7 7.1 %collective-permute-start.7 = (bf16[8,4096]{1,0:T(8,128)(2,1)S(1)}, bf16[8,4096]{1,0:T(8,128)(2,1)S(1)}, u32[]{:S(2)}, u32[]{:S(2)}) collective-permute-start(bf16[8,4096]{1,0:T(8,128)(2,1)S(1)} %pad_maximum_fusion.refs_1_), channel_id=1, source_target_pairs={{0,2},{2,4},{4,6},{6,8},{8,10},{10,12},{12,14},{14,16},{16,18},{18... | collective-permute-start | bytes 196616 | tf_op jit(solution)/shard_map/ppermute | solution.py:679
  52.4 1.7 %collective-permute-start.9 = (bf16[32,4096]{1,0:T(8,128)(2,1)S(1)}, bf16[32,4096]{1,0:T(8,128)(2,1)S(1)}, u32[]{:S(2)}, u32[]{:S(2)}) collective-permute-start(bf16[32,4096]{1,0:T(8,128)(2,1)S(1)} %get-tuple-element.34), channel_id=1, source_target_pairs={{0,1},{1,0},{2,3},{3,2},{4,5},{5,4},{6,7},{7,6},{8,9},{9,8},{10,11... | collective-permute-start | bytes 786440 | tf_op jit(solution)/shard_map/ppermute | solution.py:672

commit v9 on v7

--- a/solution.py
+++ b/solution.py
@@ -630,7 +630,7 @@
     ahead = lax.rem(owner // 2 - chip + chips, chips)
     up = ahead <= chips // 2
     hops = jnp.where(up, ahead, chips - ahead)
-    holder = jnp.where(hops == chips // 2, owner % 2, jnp.where(up, 1, 0))
+    holder = jnp.where(up, 1, 0)
     index = (2 * (hops // len(NEAR)) + jnp.where(owner % 2 == holder, 0, 1)) * per_slab + loc % per_slab
     total = None
     for near, ref in enumerate(held_refs):
@@ -669,8 +669,7 @@
 def spread(images):
     held = jnp.concatenate([images, swap_cores(images)])
     held = jnp.concatenate([held] + [onward(held, h) for h in FAR[1:]])
-    short = held[: held.shape[0] - images.shape[0]]
-    return [held] + [onward(short if h == NEAR[-1] else held, h) for h in NEAR[1:]]
+    return [held] + [onward(held, h) for h in NEAR[1:]]
 
 
 def per_device(

time: 54.6 us -> 51.5 us (0.943)
  starting transfers between devices: 29.3 us -> 25.6 us
    ppermute x3, starting transfers between devices: 13.9 us -> 10.4 us  [swap_cores(): return lax.ppermute(array, 'core', [(0, 1), (1, 0)])]
  transfers between devices with their start and end apart: 8 -> 8, of which waited for: 6 -> 7; matrix products, arithmetic and copies ran while one was open for 0% -> 0% of each run, Pallas kernels for 6% -> 6%
where the time goes in v9:
time: 51.5 us; the launch traced here: 51.4 us
  starting transfers between devices  25.6 us (50%)
  waiting for transfers between devices  14.5 us (28%)
  Pallas kernels  9.99 us (19%)
  other arithmetic  0.93 us (2%)
    ppermute x4, starting transfers between devices, onward(): return lax.ppermute(array, SLAB, pairs)  13.3 us
    ppermute x4, waiting for transfers between devices, onward(): return lax.ppermute(array, SLAB, pairs)  11 us
    ppermute x3, starting transfers between devices, swap_cores(): return lax.ppermute(array, 'core', [(0, 1), (1, 0)])  10.4 us
    pallas_call x1, Pallas kernels, late(): pl.pallas_call(late_kernel, in_specs=[VMEM_WHOLE] * len(args), out_specs=...  4.63 us
    pallas_call x1, Pallas kernels, early(): pl.pallas_call(early_kernel, in_specs=[pl.BlockSpec(memory_space=pltpu.SM...  3.33 us
    ppermute x3, waiting for transfers between devices, swap_cores(): return lax.ppermute(array, 'core', [(0, 1), (1, 0)])  2.57 us
    ppermute x1, starting transfers between devices, per_device(): lax.ppermute(to_neighbour, SLAB, pairs + [(j, i) for i, j in pairs])  1.94 us
    pallas_call x1, Pallas kernels, pack(): pl.pallas_call(pack_kernel, grid=(1,), in_specs=specs, out_specs=[VMEM_WH...  1.25 us
  transfers between devices with their start and end apart: 8, of which 7 were waited for; matrix products, arithmetic and copies ran while one was open for 0% of the time, Pallas kernels for 6%

profile of v9, /device:TPU:69, one launch (start us, length us, event | category | flops | bytes accessed | tf_op | source)
XLA Modules:
  0.0 51.4 jit_solution(14414575464754437855)
XLA Ops:
  0.0 0.0 copy-start.8
  0.0 0.0 copy-start.11
  0.0 0.0 copy-start
  0.0 0.0 copy-start.4
  0.1 0.0 copy-start.3
  0.1 0.0 copy-start.2
  0.1 1.2 %pack.1 = (bf16[128,512]{1,0:T(8,128)(2,1)S(1)}, bf16[128,512]{1,0:T(8,128)(2,1)S(1)}) custom-call(f32[2,4,2,128,512]{4,3,2,1,0:T(8,128)} %wave_ref.3, f32[2,4,2,128,512]{4,3,2,1,0:T(8,128)} %wave_ref.3, f32[128,512]{1,0:T(8,128)} %courant_ref.1, f32[128,512]{1,0:T(8,128)} %courant_ref.1, f32[128,512]{1,0:T(8,128)} %eps_ref.1, f32[128,512]{1,0:T(8,128)} %eps_ref.1, ...), custom_call_target="tpu_custom_call" | custom-call | tf_op jit(solution)/shard_map/pack/pallas_call | solution.py:164
  1.4 0.0 copy-start.9
  1.4 0.0 copy-start.10
  1.4 0.0 copy-start.12
  1.4 10.0 %collective-permute-start = (bf16[128,512]{1,0:T(8,128)(2,1)S(1)}, bf16[128,512]{1,0:T(8,128)(2,1)S(1)}, u32[]{:S(2)}, u32[]{:S(2)}) collective-permute-start(bf16[128,512]{1,0:T(8,128)(2,1)S(1)} %get-tuple-element.20), channel_id=1, source_target_pairs={{0,1},{1,0},{2,3},{3,2},{4,5},{5,4},{6,7},{7,6},{8,9},{9,8},{10,11... | collective-permute-start | bytes 393224 | tf_op jit(solution)/shard_map/ppermute | solution.py:659
  11.4 1.9 %collective-permute-start.1 = (bf16[128,512]{1,0:T(8,128)(2,1)S(1)}, bf16[128,512]{1,0:T(8,128)(2,1)S(1)}, u32[]{:S(2)}, u32[]{:S(2)}) collective-permute-start(bf16[128,512]{1,0:T(8,128)(2,1)S(1)} %get-tuple-element.21), channel_id=1, source_target_pairs={{1,2},{3,4},{5,6},{7,8},{9,10},{11,12},{13,14},{15,16},{17,18},{19... | collective-permute-start | bytes 393224 | tf_op jit(solution)/shard_map/ppermute | solution.py:684
  13.5 3.3 %early.1 = (f32[128,512]{1,0:T(8,128)S(1)}, f32[128,512]{1,0:T(8,128)S(1)}, f32[128,512]{1,0:T(8,128)S(1)}, f32[128,512]{1,0:T(8,128)S(1)}, f32[128,512]{1,0:T(8...) custom-call(s32[32]{0:T(128)S(1)} %copy-done.14, ...), custom_call_target="tpu_custom_call" | custom-call | tf_op jit(solution)/shard_map/early/pallas_call | solution.py:558
  16.8 0.0 collective-permute-done.partner_ref
  16.8 0.9 %collective-permute-done.1.neighbour_ref = bf16[128,512]{1,0:T(8,128)(2,1)S(1)} collective-permute-done((bf16[128,512]{1,0:T(8,128)(2,1)S(1)}, bf16[128,512]{1,0:T(8,128)(2,1)S(1)}, u32[]{:S(2)}, u32[]{:S(2)}) %collective-permute-start.1) | collective-permute-done | bytes 131104 | tf_op jit(solution)/shard_map/ppermute | solution.py:684
  17.7 0.0 copy-start.13
  17.7 4.6 %late.1 = bf16[4,4096]{1,0:T(4,128)(2,1)S(1)} custom-call(f32[2,4,2,128,512]{4,3,2,1,0:T(8,128)S(1)} %copy-done, bf16[128,512]{1,0:T(8,128)(2,1)S(1)} %collective-permute-done.partner_ref, bf16[128,512]{1,0:T(8,128)(2,1)S(1)} %collective-permute-done.1.neighbour_ref, f32[128,512]{1,0:T(8,128)S(1)} %get-tuple-element.22.mix_ref, ...), custom_call_target="tpu_custom_call" | custom-call | tf_op jit(solution)/shard_map/late/pallas_call | solution.py:605
  22.4 0.1 collective-permute-start.2
  22.5 1.2 %collective-permute-done.2 = bf16[4,4096]{1,0:T(4,128)(2,1)S(1)} collective-permute-done((bf16[4,4096]{1,0:T(4,128)(2,1)S(1)}, bf16[4,4096]{1,0:T(4,128)(2,1)S(1)}, u32[]{:S(2)}, u32[]{:S(2)}) %collective-permute-start.2) | collective-permute-done | bytes 32800 | tf_op jit(solution)/shard_map/ppermute | solution.py:659
  23.7 6.4 %collective-permute-start.4 = (bf16[8,4096]{1,0:T(8,128)(2,1)S(1)}, bf16[8,4096]{1,0:T(8,128)(2,1)S(1)}, u32[]{:S(2)}, u32[]{:S(2)}) collective-permute-start(bf16[8,4096]{1,0:T(8,128)(2,1)S(1)} %pad_maximum_fusion.1), channel_id=1, source_target_pairs={{0,12},{2,14},{4,16},{6,18},{8,20},{10,22},{12,24},{14,26},{16,28}... | collective-permute-start | bytes 196616 | tf_op jit(solution)/shard_map/ppermute | solution.py:666
  30.1 2.2 %collective-permute-start.3 = (bf16[8,4096]{1,0:T(8,128)(2,1)S(1)}, bf16[8,4096]{1,0:T(8,128)(2,1)S(1)}, u32[]{:S(2)}, u32[]{:S(2)}) collective-permute-start(bf16[8,4096]{1,0:T(8,128)(2,1)S(1)} %pad_maximum_fusion.1), channel_id=1, source_target_pairs={{0,6},{2,8},{4,10},{6,12},{8,14},{10,16},{12,18},{14,20},{16,22},{... | collective-permute-start | bytes 196616 | tf_op jit(solution)/shard_map/ppermute | solution.py:666
  32.4 3.9 %collective-permute-done.4 = bf16[8,4096]{1,0:T(8,128)(2,1)S(1)} collective-permute-done((bf16[8,4096]{1,0:T(8,128)(2,1)S(1)}, bf16[8,4096]{1,0:T(8,128)(2,1)S(1)}, u32[]{:S(2)}, u32[]{:S(2)}) %collective-permute-start.4) | collective-permute-done | bytes 65568 | tf_op jit(solution)/shard_map/ppermute | solution.py:666
  36.3 0.8 %collective-permute-done.3 = bf16[8,4096]{1,0:T(8,128)(2,1)S(1)} collective-permute-done((bf16[8,4096]{1,0:T(8,128)(2,1)S(1)}, bf16[8,4096]{1,0:T(8,128)(2,1)S(1)}, u32[]{:S(2)}, u32[]{:S(2)}) %collective-permute-start.3) | collective-permute-done | bytes 65568 | tf_op jit(solution)/shard_map/ppermute | solution.py:666
  37.1 0.1 pad_maximum_fusion.refs_1_
  37.2 4.7 %collective-permute-start.6 = (bf16[24,4096]{1,0:T(8,128)(2,1)S(1)}, bf16[24,4096]{1,0:T(8,128)(2,1)S(1)}, u32[]{:S(2)}, u32[]{:S(2)}) collective-permute-start(bf16[24,4096]{1,0:T(8,128)(2,1)S(1)} %pad_maximum_fusion.refs_1_), channel_id=1, source_target_pairs={{0,4},{2,6},{4,8},{6,10},{8,12},{10,14},{12,16},{14,18},{16,20},{1... | collective-permute-start | bytes 589832 | tf_op jit(solution)/shard_map/ppermute | solution.py:666
  41.8 0.0 collective-permute-start.5
  41.8 4.2 %collective-permute-done.6.refs_3_ = bf16[24,4096]{1,0:T(8,128)(2,1)S(1)} collective-permute-done((bf16[24,4096]{1,0:T(8,128)(2,1)S(1)}, bf16[24,4096]{1,0:T(8,128)(2,1)S(1)}, u32[]{:S(2)}, u32[]{:S(2)}) %collective-permute-start.6) | collective-permute-done | bytes 196640 | tf_op jit(solution)/shard_map/ppermute | solution.py:666
  46.0 2.1 %collective-permute-done.5.refs_2_ = bf16[24,4096]{1,0:T(8,128)(2,1)S(1)} collective-permute-done((bf16[24,4096]{1,0:T(8,128)(2,1)S(1)}, bf16[24,4096]{1,0:T(8,128)(2,1)S(1)}, u32[]{:S(2)}, u32[]{:S(2)}) %collective-permute-start.5) | collective-permute-done | bytes 196640 | tf_op jit(solution)/shard_map/ppermute | solution.py:666
  48.1 0.8 %pick.1 = (f32[32,4096]{1,0:T(8,128)S(1)}, bf16[32,4096]{1,0:T(8,128)(2,1)S(1)}) custom-call(s32[8,128]{1,0:T(8,128)S(1)} %bitcast.2, bf16[24,4096]{1,0:T(8,128)(2,1)S(1)} %pad_maximum_fusion.refs_1_, bf16[24,4096]{1,0:T(8,128)(2,1)S(1)} %collective-permute-done.5.refs_2_, bf16[24,4096]{1,0:T(8,128)(2,1)S(1)} %collective-permute-done.6.refs_3_), custom_call_target="tpu_custom_call" | custom-call | tf_op jit(solution)/shard_map/pick/pallas_call | solution.py:648
  48.9 0.3 collective-permute-start.7
  49.1 1.4 %collective-permute-done.7 = bf16[32,4096]{1,0:T(8,128)(2,1)S(1)} collective-permute-done((bf16[32,4096]{1,0:T(8,128)(2,1)S(1)}, bf16[32,4096]{1,0:T(8,128)(2,1)S(1)}, u32[]{:S(2)}, u32[]{:S(2)}) %collective-permute-start.7) | collective-permute-done | bytes 262176 | tf_op jit(solution)/shard_map/ppermute | solution.py:659
  50.5 0.8 %convert_add_fusion = f32[32,4096]{1,0:T(8,128)} fusion(f32[32,4096]{1,0:T(8,128)S(1)} %get-tuple-element.33, bf16[32,4096]{1,0:T(8,128)(2,1)S(1)} %collective-permute-done.7), kind=kLoop, calls=%fused_computation | loop fusion | flops 262144 | bytes 1310720 | tf_op jit(solution)/shard_map/add | solution.py:689
  (23 shorter events, 0.1 us)
Async XLA Ops:
  0.0 13.4 %copy-start.5 = (bf16[256,256]{1,0:T(8,128)(2,1)S(1)}, bf16[256,256]{1,0:T(8,128)(2,1)}, u32[]{:S(2)}) copy-start(bf16[256,256]{1,0:T(8,128)(2,1)} %constant.20.clone.x_across_ref) | copy-start | bytes 393220
  0.0 13.4 %copy-start.6 = (bf16[256,256]{1,0:T(8,128)(2,1)S(1)}, bf16[256,256]{1,0:T(8,128)(2,1)}, u32[]{:S(2)}) copy-start(bf16[256,256]{1,0:T(8,128)(2,1)} %constant.19.clone.x_ref) | copy-start | bytes 393220
  0.0 13.4 %copy-start.7 = (bf16[256,256]{1,0:T(8,128)(2,1)S(1)}, bf16[256,256]{1,0:T(8,128)(2,1)}, u32[]{:S(2)}) copy-start(bf16[256,256]{1,0:T(8,128)(2,1)} %constant.18.clone.xx_across_ref) | copy-start | bytes 393220
  0.0 13.4 %copy-start.8 = (bf16[256,256]{1,0:T(8,128)(2,1)S(1)}, bf16[256,256]{1,0:T(8,128)(2,1)}, u32[]{:S(2)}) copy-start(bf16[256,256]{1,0:T(8,128)(2,1)} %constant.17.clone.xx_ref) | copy-start | bytes 393220
  0.0 13.4 %copy-start.11 = (bf16[256,128]{1,0:T(8,128)(2,1)S(1)}, bf16[256,128]{1,0:T(8,128)(2,1)}, u32[]{:S(2)}) copy-start(bf16[256,128]{1,0:T(8,128)(2,1)} %constant.16.clone.own_ref) | copy-start | bytes 196612
  0.0 13.4 %copy-start = (f32[2,4,2,128,512]{4,3,2,1,0:T(8,128)S(1)}, f32[2,4,2,128,512]{4,3,2,1,0:T(8,128)}, u32[]{:S(2)}) copy-start(f32[2,4,2,128,512]{4,3,2,1,0:T(8,128)} %wave_ref.3) | copy-start | bytes 12582916
  0.0 13.4 %copy-start.4 = (f32[128,512]{1,0:T(8,128)S(1)}, f32[128,512]{1,0:T(8,128)}, u32[]{:S(2)}) copy-start(f32[128,512]{1,0:T(8,128)} %tilt_ref.1) | copy-start | bytes 786436
  0.1 13.4 %copy-start.3 = (f32[128,512]{1,0:T(8,128)S(1)}, f32[128,512]{1,0:T(8,128)}, u32[]{:S(2)}) copy-start(f32[128,512]{1,0:T(8,128)} %delta_ref.1) | copy-start | bytes 786436
  0.1 13.4 %copy-start.2 = (f32[128,512]{1,0:T(8,128)S(1)}, f32[128,512]{1,0:T(8,128)}, u32[]{:S(2)}) copy-start(f32[128,512]{1,0:T(8,128)} %eps_ref.1) | copy-start | bytes 786436
  0.1 13.4 %copy-start.1 = (f32[128,512]{1,0:T(8,128)S(1)}, f32[128,512]{1,0:T(8,128)}, u32[]{:S(2)}) copy-start(f32[128,512]{1,0:T(8,128)} %courant_ref.1) | copy-start | bytes 786436
  0.1 13.4 %copy-start.15 = (s32[64]{0:T(128)S(1)}, s32[64]{0:T(128)}, u32[]{:S(2)}) copy-start(s32[64]{0:T(128)} %param.27) | copy-start | bytes 772
  0.1 13.4 %copy-start.14 = (s32[32]{0:T(128)S(1)}, s32[32]{0:T(128)}, u32[]{:S(2)}) copy-start(s32[32]{0:T(128)} %counts_ref.1) | copy-start | bytes 388
  1.4 16.4 %copy-start.9 = (bf16[256,144]{1,0:T(8,128)(2,1)S(1)}, bf16[256,144]{1,0:T(8,128)(2,1)}, u32[]{:S(2)}) copy-start(bf16[256,144]{1,0:T(8,128)(2,1)} %constant.22.clone.two_ref) | copy-start | bytes 221188
  1.4 16.3 %copy-start.10 = (bf16[128,384]{1,0:T(8,128)(2,1)S(1)}, bf16[128,384]{1,0:T(8,128)(2,1)}, u32[]{:S(2)}) copy-start(bf16[128,384]{1,0:T(8,128)(2,1)} %constant.23.clone.depth_ref) | copy-start | bytes 294916
  1.4 16.3 %copy-start.12 = (bf16[64,48]{1,0:T(8,128)(2,1)S(1)}, bf16[64,48]{1,0:T(8,128)(2,1)}, u32[]{:S(2)}) copy-start(bf16[64,48]{1,0:T(8,128)(2,1)} %constant.21.clone.edge_table_ref) | copy-start | bytes 18436
  1.4 15.4 %collective-permute-start = (bf16[128,512]{1,0:T(8,128)(2,1)S(1)}, bf16[128,512]{1,0:T(8,128)(2,1)S(1)}, u32[]{:S(2)}, u32[]{:S(2)}) collective-permute-start(bf16[128,512]{1,0:T(8,128)(2,1)S(1)} %get-tuple-element.20), channel_id=1, source_target_pairs={{0,1},{1,0},{2,3},{3,2},{4,5},{5,4},{6,7},{7,6},{8,9},{9,8},{10,11... | collective-permute-start | bytes 393224 | tf_op jit(solution)/shard_map/ppermute | solution.py:659
  11.4 6.3 %collective-permute-start.1 = (bf16[128,512]{1,0:T(8,128)(2,1)S(1)}, bf16[128,512]{1,0:T(8,128)(2,1)S(1)}, u32[]{:S(2)}, u32[]{:S(2)}) collective-permute-start(bf16[128,512]{1,0:T(8,128)(2,1)S(1)} %get-tuple-element.21), channel_id=1, source_target_pairs={{1,2},{3,4},{5,6},{7,8},{9,10},{11,12},{13,14},{15,16},{17,18},{19... | collective-permute-start | bytes 393224 | tf_op jit(solution)/shard_map/ppermute | solution.py:684
  17.7 30.4 %copy-start.13 = (s32[1024]{0:T(1024)S(1)}, s32[1024]{0:T(1024)}, u32[]{:S(2)}) copy-start(s32[1024]{0:T(1024)} %param.25) | copy-start | bytes 12292
  22.4 1.3 %collective-permute-start.2 = (bf16[4,4096]{1,0:T(4,128)(2,1)S(1)}, bf16[4,4096]{1,0:T(4,128)(2,1)S(1)}, u32[]{:S(2)}, u32[]{:S(2)}) collective-permute-start(bf16[4,4096]{1,0:T(4,128)(2,1)S(1)} %late.1), channel_id=1, source_target_pairs={{0,1},{1,0},{2,3},{3,2},{4,5},{5,4},{6,7},{7,6},{8,9},{9,8},{10,11... | collective-permute-start | bytes 98312 | tf_op jit(solution)/shard_map/ppermute | solution.py:659
  23.7 12.5 %collective-permute-start.4 = (bf16[8,4096]{1,0:T(8,128)(2,1)S(1)}, bf16[8,4096]{1,0:T(8,128)(2,1)S(1)}, u32[]{:S(2)}, u32[]{:S(2)}) collective-permute-start(bf16[8,4096]{1,0:T(8,128)(2,1)S(1)} %pad_maximum_fusion.1), channel_id=1, source_target_pairs={{0,12},{2,14},{4,16},{6,18},{8,20},{10,22},{12,24},{14,26},{16,28}... | collective-permute-start | bytes 196616 | tf_op jit(solution)/shard_map/ppermute | solution.py:666
  30.1 7.0 %collective-permute-start.3 = (bf16[8,4096]{1,0:T(8,128)(2,1)S(1)}, bf16[8,4096]{1,0:T(8,128)(2,1)S(1)}, u32[]{:S(2)}, u32[]{:S(2)}) collective-permute-start(bf16[8,4096]{1,0:T(8,128)(2,1)S(1)} %pad_maximum_fusion.1), channel_id=1, source_target_pairs={{0,6},{2,8},{4,10},{6,12},{8,14},{10,16},{12,18},{14,20},{16,22},{... | collective-permute-start | bytes 196616 | tf_op jit(solution)/shard_map/ppermute | solution.py:666
  37.2 8.8 %collective-permute-start.6 = (bf16[24,4096]{1,0:T(8,128)(2,1)S(1)}, bf16[24,4096]{1,0:T(8,128)(2,1)S(1)}, u32[]{:S(2)}, u32[]{:S(2)}) collective-permute-start(bf16[24,4096]{1,0:T(8,128)(2,1)S(1)} %pad_maximum_fusion.refs_1_), channel_id=1, source_target_pairs={{0,4},{2,6},{4,8},{6,10},{8,12},{10,14},{12,16},{14,18},{16,20},{1... | collective-permute-start | bytes 589832 | tf_op jit(solution)/shard_map/ppermute | solution.py:666
  41.8 6.3 %collective-permute-start.5 = (bf16[24,4096]{1,0:T(8,128)(2,1)S(1)}, bf16[24,4096]{1,0:T(8,128)(2,1)S(1)}, u32[]{:S(2)}, u32[]{:S(2)}) collective-permute-start(bf16[24,4096]{1,0:T(8,128)(2,1)S(1)} %pad_maximum_fusion.refs_1_), channel_id=1, source_target_pairs={{0,2},{2,4},{4,6},{6,8},{8,10},{10,12},{12,14},{14,16},{16,18},{18... | collective-permute-start | bytes 589832 | tf_op jit(solution)/shard_map/ppermute | solution.py:666
  48.9 1.7 %collective-permute-start.7 = (bf16[32,4096]{1,0:T(8,128)(2,1)S(1)}, bf16[32,4096]{1,0:T(8,128)(2,1)S(1)}, u32[]{:S(2)}, u32[]{:S(2)}) collective-permute-start(bf16[32,4096]{1,0:T(8,128)(2,1)S(1)} %get-tuple-element.34), channel_id=1, source_target_pairs={{0,1},{1,0},{2,3},{3,2},{4,5},{5,4},{6,7},{7,6},{8,9},{9,8},{10,11... | collective-permute-start | bytes 786440 | tf_op jit(solution)/shard_map/ppermute | solution.py:659
